TPU v7x, 32 devices: a whole 2x2x4 slice. The times are simulated.
32 devices in a mesh: dp: 16 (over z, x, core), mp: 2 (over y).
Axes of the slice: x: 2, y: 2, z: 4, core: 2. Of those that a mesh axis runs over, the one named last changes fastest.
Arguments:
- inputs_store: bfloat16 [512, 128], replicated, may hold values from -6 to 6
- window: int32 [16], replicated, may hold values from 0 to 511
- targets_store: bfloat16 [512, 4096], P(None, ('dp', 'mp')), may hold values from -6 to 6
- jac_store: bfloat16 [512, 4096, 128], P(None, ('dp', 'mp')), may hold values from -4 to 4
- first_weight: bfloat16 [128, 1024], replicated, may hold values from -0.5 to 0.5
- first_bias: bfloat16 [1024], replicated, may hold values from -3 to 3
- hidden_weight: bfloat16 [1024, 1024], P(None, 'mp'), may hold values from -0.1875 to 0.1875
- hidden_bias: bfloat16 [1024], P('mp'), may hold values from -3 to 3
- decoder_weight: bfloat16 [4096, 1024], P(('dp', 'mp')), may hold values from -0.1875 to 0.1875
Outputs:
- first_weights: float32 [128, 1024], replicated
- first_biases: float32 [1024], replicated
- hidden_weights: float32 [1024, 1024], P(None, 'mp')
- hidden_biases: float32 [1024], P('mp')
- decoder_grad: float32 [4096, 1024], P(('dp', 'mp'))
Inputs may be any that keep to these rules, and one draw needn't show every extreme that they name: `window`: indices of stored samples; an index may repeat.
All inputs are finite; a program needn't handle non-finite values.
Results may differ from a plain program's by a relative error of at most 0.011.
Values may be sent and summed in bfloat16 or wider, within the bound.
No kernel may reach another device: no remote copies, remote signals or barrier semaphores. Data moves between devices by JAX's collectives and lax.ppermute only.
A program may use at most 64 MiB of HBM per device.

v0:
```python
import jax
import jax.numpy as jnp
from jax import lax
from jax.experimental import pallas as pl
from jax.experimental.pallas import tpu as pltpu
from jax.sharding import Mesh, PartitionSpec as P

F32 = jnp.float32
BF16 = jnp.bfloat16


def dot(a, b, contract):
    return lax.dot_general(a, b, (contract, ((), ())), preferred_element_type=F32)


def swap(value, axes, size, step):
    return lax.ppermute(value, axes, [(j, j ^ step) for j in range(size)])


def tree_sum(parts):
    while len(parts) > 1:
        parts = [parts[i] + parts[i + 1] for i in range(0, len(parts), 2)]
    return parts[0]


def place(pieces, me, axis):
    width = pieces[0].shape[axis]
    shape = list(pieces[0].shape)
    shape[axis] *= len(pieces)
    whole = jnp.zeros(shape, pieces[0].dtype)
    for step, piece in enumerate(pieces):
        whole = lax.dynamic_update_slice_in_dim(whole, piece, (me ^ step) * width, axis)
    return whole


def part(value, index, count, axis):
    width = value.shape[axis] // count
    return lax.dynamic_slice_in_dim(value, index * width, width, axis)


VMEM = pl.BlockSpec(memory_space=pltpu.VMEM)
SMEM = pl.BlockSpec(memory_space=pltpu.SMEM)
ANY = pl.BlockSpec(memory_space=pltpu.HBM)


COST_UNIT = 1 << 30


def aligned(index, size):
    return pl.ds(pl.multiple_of(index * size, size), size)


def local_call(body, outs, args, specs=None, scratch=(), limit=24 << 20, cost=1.0):
    return pallas_call(body, outs, args, specs, scratch, limit, cost)


def pallas_call(body, outs, args, specs, scratch, limit, cost):
    return pl.pallas_call(
        body,
        out_shape=[jax.ShapeDtypeStruct(shape, kind) for shape, kind in outs],
        in_specs=[VMEM] * len(args) if specs is None else specs,
        out_specs=[VMEM] * len(outs),
        scratch_shapes=list(scratch),
        compiler_params=pltpu.CompilerParams(vmem_limit_bytes=limit),
        cost_estimate=pl.CostEstimate(
            flops=int(cost * COST_UNIT), bytes_accessed=1 << 20, transcendentals=0
        ),
    )(*args)


def make_fast_step(nz, nx, nc, ny):
    nxy = nx * ny

    def on_device(
        inputs_store,
        window,
        targets_store,
        jac_store,
        first_weight,
        first_bias,
        hidden_weight,
        hidden_bias,
        decoder_weight,
    ):
        rank, hidden = first_weight.shape
        kw = hidden_weight.shape[1]
        outs, depth = decoder_weight.shape[0], inputs_store.shape[0]
        count = window.shape[0] // nc
        total = (count + 1) * rank
        hrow_c, frow_c = hidden // nc, rank // nc
        hrow_x = hrow_c // nx
        hrow_z, frow_z = hrow_x // nz, frow_c // nz
        brow = 16

        def swaps(values, axes, size):
            moved = [values[0]]
            for step in range(1, size):
                moved.append(swap(values[step], axes, size, step))
            return moved

        sent = part(hidden_weight, lax.axis_index("c"), nc, 0)
        got = swap(sent, "y", ny, 1)
        bias_got = swap(hidden_bias, "y", ny, 1)
        decoder_got = swap(decoder_weight, "c", nc, 1)

        def gather(
            window_ref, jac_ref, target_ref, input_ref, weight_ref, bias_ref,
            own_ref, away_ref, act_ref, turned_ref, sems,
        ):
            me = lax.axis_index("c")
            copies = []
            for u, ref in enumerate((away_ref, own_ref)):
                for i in range(count):
                    row = window_ref[(me ^ u ^ 1) * count + i]
                    copies.append(pltpu.make_async_copy(jac_ref.at[row], ref.at[i], sems.at[u, i]))
            for copy in copies:
                copy.start()
            line = lax.broadcasted_iota(jnp.int32, (rank, depth), 0)
            place_of = lax.broadcasted_iota(jnp.int32, (rank, depth), 1)

            def pick(member, table):
                index = jnp.full((rank, depth), -1, jnp.int32)
                for i in range(count):
                    index = jnp.where(line == i, window_ref[member * count + i], index)
                chosen = jnp.where(index == place_of, 1.0, 0.0).astype(BF16)
                return jnp.dot(chosen, table, preferred_element_type=F32)

            inputs = pick(me, input_ref[...])
            turned_ref[...] = inputs.T
            first_pre = jnp.dot(
                inputs.astype(BF16), weight_ref[...], preferred_element_type=F32
            )[:count]
            act_ref[...] = jnp.tanh(first_pre + bias_ref[...].astype(F32).reshape(1, hidden))
            own_ref[count] = pick(me, target_ref[...]).T.astype(BF16)
            away_ref[count] = pick(me ^ 1, target_ref[...]).T.astype(BF16)
            for copy in copies:
                copy.wait()

        jac_shape = ((count + 1,) + jac_store.shape[1:], BF16)
        jac_own, jac_away, first_act, turned = local_call(
            gather,
            [jac_shape, jac_shape, ((count, hidden), F32), ((rank, rank), F32)],
            (window, jac_store, targets_store, inputs_store, first_weight, first_bias),
            cost=4,
            specs=[SMEM, ANY, VMEM, VMEM, VMEM, VMEM],
            scratch=[pltpu.SemaphoreType.DMA((nc, count))],
            limit=60 << 20,
        )
        jac_got = swap(jac_away, "c", nc, 1)

        def warm(act_ref, weight_ref, half_ref, tan_ref, side_ref, lin_ref):
            act = act_ref[...]
            slope = 1.0 - act * act
            weight = weight_ref[...].astype(F32)
            pad = jnp.zeros((rank - count, hidden), F32)
            for s in range(count):
                rows = slice(s * rank, (s + 1) * rank)
                tan_ref[rows] = (slope[s : s + 1] * weight).astype(BF16)
            padded = jnp.concatenate([act, pad])
            tan_ref[count * rank :] = padded.astype(BF16)
            lin_ref[...] = jnp.dot(tan_ref[...], half_ref[...], preferred_element_type=F32)
            slope_side = jnp.concatenate([slope, pad]).T
            weight_side = weight.T
            for s in range(count):
                columns = slice(s * rank, (s + 1) * rank)
                side_ref[:, columns] = (slope_side[:, s : s + 1] * weight_side).astype(BF16)
            side_ref[:, count * rank :] = padded.T.astype(BF16)

        first_tan, first_side, lin_own = local_call(
            warm,
            [((total, hidden), BF16), ((hidden, total), BF16), ((total, kw), F32)],
            (first_act, first_weight, hidden_weight),
            cost=2,
            limit=30 << 20,
        )
        got, bias_got, decoder_got, jac_got, first_tan = lax.optimization_barrier(
            (got, bias_got, decoder_got, jac_got, first_tan)
        )
        got_core = swap(got, "c", nc, 1)

        def main(
            tan1_ref, side_ref, lin_ref, got_ref, core_ref, bias_ref, bias_got_ref,
            dec_ref, dec_got_ref, jac_ref, jac_got_ref,
            half_ref, tan_ref, miss_ref, round_ref, sum_ref, out_ref,
            lin_got_ref, wide_ref, net_ref, back_ref,
        ):
            me, my = lax.axis_index("c"), lax.axis_index("y")
            half_ref[aligned(me, hrow_c)] = got_ref[...]
            half_ref[aligned(me ^ 1, hrow_c)] = core_ref[...]
            for b in range(ny):
                columns = slice(b * kw, (b + 1) * kw)
                wide_ref[:outs, columns] = dec_ref[:, aligned(my ^ b, kw)]
                wide_ref[outs:, columns] = dec_got_ref[:, aligned(my ^ b, kw)]
            lin_got_ref[...] = jnp.dot(tan1_ref[...], half_ref[...], preferred_element_type=F32)
            pad = jnp.zeros((rank - count, kw), F32)
            last = slice(count * rank, total)
            lins, acts, slopes = (lin_ref, lin_got_ref), [], []
            for b, (lin, bias) in enumerate(zip(lins, (bias_ref, bias_got_ref))):
                columns = slice(b * kw, (b + 1) * kw)
                pre = lin[count * rank : count * rank + count]
                act = jnp.tanh(pre + bias[...].astype(F32).reshape(1, kw))
                slope = 1.0 - act * act
                acts.append(act)
                slopes.append(slope)
                tan_ref[last, columns] = jnp.concatenate([act, pad]).astype(BF16)
                for s in range(count):
                    rows = slice(s * rank, (s + 1) * rank)
                    tan_ref[rows, columns] = (slope[s : s + 1] * lin[rows]).astype(BF16)
            net_ref[...] = dot(wide_ref[...], tan_ref[...], ((1,), (1,)))
            for s in range(count + 1):
                columns = slice(s * rank, (s + 1) * rank)
                for part_rows, jac in ((slice(0, outs), jac_ref), (slice(outs, None), jac_got_ref)):
                    miss = net_ref[part_rows, columns] - jac[s].astype(F32)
                    miss_ref[part_rows, columns] = miss.astype(BF16)
            back_ref[...] = dot(miss_ref[...], wide_ref[...], ((0,), (0,)))
            for b, lin in enumerate(lins):
                columns = slice(b * kw, (b + 1) * kw)
                act, slope = acts[b], slopes[b]
                sums = []
                for s in range(count):
                    rows = slice(s * rank, (s + 1) * rank)
                    back = back_ref[rows, columns]
                    sums.append(jnp.sum(back * lin[rows], axis=0, keepdims=True))
                    round_ref[rows, columns] = (back * slope[s : s + 1]).astype(BF16)
                act_back = back_ref[count * rank : count * rank + count, columns]
                sums = jnp.concatenate(sums)
                pre_back = act_back * slope - 2.0 * act * slope * sums
                round_ref[last, columns] = jnp.concatenate([pre_back, pad]).astype(BF16)
                sum_ref[:, columns] = jnp.sum(pre_back, axis=0, keepdims=True)
            out_ref[...] = jnp.dot(
                side_ref[aligned(me ^ 1, hrow_c)], round_ref[...], preferred_element_type=F32
            ).astype(BF16)

        half_got, hidden_tan, miss, lin_round, hidden_sum, g_away = local_call(
            main,
            [
                ((hidden, kw), BF16),
                ((total, hidden), BF16),
                ((nc * outs, total), BF16),
                ((total, hidden), BF16),
                ((1, hidden), F32),
                ((hrow_c, hidden), BF16),
            ],
            (
                first_tan, first_side, lin_own, got, got_core, hidden_bias, bias_got,
                decoder_weight, decoder_got, jac_own, jac_got,
            ),
            cost=6.5,
            scratch=[
                pltpu.VMEM((total, kw), F32),
                pltpu.VMEM((nc * outs, hidden), BF16),
                pltpu.VMEM((nc * outs, total), F32),
                pltpu.VMEM((total, hidden), F32),
            ],
            limit=40 << 20,
        )
        g_got = swap(g_away, "c", nc, 1)

        def own_rows(side_ref, round_ref, out_ref):
            me = lax.axis_index("c")
            out_ref[...] = jnp.dot(
                side_ref[aligned(me, hrow_c)], round_ref[...], preferred_element_type=F32
            )

        (g_own,) = local_call(
            own_rows, [((hrow_c, hidden), F32)], (first_side, lin_round), cost=1.5, limit=16 << 20
        )

        def merge_core(g_ref, got_ref, *out_refs):
            mx = lax.axis_index("x")
            for s, out_ref in enumerate(out_refs):
                a, b = s // ny, s % ny
                rows, columns = aligned(mx ^ a, hrow_x), slice(b * kw, (b + 1) * kw)
                value = g_ref[rows, columns] + got_ref[rows, columns].astype(F32)
                out_ref[...] = value.astype(BF16)

        plane = local_call(merge_core, [((hrow_x, kw), BF16)] * nxy, (g_own, g_got))
        (lin_round, miss, hidden_tan), _ = lax.optimization_barrier(
            ((lin_round, miss, hidden_tan), plane[0])
        )
        plane = swaps(plane, ("x", "y"), nxy)

        def lower(
            round_ref, half_ref, got_ref, act_ref, weight_ref, turned_ref, sum_ref,
            own_ref, away_ref, bias_ref, low_ref, first_ref,
        ):
            me, my = lax.axis_index("c"), lax.axis_index("y")
            low_ref[...] = dot(round_ref[:, :kw], half_ref[...], ((1,), (1,)))
            low_ref[...] += dot(round_ref[:, kw:], got_ref[...], ((1,), (1,)))
            act = act_ref[...]
            slope = 1.0 - act * act
            weight = weight_ref[...].astype(F32)
            sums = []
            for s in range(count):
                low = low_ref[s * rank : (s + 1) * rank]
                sums.append(jnp.sum(low * weight, axis=0, keepdims=True))
            act_lower = low_ref[count * rank : count * rank + count]
            pre_lower = act_lower * slope - 2.0 * act * slope * jnp.concatenate(sums)
            turned = turned_ref[...]
            value = jnp.zeros((rank, hidden), F32)
            for s in range(count):
                low = low_ref[s * rank : (s + 1) * rank]
                value = value + low * slope[s : s + 1]
                value = value + turned[:, s : s + 1] * pre_lower[s : s + 1]
            first_ref[...] = value
            own_ref[...] = first_ref[aligned(me, frow_c)]
            away = first_ref[aligned(me ^ 1, frow_c)].astype(BF16)
            for b in range(ny):
                away_ref[b * frow_c : (b + 1) * frow_c] = away[:, b * kw : (b + 1) * kw]
            sums = sum_ref[...]
            halves = [sums[:, :kw], sums[:, kw:]]
            first_sum = jnp.sum(pre_lower, axis=0, keepdims=True)
            bias = jnp.concatenate(
                [
                    jnp.where(my == 0, halves[0], halves[1]),
                    jnp.where(my == 0, halves[1], halves[0]),
                    first_sum[:, :kw],
                    first_sum[:, kw:],
                    jnp.zeros((brow - 2 * ny, kw), F32),
                ]
            ).astype(BF16)
            away_ref[ny * frow_c :] = bias
            bias_ref[...] = bias

        f_own, f_away, b_own = local_call(
            lower,
            [
                ((frow_c, hidden), F32),
                ((ny * frow_c + brow, kw), BF16),
                ((brow, kw), BF16),
            ],
            (lin_round, hidden_weight, half_got, first_act, first_weight, turned, hidden_sum),
            cost=3,
            scratch=[pltpu.VMEM((total, hidden), F32), pltpu.VMEM((rank, hidden), F32)],
            limit=30 << 20,
        )
        _, f_got = swaps([f_away] * nc, "c", nc)

        def merge_first(f_ref, got_ref, b_ref, *out_refs):
            mz = lax.axis_index("z")
            bias = (b_ref[...].astype(F32) + got_ref[ny * frow_c :].astype(F32)).astype(BF16)
            for s, out_ref in enumerate(out_refs):
                rows = aligned(mz ^ s, frow_z)
                for b in range(ny):
                    there = pl.ds(pl.multiple_of(b * frow_c + (mz ^ s) * frow_z, frow_z), frow_z)
                    value = f_ref[rows, b * kw : (b + 1) * kw] + got_ref[there].astype(F32)
                    out_ref[b * frow_z : (b + 1) * frow_z] = value.astype(BF16)
                out_ref[ny * frow_z :] = bias

        side = local_call(
            merge_first, [((ny * frow_z + brow, kw), BF16)] * nz, (f_own, f_got, b_own)
        )
        side = swaps(side, "z", nz)

        def readout(miss_ref, tan_ref, own_ref, away_ref):
            own_ref[...] = jnp.dot(miss_ref[:outs], tan_ref[...], preferred_element_type=F32)
            away_ref[...] = jnp.dot(miss_ref[outs:], tan_ref[...], preferred_element_type=F32)

        d_own, d_away = local_call(
            readout, [((outs, hidden), F32)] * 2, (miss, hidden_tan), cost=1, limit=16 << 20
        )
        *plane, d_away = lax.optimization_barrier((*plane, d_away))
        d_got = swap(d_away, "c", nc, 1)

        def join(own_ref, got_ref, out_ref):
            my = lax.axis_index("y")
            for b in range(ny):
                columns = slice(b * kw, (b + 1) * kw)
                out_ref[:, aligned(my ^ b, kw)] = own_ref[:, columns] + got_ref[:, columns]

        (decoder_grad,) = local_call(
            join, [((outs, hidden), F32)], (d_own, d_got), cost=1, limit=8 << 20
        )

        def merge_plane(*refs):
            in_refs, out_refs, total_ref = refs[:nxy], refs[nxy:-1], refs[-1]
            mz = lax.axis_index("z")
            total_ref[...] = tree_sum([ref[...].astype(F32) for ref in in_refs])
            for s, out_ref in enumerate(out_refs):
                out_ref[...] = total_ref[aligned(mz ^ s, hrow_z)].astype(BF16)

        line = local_call(
            merge_plane,
            [((hrow_z, kw), BF16)] * nz,
            tuple(plane),
            scratch=[pltpu.VMEM((hrow_x, kw), F32)],
        )
        line = swaps(line, "z", nz)

        def add_rounded(*refs):
            total_sum = tree_sum([ref[...].astype(F32) for ref in refs[:-1]])
            refs[-1][...] = total_sum.astype(BF16)

        (side_sum,) = local_call(add_rounded, [((ny * frow_z + brow, kw), BF16)], tuple(side))
        side = swaps([side_sum] * nxy, ("x", "y"), nxy)
        *line, decoder_grad = lax.optimization_barrier((*line, decoder_grad))
        (piece,) = local_call(add_rounded, [((hrow_z, kw), BF16)], tuple(line))
        pieces = swaps([piece] * nz, "z", nz)

        def finish_side(*refs):
            in_refs, (out_ref, hidden_ref, first_ref) = refs[:nxy], refs[nxy:]
            my = lax.axis_index("y")
            total_sum = tree_sum([ref[...].astype(F32) for ref in in_refs])
            out_ref[...] = total_sum[: ny * frow_z].astype(BF16)
            bias = total_sum[ny * frow_z :]
            hidden_ref[...] = jnp.where(my == 0, bias[0:1], bias[1:2]).reshape(kw)
            for b in range(ny):
                row = bias[ny + b : ny + b + 1]
                first_ref[b * kw : (b + 1) * kw] = row.reshape(kw)

        side_piece, hidden_bias_out, first_bias_out = local_call(
            finish_side, [((ny * frow_z, kw), BF16), ((kw,), F32), ((hidden,), F32)], tuple(side)
        )
        side_pieces = swaps([side_piece] * nz, "z", nz)

        def stack(*refs):
            mz = lax.axis_index("z")
            for s, ref in enumerate(refs[:nz]):
                refs[nz][mz ^ s] = ref[...]

        (both,) = local_call(stack, [((nz, hrow_z, kw), BF16)], tuple(pieces))
        (first,) = local_call(stack, [((nz, ny * frow_z, kw), BF16)], tuple(side_pieces))
        _, across = swaps([both] * nx, "x", nx)
        _, both_core = swaps([both] * nc, "c", nc)
        _, first_core = swaps([first] * nc, "c", nc)
        across, both_core, first_core = lax.optimization_barrier((across, both_core, first_core))
        across_core = swap(across, "c", nc, 1)

        def spread_out(*refs):
            in_refs, side_refs = refs[: nc * nx], refs[nc * nx : nc * nx + nc]
            hidden_ref, first_ref = refs[-2:]
            mx, mc = lax.axis_index("x"), lax.axis_index("c")
            for s, ref in enumerate(in_refs):
                base = (mc ^ (s // nx)) * nx + (mx ^ (s % nx))
                for i in range(nz):
                    hidden_ref[aligned(base * nz + i, hrow_z)] = ref[i].astype(F32)
            for u, ref in enumerate(side_refs):
                for i in range(nz):
                    rows = aligned((mc ^ u) * nz + i, frow_z)
                    value = ref[i].astype(F32)
                    for b in range(ny):
                        first_ref[rows, b * kw : (b + 1) * kw] = value[b * frow_z : (b + 1) * frow_z]

        hidden_out, first_out = local_call(
            spread_out,
            [((hidden, kw), F32), ((rank, hidden), F32)],
            (both, across, both_core, across_core, first, first_core),
            cost=2,
        )
        return (first_out, first_bias_out, hidden_out, hidden_bias_out, decoder_grad)

    return on_device


def make_step(nz, nx, nc, ny):
    nxy = nx * ny

    def on_device(
        inputs_store,
        window,
        targets_store,
        jac_store,
        first_weight,
        first_bias,
        hidden_weight,
        hidden_bias,
        decoder_weight,
    ):
        z, x, c, y = (lax.axis_index(name) for name in ("z", "x", "c", "y"))
        rank, hidden = first_weight.shape
        kw = hidden_weight.shape[1]
        pieces = [hidden_weight]
        biases = [hidden_bias]
        mine = part(hidden_weight, c, nc, 0)
        for t in range(1, ny):
            got = swap(mine, "y", ny, t)
            rest = [got] + [swap(got, "c", nc, u) for u in range(1, nc)]
            pieces.append(place(rest, c, 0))
            biases.append(swap(hidden_bias, "y", ny, t))
        wide_hidden = jnp.concatenate(pieces, axis=1)
        wide_bias = jnp.concatenate(biases)
        jac_parts, target_parts, decoder_parts = [], [], []
        for u in range(nc):
            rows = part(window, c ^ u, nc, 0)
            jac, target = jac_store[rows], targets_store[rows]
            decoder = decoder_weight
            if u:
                jac, target, decoder = (swap(v, "c", nc, u) for v in (jac, target, decoder))
            jac_parts.append(jac)
            target_parts.append(target)
            decoder_parts.append(decoder)
        jac = jnp.concatenate(jac_parts, axis=1)
        target = jnp.concatenate(target_parts, axis=1)
        decoder = jnp.concatenate(decoder_parts, axis=0)
        decoder = jnp.concatenate([part(decoder, y ^ t, ny, 1) for t in range(ny)], axis=1)
        inputs = inputs_store[part(window, c, nc, 0)]
        count = inputs.shape[0]
        weight_one = first_weight.astype(F32)
        first_act = jnp.tanh(dot(inputs, first_weight, ((1,), (0,))) + first_bias.astype(F32))
        first_slope = 1.0 - first_act * first_act
        first_tan = (first_slope[:, None, :] * weight_one[None]).astype(BF16)
        first_tan = first_tan.reshape(count * rank, hidden)
        first_round = first_act.astype(BF16)
        hidden_lin = dot(first_tan, wide_hidden, ((1,), (0,))).reshape(count, rank, -1)
        hidden_act = jnp.tanh(
            dot(first_round, wide_hidden, ((1,), (0,))) + wide_bias.astype(F32)
        )
        hidden_slope = 1.0 - hidden_act * hidden_act
        hidden_tan = (hidden_slope[:, None, :] * hidden_lin).astype(BF16)
        hidden_round = hidden_act.astype(BF16)
        output_miss = dot(hidden_round, decoder, ((1,), (1,))) - target.astype(F32)
        output_miss = output_miss.astype(BF16)
        jac_net = dot(decoder, hidden_tan, ((1,), (2,)))
        jac_miss = (jac_net - jac.transpose(1, 0, 2).astype(F32)).astype(BF16)
        jac_miss = jac_miss.reshape(-1, count * rank)
        grad = dot(output_miss, hidden_round, ((0,), (0,))) + dot(
            jac_miss, hidden_tan.reshape(count * rank, -1), ((1,), (0,))
        )
        blocks = jnp.split(grad, nc, axis=0)
        own = [blocks[0]] + [swap(blocks[u], "c", nc, u) for u in range(1, nc)]
        grad = tree_sum(own)
        decoder_grad = place(jnp.split(grad, ny, axis=1), y, 1)

        act_back = dot(output_miss, decoder, ((1,), (0,)))
        tan_back = dot(jac_miss, decoder, ((0,), (0,))).reshape(count, rank, -1)
        pre_back = act_back * hidden_slope - 2.0 * hidden_act * hidden_slope * jnp.sum(
            tan_back * hidden_lin, axis=1
        )
        lin_round = (tan_back * hidden_slope[:, None, :]).astype(BF16)
        lin_round = lin_round.reshape(count * rank, -1)
        pre_round = pre_back.astype(BF16)
        hidden_grad = dot(first_round, pre_round, ((0,), (0,))) + dot(
            first_tan, lin_round, ((0,), (0,))
        )
        tan_lower = dot(lin_round, wide_hidden, ((1,), (1,))).reshape(count, rank, hidden)
        act_lower = dot(pre_round, wide_hidden, ((1,), (1,)))
        pre_lower = act_lower * first_slope - 2.0 * first_act * first_slope * jnp.sum(
            tan_lower * weight_one[None], axis=1
        )
        first_grad = jnp.einsum(
            "sr,sh->rh", inputs.astype(F32), pre_lower, precision=lax.Precision.HIGHEST
        ) + jnp.sum(tan_lower * first_slope[:, None, :], axis=0)
        hidden_bsum = jnp.sum(pre_back, axis=0).reshape(ny, kw)
        hidden_bsum = place([hidden_bsum[t : t + 1] for t in range(ny)], y, 0)
        first_bsum = jnp.sum(pre_lower, axis=0).reshape(ny, kw)
        bias_sum = jnp.concatenate([hidden_bsum, first_bsum])

        def exchange(axes, size, hidden_of, first_of, bias):
            totals = []
            for s in range(size):
                sent = (hidden_of(s), first_of(s), bias)
                sent = [v.astype(BF16) for v in sent]
                if s:
                    sent = [swap(v, axes, size, s) for v in sent]
                totals.append([v.astype(F32) for v in sent])
            return [tree_sum(list(group)) for group in zip(*totals)]

        hidden_grad, first_grad, bias_sum = exchange(
            "c",
            nc,
            lambda s: part(hidden_grad, c ^ s, nc, 0),
            lambda s: part(first_grad, c ^ s, nc, 0),
            bias_sum,
        )
        whole_hidden, whole_first = hidden_grad, first_grad
        hidden_grad, first_grad, bias_sum = exchange(
            ("x", "y"),
            nxy,
            lambda s: part(whole_hidden, x ^ (s // ny), nx, 0)[
                :, (s % ny) * kw : (s % ny + 1) * kw
            ],
            lambda s: part(part(whole_first, x ^ (s // ny), nx, 0), y ^ (s % ny), ny, 1),
            bias_sum,
        )
        half_hidden, half_first = hidden_grad, first_grad
        hidden_grad, first_grad, bias_sum = exchange(
            "z",
            nz,
            lambda s: part(half_hidden, z ^ s, nz, 0),
            lambda s: part(half_first, z ^ s, nz, 0),
            bias_sum,
        )

        def spread(value, axes, size, me, axis):
            return place([value] + [swap(value, axes, size, s) for s in range(1, size)], me, axis)

        hidden_out = hidden_grad.astype(BF16)
        first_out = first_grad.astype(BF16)
        hidden_out = spread(hidden_out, "z", nz, z, 0)
        first_out = spread(first_out, "z", nz, z, 0)
        hidden_out = spread(hidden_out, "x", nx, x, 0)
        first_out = spread(first_out, "x", nx, x, 0)
        first_out = spread(first_out, "y", ny, y, 1)
        hidden_out = spread(hidden_out, "c", nc, c, 0)
        first_out = spread(first_out, "c", nc, c, 0)
        return (
            first_out.astype(F32),
            bias_sum[ny:].reshape(-1),
            hidden_out.astype(F32),
            bias_sum[y],
            decoder_grad,
        )

    return on_device


def solution(mesh):
    dp, mp = mesh.shape["dp"], mesh.shape["mp"]
    nc = 2 if dp % 2 == 0 else 1
    nx = 2 if dp % (2 * nc) == 0 else 1
    nz = dp // (nc * nx)
    fine = Mesh(mesh.devices.reshape(nz, nx, nc, mp), ("z", "x", "c", "y"))
    dps = ("z", "x", "c")
    every = dps + ("y",)
    placed = (
        P(),
        P(),
        P(None, every),
        P(None, every, None),
        P(),
        P(),
        P(None, "y"),
        P("y"),
        P(every, None),
    )
    pieces = nc * nx * nz

    def step(*args):
        window, weight, part_weight = args[1], args[4], args[6]
        rank, hidden = weight.shape
        packed = nc == nx == mp == 2 and window.shape[0] % nc == 0
        packed = packed and rank % (8 * pieces) == 0 and hidden % (16 * pieces) == 0
        packed = packed and part_weight.shape[1] % 128 == 0
        build = make_fast_step if packed else make_step
        return build(nz, nx, nc, mp)(*args)

    return jax.shard_map(
        step,
        mesh=fine,
        in_specs=placed,
        out_specs=(P(), P(), P(None, "y"), P("y"), P(every, None)),
        check_vma=False,
    )
```

profile of v0, /device:TPU:0, one launch (start us, length us, event | category | flops | bytes accessed | tf_op | source)
XLA Modules:
  0.0 91.6 jit_solution(6995254174531501759)
XLA Ops:
  0.6 1.1 %constant_dynamic-slice_fusion = bf16[512,512]{1,0:T(8,128)(2,1)S(1)} fusion(bf16[1024,512]{1,0:T(8,128)(2,1)} %half_ref.3, s32[]{:T(128)S(6)} %select_n.3), kind=kLoop, calls=%fused_computation | loop fusion | bytes 1048580 | tf_op jit(solution)/shard_map/dynamic_slice | solution.py:38
  1.8 3.1 %collective-permute-start = (bf16[512,512]{1,0:T(8,128)(2,1)S(1)}, bf16[512,512]{1,0:T(8,128)(2,1)S(1)}, u32[]{:S(2)}, u32[]{:S(2)}) collective-permute-start(bf16[512,512]{1,0:T(8,128)(2,1)S(1)} %constant_dynamic-slice_fusion), channel_id=1, source_target_pairs={{0,1},{1,0},{2,3},{3,2},{4,5},{5,4},{6,7},{7,6},{8,9},{9,8},{10,11... | collective-permute-start | bytes 1572872 | tf_op jit(solution)/shard_map/ppermute | solution.py:17
  4.8 3.3 %shard_map.128 = (bf16[9,128,128]{2,1,0:T(8,128)(2,1)}, bf16[9,128,128]{2,1,0:T(8,128)(2,1)}, f32[8,1024]{1,0:T(8,128)}, f32[128,128]{1,0:T(8,128)}) custom-call(s32[16]{0:T(128)} %window_ref.1, bf16[512,128,128]{2,1,0:T(8,128)(2,1)} %jac_ref.1, bf16[512,128]{1,0:T(8,128)(2,1)} %target_ref.1, bf16[512,128]{1,0:T(8,128)(2,1)} %input_ref.1, ...), custom_call_target="tpu_custom_call" | custom-call | flops 4294967296 | bytes 1048576 | tf_op jit(solution)/shard_map/pallas_call | solution.py:58
  8.2 0.5 collective-permute-start.2
  8.8 0.8 copy-done.5
  9.6 1.8 %shard_map.129 = (bf16[1152,1024]{1,0:T(8,128)(2,1)S(1)}, bf16[1024,1152]{1,0:T(8,128)(2,1)S(1)}, f32[1152,512]{1,0:T(8,128)S(1)}) custom-call(f32[8,1024]{1,0:T(8,128)S(1)} %copy-done.5, bf16[128,1024]{1,0:T(8,128)(2,1)S(1)} %copy-done, bf16[1024,512]{1,0:T(8,128)(2,1)S(1)} %copy-done.1), custom_call_target="tpu_custom_call" | custom-call | flops 2147483648 | bytes 1048576 | tf_op jit(solution)/shard_map/pallas_call | solution.py:58
  11.4 1.4 %copy-done.8 = f32[1152,512]{1,0:T(8,128)} copy-done((f32[1152,512]{1,0:T(8,128)}, f32[1152,512]{1,0:T(8,128)S(1)}, u32[]{:S(2)}) %copy-start.8) | copy-done | bytes 2359320
  12.8 4.0 %collective-permute-done.1.bias_got_ref = bf16[512]{0:T(512)(128)(2,1)S(1)} collective-permute-done((bf16[512]{0:T(512)(128)(2,1)S(1)}, bf16[512]{0:T(512)(128)(2,1)S(1)}, u32[]{:S(2)}, u32[]{:S(2)}) %collective-permute-start.1) | collective-permute-done | bytes 1056 | tf_op jit(solution)/shard_map/ppermute | solution.py:17
  16.9 1.9 %collective-permute-done.4.core_ref = bf16[512,512]{1,0:T(8,128)(2,1)S(1)} collective-permute-done((bf16[512,512]{1,0:T(8,128)(2,1)S(1)}, bf16[512,512]{1,0:T(8,128)(2,1)S(1)}, u32[]{:S(2)}, u32[]{:S(2)}) %collective-permute-start.4) | collective-permute-done | bytes 524320 | tf_op jit(solution)/shard_map/ppermute | solution.py:17
  18.8 6.5 %shard_map.130 = (bf16[1024,512]{1,0:T(8,128)(2,1)S(1)}, bf16[1152,1024]{1,0:T(8,128)(2,1)S(1)}, bf16[256,1152]{1,0:T(8,128)(2,1)S(1)}, bf16[1152,1024]{1,0:T(8,...) custom-call(bf16[1152,1024]{1,0:T(8,128)(2,1)S(1)} %get-tuple-element.65.tan1_ref, ...), custom_call_target="tpu_custom_call" | custom-call | flops 6979321856 | bytes 1048576 | tf_op jit(solution)/shard_map/pallas_call | solution.py:58
  25.3 0.2 collective-permute-start.5
  25.5 1.5 %shard_map.131.g_ref = f32[512,1024]{1,0:T(8,128)S(1)} custom-call(bf16[1024,1152]{1,0:T(8,128)(2,1)S(1)} %get-tuple-element.62.side_ref, bf16[1152,1024]{1,0:T(8,128)(2,1)S(1)} %get-tuple-element.97.round_ref), custom_call_target="tpu_custom_call" | custom-call | flops 1610612736 | bytes 1048576 | tf_op jit(solution)/shard_map/pallas_call | solution.py:58
  27.1 1.0 %collective-permute-done.5.got_ref = bf16[512,1024]{1,0:T(8,128)(2,1)S(1)} collective-permute-done((bf16[512,1024]{1,0:T(8,128)(2,1)S(1)}, bf16[512,1024]{1,0:T(8,128)(2,1)S(1)}, u32[]{:S(2)}, u32[]{:S(2)}) %collective-permute-start.5) | collective-permute-done | bytes 1048608 | tf_op jit(solution)/shard_map/ppermute | solution.py:17
  28.1 0.2 shard_map.132
  28.3 1.8 %collective-permute-start.6 = (bf16[256,512]{1,0:T(8,128)(2,1)S(1)}, bf16[256,512]{1,0:T(8,128)(2,1)S(1)}, u32[]{:S(2)}, u32[]{:S(2)}) collective-permute-start(bf16[256,512]{1,0:T(8,128)(2,1)S(1)} %get-tuple-element.75), channel_id=1, source_target_pairs={{0,1},{1,0},{4,5},{5,4},{2,3},{3,2},{6,7},{7,6},{8,9},{9,8},{12,13... | collective-permute-start | bytes 786440 | tf_op jit(solution)/shard_map/ppermute | solution.py:17
  30.1 1.5 %collective-permute-start.7 = (bf16[256,512]{1,0:T(8,128)(2,1)S(1)}, bf16[256,512]{1,0:T(8,128)(2,1)S(1)}, u32[]{:S(2)}, u32[]{:S(2)}) collective-permute-start(bf16[256,512]{1,0:T(8,128)(2,1)S(1)} %get-tuple-element.76), channel_id=1, source_target_pairs={{0,4},{1,5},{4,0},{5,1},{2,6},{3,7},{6,2},{7,3},{8,12},{9,13},{12,... | collective-permute-start | bytes 786440 | tf_op jit(solution)/shard_map/ppermute | solution.py:17
  31.5 0.3 collective-permute-start.8
  31.8 0.8 shard_map.133
  32.7 4.0 %collective-permute-done.6.refs_1_ = bf16[256,512]{1,0:T(8,128)(2,1)S(1)} collective-permute-done((bf16[256,512]{1,0:T(8,128)(2,1)S(1)}, bf16[256,512]{1,0:T(8,128)(2,1)S(1)}, u32[]{:S(2)}, u32[]{:S(2)}) %collective-permute-start.6) | collective-permute-done | bytes 262176 | tf_op jit(solution)/shard_map/ppermute | solution.py:17
  36.7 2.6 %collective-permute-done.7.refs_2_ = bf16[256,512]{1,0:T(8,128)(2,1)S(1)} collective-permute-done((bf16[256,512]{1,0:T(8,128)(2,1)S(1)}, bf16[256,512]{1,0:T(8,128)(2,1)S(1)}, u32[]{:S(2)}, u32[]{:S(2)}) %collective-permute-start.7) | collective-permute-done | bytes 262176 | tf_op jit(solution)/shard_map/ppermute | solution.py:17
  39.2 4.3 %collective-permute-done.8.refs_3_ = bf16[256,512]{1,0:T(8,128)(2,1)S(1)} collective-permute-done((bf16[256,512]{1,0:T(8,128)(2,1)S(1)}, bf16[256,512]{1,0:T(8,128)(2,1)S(1)}, u32[]{:S(2)}, u32[]{:S(2)}) %collective-permute-start.8) | collective-permute-done | bytes 262176 | tf_op jit(solution)/shard_map/ppermute | solution.py:17
  43.5 3.2 %shard_map.138 = (f32[64,1024]{1,0:T(8,128)S(1)}, bf16[144,512]{1,0:T(8,128)(2,1)S(1)}, bf16[16,512]{1,0:T(8,128)(2,1)S(1)}) custom-call(bf16[1152,1024]{1,0:T(8,128)(2,1)S(1)} %get-tuple-element.97.round_ref, bf16[1024,512]{1,0:T(8,128)(2,1)S(1)} %copy-done.1, bf16[1024,512]{1,0:T(8,128)(2,1)S(1)} %get-tuple-element.98.got_ref, f32[8,1024]{1,0:T(8,128)S(1)} %copy-done.6, ...), custom_call_target="tpu_custom_call" | custom-call | flops 3221225472 | bytes 1048576 | tf_op jit(solution)/shard_map/pallas_call | solution.py:58
  46.7 0.6 collective-permute-start.18
  47.3 1.0 %collective-permute-done.18.got_ref = bf16[144,512]{1,0:T(8,128)(2,1)S(1)} collective-permute-done((bf16[144,512]{1,0:T(8,128)(2,1)S(1)}, bf16[144,512]{1,0:T(8,128)(2,1)S(1)}, u32[]{:S(2)}, u32[]{:S(2)}) %collective-permute-start.18) | collective-permute-done | bytes 147488 | tf_op jit(solution)/shard_map/ppermute | solution.py:17
  48.4 1.8 %collective-permute-start.19 = (bf16[48,512]{1,0:T(8,128)(2,1)S(1)}, bf16[48,512]{1,0:T(8,128)(2,1)S(1)}, u32[]{:S(2)}, u32[]{:S(2)}) collective-permute-start(bf16[48,512]{1,0:T(8,128)(2,1)S(1)} %get-tuple-element.105), channel_id=1, source_target_pairs={{0,8},{8,0},{16,24},{24,16},{1,9},{9,1},{17,25},{25,17},{2,10},{10... | collective-permute-start | bytes 147464 | tf_op jit(solution)/shard_map/ppermute | solution.py:17
  50.2 2.6 %collective-permute-start.20 = (bf16[48,512]{1,0:T(8,128)(2,1)S(1)}, bf16[48,512]{1,0:T(8,128)(2,1)S(1)}, u32[]{:S(2)}, u32[]{:S(2)}) collective-permute-start(bf16[48,512]{1,0:T(8,128)(2,1)S(1)} %get-tuple-element.106), channel_id=1, source_target_pairs={{0,16},{8,24},{16,0},{24,8},{1,17},{9,25},{17,1},{25,9},{2,18},{10... | collective-permute-start | bytes 147464 | tf_op jit(solution)/shard_map/ppermute | solution.py:17
  52.8 3.4 %collective-permute-done.20.refs_2_ = bf16[48,512]{1,0:T(8,128)(2,1)S(1)} collective-permute-done((bf16[48,512]{1,0:T(8,128)(2,1)S(1)}, bf16[48,512]{1,0:T(8,128)(2,1)S(1)}, u32[]{:S(2)}, u32[]{:S(2)}) %collective-permute-start.20) | collective-permute-done | bytes 49184 | tf_op jit(solution)/shard_map/ppermute | solution.py:17
  56.2 2.4 %collective-permute-done.21.refs_3_ = bf16[48,512]{1,0:T(8,128)(2,1)S(1)} collective-permute-done((bf16[48,512]{1,0:T(8,128)(2,1)S(1)}, bf16[48,512]{1,0:T(8,128)(2,1)S(1)}, u32[]{:S(2)}, u32[]{:S(2)}) %collective-permute-start.21) | collective-permute-done | bytes 49184 | tf_op jit(solution)/shard_map/ppermute | solution.py:17
  58.7 2.5 %collective-permute-start.24 = (bf16[48,512]{1,0:T(8,128)(2,1)S(1)}, bf16[48,512]{1,0:T(8,128)(2,1)S(1)}, u32[]{:S(2)}, u32[]{:S(2)}) collective-permute-start(bf16[48,512]{1,0:T(8,128)(2,1)S(1)} %shard_map.140.refs_0_), channel_id=1, source_target_pairs={{0,5},{1,4},{4,1},{5,0},{2,7},{3,6},{6,3},{7,2},{8,13},{9,12},{12,... | collective-permute-start | bytes 147464 | tf_op jit(solution)/shard_map/ppermute | solution.py:17
  61.2 0.5 collective-permute-start.23
  61.7 0.3 shard_map.134
  62.1 1.8 %collective-permute-start.10 = (bf16[64,512]{1,0:T(8,128)(2,1)S(1)}, bf16[64,512]{1,0:T(8,128)(2,1)S(1)}, u32[]{:S(2)}, u32[]{:S(2)}) collective-permute-start(bf16[64,512]{1,0:T(8,128)(2,1)S(1)} %get-tuple-element.89), channel_id=1, source_target_pairs={{0,16},{8,24},{16,0},{24,8},{1,17},{9,25},{17,1},{25,9},{2,18},{10... | collective-permute-start | bytes 196616 | tf_op jit(solution)/shard_map/ppermute | solution.py:17
  63.9 2.6 %collective-permute-start.11 = (bf16[64,512]{1,0:T(8,128)(2,1)S(1)}, bf16[64,512]{1,0:T(8,128)(2,1)S(1)}, u32[]{:S(2)}, u32[]{:S(2)}) collective-permute-start(bf16[64,512]{1,0:T(8,128)(2,1)S(1)} %get-tuple-element.90), channel_id=1, source_target_pairs={{0,24},{8,16},{16,8},{24,0},{1,25},{9,17},{17,9},{25,1},{2,26},{10... | collective-permute-start | bytes 196616 | tf_op jit(solution)/shard_map/ppermute | solution.py:17
  66.4 0.8 shard_map.135
  67.3 0.4 collective-permute-done.9.refs_1_
  67.7 0.5 collective-permute-start.22
  68.2 1.8 %collective-permute-done.11.refs_3_ = bf16[64,512]{1,0:T(8,128)(2,1)S(1)} collective-permute-done((bf16[64,512]{1,0:T(8,128)(2,1)S(1)}, bf16[64,512]{1,0:T(8,128)(2,1)S(1)}, u32[]{:S(2)}, u32[]{:S(2)}) %collective-permute-start.11) | collective-permute-done | bytes 65568 | tf_op jit(solution)/shard_map/ppermute | solution.py:17
  70.1 2.6 %collective-permute-start.15 = (bf16[64,512]{1,0:T(8,128)(2,1)S(1)}, bf16[64,512]{1,0:T(8,128)(2,1)S(1)}, u32[]{:S(2)}, u32[]{:S(2)}) collective-permute-start(bf16[64,512]{1,0:T(8,128)(2,1)S(1)} %shard_map.136.refs_0_), channel_id=1, source_target_pairs={{0,24},{8,16},{16,8},{24,0},{1,25},{9,17},{17,9},{25,1},{2,26},{10... | collective-permute-start | bytes 196616 | tf_op jit(solution)/shard_map/ppermute | solution.py:17
  72.7 1.8 %collective-permute-start.13 = (bf16[64,512]{1,0:T(8,128)(2,1)S(1)}, bf16[64,512]{1,0:T(8,128)(2,1)S(1)}, u32[]{:S(2)}, u32[]{:S(2)}) collective-permute-start(bf16[64,512]{1,0:T(8,128)(2,1)S(1)} %shard_map.136.refs_0_), channel_id=1, source_target_pairs={{0,8},{8,0},{16,24},{24,16},{1,9},{9,1},{17,25},{25,17},{2,10},{10... | collective-permute-start | bytes 196616 | tf_op jit(solution)/shard_map/ppermute | solution.py:17
  74.6 0.6 shard_map.141
  75.2 2.5 %collective-permute-start.27 = (bf16[32,512]{1,0:T(8,128)(2,1)S(1)}, bf16[32,512]{1,0:T(8,128)(2,1)S(1)}, u32[]{:S(2)}, u32[]{:S(2)}) collective-permute-start(bf16[32,512]{1,0:T(8,128)(2,1)S(1)} %get-tuple-element.108.refs_0_), channel_id=1, source_target_pairs={{0,24},{8,16},{16,8},{24,0},{1,25},{9,17},{17,9},{25,1},{2,26},{10... | collective-permute-start | bytes 98312 | tf_op jit(solution)/shard_map/ppermute | solution.py:17
  77.7 1.8 %collective-permute-start.25 = (bf16[32,512]{1,0:T(8,128)(2,1)S(1)}, bf16[32,512]{1,0:T(8,128)(2,1)S(1)}, u32[]{:S(2)}, u32[]{:S(2)}) collective-permute-start(bf16[32,512]{1,0:T(8,128)(2,1)S(1)} %get-tuple-element.108.refs_0_), channel_id=1, source_target_pairs={{0,8},{8,0},{16,24},{24,16},{1,9},{9,1},{17,25},{25,17},{2,10},{10... | collective-permute-start | bytes 98312 | tf_op jit(solution)/shard_map/ppermute | solution.py:17
  79.7 1.5 %collective-permute-start.16 = (bf16[4,64,512]{2,1,0:T(8,128)(2,1)S(1)}, bf16[4,64,512]{2,1,0:T(8,128)(2,1)S(1)}, u32[]{:S(2)}, u32[]{:S(2)}) collective-permute-start(bf16[4,64,512]{2,1,0:T(8,128)(2,1)S(1)} %shard_map.137.refs_0_), channel_id=1, source_target_pairs={{0,4},{4,0},{1,5},{5,1},{2,6},{6,2},{3,7},{7,3},{8,12},{12,8},{9,1... | collective-permute-start | bytes 786440 | tf_op jit(solution)/shard_map/ppermute | solution.py:17
  81.2 1.3 %collective-permute-done.26.refs_2_ = bf16[32,512]{1,0:T(8,128)(2,1)S(1)} collective-permute-done((bf16[32,512]{1,0:T(8,128)(2,1)S(1)}, bf16[32,512]{1,0:T(8,128)(2,1)S(1)}, u32[]{:S(2)}, u32[]{:S(2)}) %collective-permute-start.26) | collective-permute-done | bytes 32800 | tf_op jit(solution)/shard_map/ppermute | solution.py:17
  82.6 1.3 %collective-permute-done.28.refs_5_ = bf16[4,32,512]{2,1,0:T(8,128)(2,1)S(1)} collective-permute-done((bf16[4,32,512]{2,1,0:T(8,128)(2,1)S(1)}, bf16[4,32,512]{2,1,0:T(8,128)(2,1)S(1)}, u32[]{:S(2)}, u32[]{:S(2)}) %collective-permute-start.28) | collective-permute-done | bytes 131104 | tf_op jit(solution)/shard_map/ppermute | solution.py:17
  84.0 4.4 %collective-permute-done.16.refs_1_ = bf16[4,64,512]{2,1,0:T(8,128)(2,1)S(1)} collective-permute-done((bf16[4,64,512]{2,1,0:T(8,128)(2,1)S(1)}, bf16[4,64,512]{2,1,0:T(8,128)(2,1)S(1)}, u32[]{:S(2)}, u32[]{:S(2)}) %collective-permute-start.16) | collective-permute-done | bytes 262176 | tf_op jit(solution)/shard_map/ppermute | solution.py:17
  88.4 1.5 %collective-permute-done.29.refs_3_ = bf16[4,64,512]{2,1,0:T(8,128)(2,1)S(1)} collective-permute-done((bf16[4,64,512]{2,1,0:T(8,128)(2,1)S(1)}, bf16[4,64,512]{2,1,0:T(8,128)(2,1)S(1)}, u32[]{:S(2)}, u32[]{:S(2)}) %collective-permute-start.29) | collective-permute-done | bytes 262176 | tf_op jit(solution)/shard_map/ppermute | solution.py:17
  89.9 1.7 %shard_map.143 = (f32[1024,512]{1,0:T(8,128)}, f32[128,1024]{1,0:T(8,128)}) custom-call(bf16[4,64,512]{2,1,0:T(8,128)(2,1)S(1)} %shard_map.137.refs_0_, bf16[4,64,512]{2,1,0:T(8,128)(2,1)S(1)} %collective-permute-done.16.refs_1_, bf16[4,64,512]{2,1,0:T(8,128)(2,1)S(1)} %collective-permute-done.17.refs_2_, ...), custom_call_target="tpu_custom_call" | custom-call | flops 2147483648 | bytes 1048576 | tf_op jit(solution)/shard_map/pallas_call | solution.py:58
  (47 shorter events, 0.8 us)
Async XLA Ops:
  1.7 6.5 %copy-start.3 = (bf16[128,1024]{1,0:T(8,128)(2,1)S(1)}, bf16[128,1024]{1,0:T(8,128)(2,1)}, u32[]{:S(2)}) copy-start(bf16[128,1024]{1,0:T(8,128)(2,1)} %dec_ref.1) | copy-start | bytes 786436
  1.7 7.0 %copy-start.7 = (bf16[512]{0:T(512)(128)(2,1)S(1)}, bf16[512]{0:T(512)(128)(2,1)}, u32[]{:S(2)}) copy-start(bf16[512]{0:T(512)(128)(2,1)} %bias_ref.3) | copy-start | bytes 3076
  1.7 7.1 %copy-start = (bf16[128,1024]{1,0:T(8,128)(2,1)S(1)}, bf16[128,1024]{1,0:T(8,128)(2,1)}, u32[]{:S(2)}) copy-start(bf16[128,1024]{1,0:T(8,128)(2,1)} %weight_ref.5) | copy-start | bytes 786436
  1.8 7.1 %copy-start.1 = (bf16[1024,512]{1,0:T(8,128)(2,1)S(1)}, bf16[1024,512]{1,0:T(8,128)(2,1)}, u32[]{:S(2)}) copy-start(bf16[1024,512]{1,0:T(8,128)(2,1)} %half_ref.3) | copy-start | bytes 3145732
  1.8 15.1 %collective-permute-start = (bf16[512,512]{1,0:T(8,128)(2,1)S(1)}, bf16[512,512]{1,0:T(8,128)(2,1)S(1)}, u32[]{:S(2)}, u32[]{:S(2)}) collective-permute-start(bf16[512,512]{1,0:T(8,128)(2,1)S(1)} %constant_dynamic-slice_fusion), channel_id=1, source_target_pairs={{0,1},{1,0},{2,3},{3,2},{4,5},{5,4},{6,7},{7,6},{8,9},{9,8},{10,11... | collective-permute-start | bytes 1572872 | tf_op jit(solution)/shard_map/ppermute | solution.py:17
  8.1 8.7 %collective-permute-start.3 = (bf16[9,128,128]{2,1,0:T(8,128)(2,1)}, bf16[9,128,128]{2,1,0:T(8,128)(2,1)S(1)}, u32[]{:S(2)}, u32[]{:S(2)}) collective-permute-start(bf16[9,128,128]{2,1,0:T(8,128)(2,1)} %get-tuple-element.63), channel_id=1, source_target_pairs={{0,2},{2,0},{1,3},{3,1},{4,6},{6,4},{5,7},{7,5},{8,10},{10,8},{9,1... | collective-permute-start | bytes 884744 | tf_op jit(solution)/shard_map/ppermute | solution.py:17
  8.2 8.6 %collective-permute-start.2 = (bf16[128,1024]{1,0:T(8,128)(2,1)S(1)}, bf16[128,1024]{1,0:T(8,128)(2,1)S(1)}, u32[]{:S(2)}, u32[]{:S(2)}) collective-permute-start(bf16[128,1024]{1,0:T(8,128)(2,1)S(1)} %copy-done.3), channel_id=1, source_target_pairs={{0,2},{2,0},{1,3},{3,1},{4,6},{6,4},{5,7},{7,5},{8,10},{10,8},{9,1... | collective-permute-start | bytes 786440 | tf_op jit(solution)/shard_map/ppermute | solution.py:17
  8.7 8.1 %collective-permute-start.1 = (bf16[512]{0:T(512)(128)(2,1)S(1)}, bf16[512]{0:T(512)(128)(2,1)S(1)}, u32[]{:S(2)}, u32[]{:S(2)}) collective-permute-start(bf16[512]{0:T(512)(128)(2,1)S(1)} %copy-done.7), channel_id=1, source_target_pairs={{0,1},{1,0},{2,3},{3,2},{4,5},{5,4},{6,7},{7,6},{8,9},{9,8},{10,11... | collective-permute-start | bytes 3080 | tf_op jit(solution)/shard_map/ppermute | solution.py:17
  8.8 0.8 copy-start.5
  9.6 9.2 %copy-start.2 = (bf16[9,128,128]{2,1,0:T(8,128)(2,1)S(1)}, bf16[9,128,128]{2,1,0:T(8,128)(2,1)}, u32[]{:S(2)}) copy-start(bf16[9,128,128]{2,1,0:T(8,128)(2,1)} %get-tuple-element.70.jac_ref) | copy-start | bytes 884740
  11.4 1.4 %copy-start.8 = (f32[1152,512]{1,0:T(8,128)}, f32[1152,512]{1,0:T(8,128)S(1)}, u32[]{:S(2)}) copy-start(f32[1152,512]{1,0:T(8,128)S(1)} %get-tuple-element.66.lin_ref) | copy-start | bytes 7077892
  16.8 2.0 %collective-permute-start.4 = (bf16[512,512]{1,0:T(8,128)(2,1)S(1)}, bf16[512,512]{1,0:T(8,128)(2,1)S(1)}, u32[]{:S(2)}, u32[]{:S(2)}) collective-permute-start(bf16[512,512]{1,0:T(8,128)(2,1)S(1)} %collective-permute-done.got_ref), channel_id=1, source_target_pairs={{0,2},{2,0},{1,3},{3,1},{4,6},{6,4},{5,7},{7,5},{8,10},{10,8},{9,1... | collective-permute-start | bytes 1572872 | tf_op jit(solution)/shard_map/ppermute | solution.py:17
  25.3 2.7 %collective-permute-start.5 = (bf16[512,1024]{1,0:T(8,128)(2,1)S(1)}, bf16[512,1024]{1,0:T(8,128)(2,1)S(1)}, u32[]{:S(2)}, u32[]{:S(2)}) collective-permute-start(bf16[512,1024]{1,0:T(8,128)(2,1)S(1)} %get-tuple-element.73), channel_id=1, source_target_pairs={{0,2},{2,0},{1,3},{3,1},{4,6},{6,4},{5,7},{7,5},{8,10},{10,8},{9,1... | collective-permute-start | bytes 3145736 | tf_op jit(solution)/shard_map/ppermute | solution.py:17
  28.2 15.3 %copy-start.4 = (f32[128,128]{1,0:T(8,128)S(1)}, f32[128,128]{1,0:T(8,128)}, u32[]{:S(2)}) copy-start(f32[128,128]{1,0:T(8,128)} %get-tuple-element.99.turned_ref) | copy-start | bytes 196612
  28.3 15.3 %copy-start.6 = (f32[8,1024]{1,0:T(8,128)S(1)}, f32[8,1024]{1,0:T(8,128)}, u32[]{:S(2)}) copy-start(f32[8,1024]{1,0:T(8,128)} %get-tuple-element.61.act_ref) | copy-start | bytes 98308
  28.3 8.4 %collective-permute-start.6 = (bf16[256,512]{1,0:T(8,128)(2,1)S(1)}, bf16[256,512]{1,0:T(8,128)(2,1)S(1)}, u32[]{:S(2)}, u32[]{:S(2)}) collective-permute-start(bf16[256,512]{1,0:T(8,128)(2,1)S(1)} %get-tuple-element.75), channel_id=1, source_target_pairs={{0,1},{1,0},{4,5},{5,4},{2,3},{3,2},{6,7},{7,6},{8,9},{9,8},{12,13... | collective-permute-start | bytes 786440 | tf_op jit(solution)/shard_map/ppermute | solution.py:17
  30.1 9.2 %collective-permute-start.7 = (bf16[256,512]{1,0:T(8,128)(2,1)S(1)}, bf16[256,512]{1,0:T(8,128)(2,1)S(1)}, u32[]{:S(2)}, u32[]{:S(2)}) collective-permute-start(bf16[256,512]{1,0:T(8,128)(2,1)S(1)} %get-tuple-element.76), channel_id=1, source_target_pairs={{0,4},{1,5},{4,0},{5,1},{2,6},{3,7},{6,2},{7,3},{8,12},{9,13},{12,... | collective-permute-start | bytes 786440 | tf_op jit(solution)/shard_map/ppermute | solution.py:17
  31.5 12.0 %collective-permute-start.8 = (bf16[256,512]{1,0:T(8,128)(2,1)S(1)}, bf16[256,512]{1,0:T(8,128)(2,1)S(1)}, u32[]{:S(2)}, u32[]{:S(2)}) collective-permute-start(bf16[256,512]{1,0:T(8,128)(2,1)S(1)} %get-tuple-element.77), channel_id=1, source_target_pairs={{0,5},{1,4},{4,1},{5,0},{2,7},{3,6},{6,3},{7,2},{8,13},{9,12},{12,... | collective-permute-start | bytes 786440 | tf_op jit(solution)/shard_map/ppermute | solution.py:17
  43.5 20.4 %collective-permute-start.12 = (f32[128,1024]{1,0:T(8,128)S(1)}, f32[128,1024]{1,0:T(8,128)S(1)}, u32[]{:S(2)}, u32[]{:S(2)}) collective-permute-start(f32[128,1024]{1,0:T(8,128)S(1)} %get-tuple-element.92), channel_id=1, source_target_pairs={{0,2},{2,0},{1,3},{3,1},{4,6},{6,4},{5,7},{7,5},{8,10},{10,8},{9,1... | collective-permute-start | bytes 1572872 | tf_op jit(solution)/shard_map/ppermute | solution.py:17
  46.7 1.6 %collective-permute-start.18 = (bf16[144,512]{1,0:T(8,128)(2,1)S(1)}, bf16[144,512]{1,0:T(8,128)(2,1)S(1)}, u32[]{:S(2)}, u32[]{:S(2)}) collective-permute-start(bf16[144,512]{1,0:T(8,128)(2,1)S(1)} %get-tuple-element.102), channel_id=1, source_target_pairs={{0,2},{2,0},{1,3},{3,1},{4,6},{6,4},{5,7},{7,5},{8,10},{10,8},{9,1... | collective-permute-start | bytes 442376 | tf_op jit(solution)/shard_map/ppermute | solution.py:17
  48.4 4.5 %collective-permute-start.19 = (bf16[48,512]{1,0:T(8,128)(2,1)S(1)}, bf16[48,512]{1,0:T(8,128)(2,1)S(1)}, u32[]{:S(2)}, u32[]{:S(2)}) collective-permute-start(bf16[48,512]{1,0:T(8,128)(2,1)S(1)} %get-tuple-element.105), channel_id=1, source_target_pairs={{0,8},{8,0},{16,24},{24,16},{1,9},{9,1},{17,25},{25,17},{2,10},{10... | collective-permute-start | bytes 147464 | tf_op jit(solution)/shard_map/ppermute | solution.py:17
  50.2 6.1 %collective-permute-start.20 = (bf16[48,512]{1,0:T(8,128)(2,1)S(1)}, bf16[48,512]{1,0:T(8,128)(2,1)S(1)}, u32[]{:S(2)}, u32[]{:S(2)}) collective-permute-start(bf16[48,512]{1,0:T(8,128)(2,1)S(1)} %get-tuple-element.106), channel_id=1, source_target_pairs={{0,16},{8,24},{16,0},{24,8},{1,17},{9,25},{17,1},{25,9},{2,18},{10... | collective-permute-start | bytes 147464 | tf_op jit(solution)/shard_map/ppermute | solution.py:17
  52.7 5.9 %collective-permute-start.21 = (bf16[48,512]{1,0:T(8,128)(2,1)S(1)}, bf16[48,512]{1,0:T(8,128)(2,1)S(1)}, u32[]{:S(2)}, u32[]{:S(2)}) collective-permute-start(bf16[48,512]{1,0:T(8,128)(2,1)S(1)} %get-tuple-element.107), channel_id=1, source_target_pairs={{0,24},{8,16},{16,8},{24,0},{1,25},{9,17},{17,9},{25,1},{2,26},{10... | collective-permute-start | bytes 147464 | tf_op jit(solution)/shard_map/ppermute | solution.py:17
  58.7 14.0 %collective-permute-start.24 = (bf16[48,512]{1,0:T(8,128)(2,1)S(1)}, bf16[48,512]{1,0:T(8,128)(2,1)S(1)}, u32[]{:S(2)}, u32[]{:S(2)}) collective-permute-start(bf16[48,512]{1,0:T(8,128)(2,1)S(1)} %shard_map.140.refs_0_), channel_id=1, source_target_pairs={{0,5},{1,4},{4,1},{5,0},{2,7},{3,6},{6,3},{7,2},{8,13},{9,12},{12,... | collective-permute-start | bytes 147464 | tf_op jit(solution)/shard_map/ppermute | solution.py:17
  61.2 13.4 %collective-permute-start.23 = (bf16[48,512]{1,0:T(8,128)(2,1)S(1)}, bf16[48,512]{1,0:T(8,128)(2,1)S(1)}, u32[]{:S(2)}, u32[]{:S(2)}) collective-permute-start(bf16[48,512]{1,0:T(8,128)(2,1)S(1)} %shard_map.140.refs_0_), channel_id=1, source_target_pairs={{0,4},{1,5},{4,0},{5,1},{2,6},{3,7},{6,2},{7,3},{8,12},{9,13},{12,... | collective-permute-start | bytes 147464 | tf_op jit(solution)/shard_map/ppermute | solution.py:17
  62.0 5.7 %collective-permute-start.9 = (bf16[64,512]{1,0:T(8,128)(2,1)S(1)}, bf16[64,512]{1,0:T(8,128)(2,1)S(1)}, u32[]{:S(2)}, u32[]{:S(2)}) collective-permute-start(bf16[64,512]{1,0:T(8,128)(2,1)S(1)} %get-tuple-element.88), channel_id=1, source_target_pairs={{0,8},{8,0},{16,24},{24,16},{1,9},{9,1},{17,25},{25,17},{2,10},{10... | collective-permute-start | bytes 196616 | tf_op jit(solution)/shard_map/ppermute | solution.py:17
  62.1 6.2 %collective-permute-start.10 = (bf16[64,512]{1,0:T(8,128)(2,1)S(1)}, bf16[64,512]{1,0:T(8,128)(2,1)S(1)}, u32[]{:S(2)}, u32[]{:S(2)}) collective-permute-start(bf16[64,512]{1,0:T(8,128)(2,1)S(1)} %get-tuple-element.89), channel_id=1, source_target_pairs={{0,16},{8,24},{16,0},{24,8},{1,17},{9,25},{17,1},{25,9},{2,18},{10... | collective-permute-start | bytes 196616 | tf_op jit(solution)/shard_map/ppermute | solution.py:17
  63.9 6.2 %collective-permute-start.11 = (bf16[64,512]{1,0:T(8,128)(2,1)S(1)}, bf16[64,512]{1,0:T(8,128)(2,1)S(1)}, u32[]{:S(2)}, u32[]{:S(2)}) collective-permute-start(bf16[64,512]{1,0:T(8,128)(2,1)S(1)} %get-tuple-element.90), channel_id=1, source_target_pairs={{0,24},{8,16},{16,8},{24,0},{1,25},{9,17},{17,9},{25,1},{2,26},{10... | collective-permute-start | bytes 196616 | tf_op jit(solution)/shard_map/ppermute | solution.py:17
  67.7 6.8 %collective-permute-start.22 = (bf16[48,512]{1,0:T(8,128)(2,1)S(1)}, bf16[48,512]{1,0:T(8,128)(2,1)S(1)}, u32[]{:S(2)}, u32[]{:S(2)}) collective-permute-start(bf16[48,512]{1,0:T(8,128)(2,1)S(1)} %shard_map.140.refs_0_), channel_id=1, source_target_pairs={{0,1},{1,0},{4,5},{5,4},{2,3},{3,2},{6,7},{7,6},{8,9},{9,8},{12,13... | collective-permute-start | bytes 147464 | tf_op jit(solution)/shard_map/ppermute | solution.py:17
  70.1 7.6 %collective-permute-start.15 = (bf16[64,512]{1,0:T(8,128)(2,1)S(1)}, bf16[64,512]{1,0:T(8,128)(2,1)S(1)}, u32[]{:S(2)}, u32[]{:S(2)}) collective-permute-start(bf16[64,512]{1,0:T(8,128)(2,1)S(1)} %shard_map.136.refs_0_), channel_id=1, source_target_pairs={{0,24},{8,16},{16,8},{24,0},{1,25},{9,17},{17,9},{25,1},{2,26},{10... | collective-permute-start | bytes 196616 | tf_op jit(solution)/shard_map/ppermute | solution.py:17
  72.7 6.9 %collective-permute-start.14 = (bf16[64,512]{1,0:T(8,128)(2,1)S(1)}, bf16[64,512]{1,0:T(8,128)(2,1)S(1)}, u32[]{:S(2)}, u32[]{:S(2)}) collective-permute-start(bf16[64,512]{1,0:T(8,128)(2,1)S(1)} %shard_map.136.refs_0_), channel_id=1, source_target_pairs={{0,16},{8,24},{16,0},{24,8},{1,17},{9,25},{17,1},{25,9},{2,18},{10... | collective-permute-start | bytes 196616 | tf_op jit(solution)/shard_map/ppermute | solution.py:17
  72.7 6.9 %collective-permute-start.13 = (bf16[64,512]{1,0:T(8,128)(2,1)S(1)}, bf16[64,512]{1,0:T(8,128)(2,1)S(1)}, u32[]{:S(2)}, u32[]{:S(2)}) collective-permute-start(bf16[64,512]{1,0:T(8,128)(2,1)S(1)} %shard_map.136.refs_0_), channel_id=1, source_target_pairs={{0,8},{8,0},{16,24},{24,16},{1,9},{9,1},{17,25},{25,17},{2,10},{10... | collective-permute-start | bytes 196616 | tf_op jit(solution)/shard_map/ppermute | solution.py:17
  75.2 6.1 %collective-permute-start.27 = (bf16[32,512]{1,0:T(8,128)(2,1)S(1)}, bf16[32,512]{1,0:T(8,128)(2,1)S(1)}, u32[]{:S(2)}, u32[]{:S(2)}) collective-permute-start(bf16[32,512]{1,0:T(8,128)(2,1)S(1)} %get-tuple-element.108.refs_0_), channel_id=1, source_target_pairs={{0,24},{8,16},{16,8},{24,0},{1,25},{9,17},{17,9},{25,1},{2,26},{10... | collective-permute-start | bytes 98312 | tf_op jit(solution)/shard_map/ppermute | solution.py:17
  77.7 4.8 %collective-permute-start.26 = (bf16[32,512]{1,0:T(8,128)(2,1)S(1)}, bf16[32,512]{1,0:T(8,128)(2,1)S(1)}, u32[]{:S(2)}, u32[]{:S(2)}) collective-permute-start(bf16[32,512]{1,0:T(8,128)(2,1)S(1)} %get-tuple-element.108.refs_0_), channel_id=1, source_target_pairs={{0,16},{8,24},{16,0},{24,8},{1,17},{9,25},{17,1},{25,9},{2,18},{10... | collective-permute-start | bytes 98312 | tf_op jit(solution)/shard_map/ppermute | solution.py:17
  77.7 4.8 %collective-permute-start.25 = (bf16[32,512]{1,0:T(8,128)(2,1)S(1)}, bf16[32,512]{1,0:T(8,128)(2,1)S(1)}, u32[]{:S(2)}, u32[]{:S(2)}) collective-permute-start(bf16[32,512]{1,0:T(8,128)(2,1)S(1)} %get-tuple-element.108.refs_0_), channel_id=1, source_target_pairs={{0,8},{8,0},{16,24},{24,16},{1,9},{9,1},{17,25},{25,17},{2,10},{10... | collective-permute-start | bytes 98312 | tf_op jit(solution)/shard_map/ppermute | solution.py:17
  79.6 4.4 %collective-permute-start.17 = (bf16[4,64,512]{2,1,0:T(8,128)(2,1)S(1)}, bf16[4,64,512]{2,1,0:T(8,128)(2,1)S(1)}, u32[]{:S(2)}, u32[]{:S(2)}) collective-permute-start(bf16[4,64,512]{2,1,0:T(8,128)(2,1)S(1)} %shard_map.137.refs_0_), channel_id=1, source_target_pairs={{0,2},{2,0},{1,3},{3,1},{4,6},{6,4},{5,7},{7,5},{8,10},{10,8},{9,1... | collective-permute-start | bytes 786440 | tf_op jit(solution)/shard_map/ppermute | solution.py:17
  79.7 8.7 %collective-permute-start.16 = (bf16[4,64,512]{2,1,0:T(8,128)(2,1)S(1)}, bf16[4,64,512]{2,1,0:T(8,128)(2,1)S(1)}, u32[]{:S(2)}, u32[]{:S(2)}) collective-permute-start(bf16[4,64,512]{2,1,0:T(8,128)(2,1)S(1)} %shard_map.137.refs_0_), channel_id=1, source_target_pairs={{0,4},{4,0},{1,5},{5,1},{2,6},{6,2},{3,7},{7,3},{8,12},{12,8},{9,1... | collective-permute-start | bytes 786440 | tf_op jit(solution)/shard_map/ppermute | solution.py:17
  82.5 1.4 %collective-permute-start.28 = (bf16[4,32,512]{2,1,0:T(8,128)(2,1)S(1)}, bf16[4,32,512]{2,1,0:T(8,128)(2,1)S(1)}, u32[]{:S(2)}, u32[]{:S(2)}) collective-permute-start(bf16[4,32,512]{2,1,0:T(8,128)(2,1)S(1)} %shard_map.142.refs_4_), channel_id=1, source_target_pairs={{0,2},{2,0},{1,3},{3,1},{4,6},{6,4},{5,7},{7,5},{8,10},{10,8},{9,1... | collective-permute-start | bytes 393224 | tf_op jit(solution)/shard_map/ppermute | solution.py:17
  88.4 1.5 %collective-permute-start.29 = (bf16[4,64,512]{2,1,0:T(8,128)(2,1)S(1)}, bf16[4,64,512]{2,1,0:T(8,128)(2,1)S(1)}, u32[]{:S(2)}, u32[]{:S(2)}) collective-permute-start(bf16[4,64,512]{2,1,0:T(8,128)(2,1)S(1)} %collective-permute-done.16.refs_1_), channel_id=1, source_target_pairs={{0,2},{2,0},{1,3},{3,1},{4,6},{6,4},{5,7},{7,5},{8,10},{10,8},{9,1... | collective-permute-start | bytes 786440 | tf_op jit(solution)/shard_map/ppermute | solution.py:17
where the time goes:
time: 92 us; the launch traced here: 91.6 us
  waiting for transfers between devices  35.4 us (38%)
  starting transfers between devices  31.1 us (34%)
  Pallas kernels  20.9 us (23%)
  local copies, waits for them, and re-layouts  3.3 us (4%)
    ppermute x30, waiting for transfers between devices, swap(): return lax.ppermute(value, axes, [(j, j ^ step) for j in range(size)])  35.4 us
    ppermute x30, starting transfers between devices, swap(): return lax.ppermute(value, axes, [(j, j ^ step) for j in range(size)])  31.1 us
    pallas_call x16, Pallas kernels, pallas_call(): pl.pallas_call(body, out_shape=[jax.ShapeDtypeStruct(shape, kind) for sha...  20.9 us
    unnamed x18, local copies, waits for them, and re-layouts  2.22 us
  transfers between devices with their start and end apart: 30, of which 15 were waited for; matrix products, arithmetic and copies ran while one was open for 0% of the time, Pallas kernels for 14%

commit v1 on v0

--- a/solution.py
+++ b/solution.py
@@ -50,16 +50,19 @@
     return pl.ds(pl.multiple_of(index * size, size), size)
 
 
-def local_call(body, outs, args, specs=None, scratch=(), limit=24 << 20, cost=1.0):
-    return pallas_call(body, outs, args, specs, scratch, limit, cost)
-
-
-def pallas_call(body, outs, args, specs, scratch, limit, cost):
+def local_call(body, outs, args, **options):
+    return kernel_call(body, outs, args, **options)
+
+
+def kernel_call(
+    body, outs, args, specs=None, out_specs=None, scratch=(), aliases=None, limit=24 << 20, cost=1.0
+):
     return pl.pallas_call(
         body,
         out_shape=[jax.ShapeDtypeStruct(shape, kind) for shape, kind in outs],
         in_specs=[VMEM] * len(args) if specs is None else specs,
-        out_specs=[VMEM] * len(outs),
+        out_specs=[VMEM] * len(outs) if out_specs is None else out_specs,
+        input_output_aliases=aliases or {},
         scratch_shapes=list(scratch),
         compiler_params=pltpu.CompilerParams(vmem_limit_bytes=limit),
         cost_estimate=pl.CostEstimate(
@@ -98,10 +101,19 @@
                 moved.append(swap(values[step], axes, size, step))
             return moved
 
-        sent = part(hidden_weight, lax.axis_index("c"), nc, 0)
-        got = swap(sent, "y", ny, 1)
-        bias_got = swap(hidden_bias, "y", ny, 1)
-        decoder_got = swap(decoder_weight, "c", nc, 1)
+        shared = hrow_c // 2
+        near_rows = shared // nx
+        c, x = lax.axis_index("c"), lax.axis_index("x")
+        near = lax.dynamic_slice_in_dim(hidden_weight, c * hrow_c + x * near_rows, near_rows)
+        rest = lax.dynamic_slice_in_dim(
+            hidden_weight, c * hrow_c + shared - brow, hrow_c - shared + brow
+        )
+        line = lax.broadcasted_iota(jnp.int32, rest.shape, 0)
+        rest = jnp.where(line < brow, hidden_bias[None, :], rest)
+        _, near_got = swaps([near] * ny, "y", ny)
+        _, rest_got = swaps([rest] * ny, "y", ny)
+        _, decoder_got = swaps([decoder_weight] * nc, "c", nc)
+        _, far_got = swaps([near_got] * nx, "x", nx)
 
         def gather(
             window_ref, jac_ref, target_ref, input_ref, weight_ref, bias_ref,
@@ -115,24 +127,27 @@
                     copies.append(pltpu.make_async_copy(jac_ref.at[row], ref.at[i], sems.at[u, i]))
             for copy in copies:
                 copy.start()
-            line = lax.broadcasted_iota(jnp.int32, (rank, depth), 0)
-            place_of = lax.broadcasted_iota(jnp.int32, (rank, depth), 1)
+            padded_rows = -(-count // 16) * 16
+            line = lax.broadcasted_iota(jnp.int32, (padded_rows, depth), 0)
+            place_of = lax.broadcasted_iota(jnp.int32, (padded_rows, depth), 1)
+            pad = jnp.zeros((rank - padded_rows, rank), F32)
 
             def pick(member, table):
-                index = jnp.full((rank, depth), -1, jnp.int32)
+                index = jnp.full((padded_rows, depth), -1, jnp.int32)
                 for i in range(count):
                     index = jnp.where(line == i, window_ref[member * count + i], index)
                 chosen = jnp.where(index == place_of, 1.0, 0.0).astype(BF16)
                 return jnp.dot(chosen, table, preferred_element_type=F32)
 
             inputs = pick(me, input_ref[...])
-            turned_ref[...] = inputs.T
+            turned_ref[...] = jnp.concatenate([inputs, pad]).T
             first_pre = jnp.dot(
                 inputs.astype(BF16), weight_ref[...], preferred_element_type=F32
             )[:count]
             act_ref[...] = jnp.tanh(first_pre + bias_ref[...].astype(F32).reshape(1, hidden))
-            own_ref[count] = pick(me, target_ref[...]).T.astype(BF16)
-            away_ref[count] = pick(me ^ 1, target_ref[...]).T.astype(BF16)
+            for member, ref in ((me, own_ref), (me ^ 1, away_ref)):
+                target = jnp.concatenate([pick(member, target_ref[...]), pad])
+                ref[count] = target.T.astype(BF16)
             for copy in copies:
                 copy.wait()
 
@@ -146,7 +161,7 @@
             scratch=[pltpu.SemaphoreType.DMA((nc, count))],
             limit=60 << 20,
         )
-        jac_got = swap(jac_away, "c", nc, 1)
+        _, jac_got = swaps([jac_away] * nc, "c", nc)
 
         def warm(act_ref, weight_ref, half_ref, tan_ref, side_ref, lin_ref):
             act = act_ref[...]
@@ -173,49 +188,74 @@
             cost=2,
             limit=30 << 20,
         )
-        got, bias_got, decoder_got, jac_got, first_tan = lax.optimization_barrier(
-            (got, bias_got, decoder_got, jac_got, first_tan)
-        )
-        got_core = swap(got, "c", nc, 1)
-
-        def main(
-            tan1_ref, side_ref, lin_ref, got_ref, core_ref, bias_ref, bias_got_ref,
-            dec_ref, dec_got_ref, jac_ref, jac_got_ref,
-            half_ref, tan_ref, miss_ref, round_ref, sum_ref, out_ref,
-            lin_got_ref, wide_ref, net_ref, back_ref,
+
+        def ready(
+            lin_ref, bias_ref, dec_ref, dec_got_ref, jac_ref, jac_got_ref,
+            wide_ref, tan_ref, net_ref,
         ):
-            me, my = lax.axis_index("c"), lax.axis_index("y")
-            half_ref[aligned(me, hrow_c)] = got_ref[...]
-            half_ref[aligned(me ^ 1, hrow_c)] = core_ref[...]
+            my = lax.axis_index("y")
             for b in range(ny):
                 columns = slice(b * kw, (b + 1) * kw)
                 wide_ref[:outs, columns] = dec_ref[:, aligned(my ^ b, kw)]
                 wide_ref[outs:, columns] = dec_got_ref[:, aligned(my ^ b, kw)]
-            lin_got_ref[...] = jnp.dot(tan1_ref[...], half_ref[...], preferred_element_type=F32)
-            pad = jnp.zeros((rank - count, kw), F32)
-            last = slice(count * rank, total)
-            lins, acts, slopes = (lin_ref, lin_got_ref), [], []
-            for b, (lin, bias) in enumerate(zip(lins, (bias_ref, bias_got_ref))):
-                columns = slice(b * kw, (b + 1) * kw)
-                pre = lin[count * rank : count * rank + count]
-                act = jnp.tanh(pre + bias[...].astype(F32).reshape(1, kw))
-                slope = 1.0 - act * act
-                acts.append(act)
-                slopes.append(slope)
-                tan_ref[last, columns] = jnp.concatenate([act, pad]).astype(BF16)
-                for s in range(count):
-                    rows = slice(s * rank, (s + 1) * rank)
-                    tan_ref[rows, columns] = (slope[s : s + 1] * lin[rows]).astype(BF16)
-            net_ref[...] = dot(wide_ref[...], tan_ref[...], ((1,), (1,)))
+            hidden_tangents(lin_ref, *hidden_slopes(lin_ref, hidden_row(bias_ref)), tan_ref)
+            net_ref[...] = dot(wide_ref[:, :kw], tan_ref[...], ((1,), (1,)))
             for s in range(count + 1):
                 columns = slice(s * rank, (s + 1) * rank)
-                for part_rows, jac in ((slice(0, outs), jac_ref), (slice(outs, None), jac_got_ref)):
-                    miss = net_ref[part_rows, columns] - jac[s].astype(F32)
-                    miss_ref[part_rows, columns] = miss.astype(BF16)
+                net_ref[:outs, columns] -= jac_ref[s].astype(F32)
+                net_ref[outs:, columns] -= jac_got_ref[s].astype(F32)
+
+        def hidden_row(bias_ref):
+            return bias_ref[...].astype(F32).reshape(1, kw)
+
+        def hidden_slopes(lin_ref, bias):
+            act = jnp.tanh(lin_ref[count * rank : count * rank + count] + bias)
+            return act, 1.0 - act * act
+
+        def hidden_tangents(lin_ref, act, slope, tan_ref):
+            pad = jnp.zeros((rank - count, kw), F32)
+            for s in range(count):
+                rows = slice(s * rank, (s + 1) * rank)
+                tan_ref[rows] = (slope[s : s + 1] * lin_ref[rows]).astype(BF16)
+            tan_ref[count * rank :] = jnp.concatenate([act, pad]).astype(BF16)
+
+        wide, tan_own, net_own = local_call(
+            ready,
+            [((nc * outs, hidden), BF16), ((total, kw), BF16), ((nc * outs, total), F32)],
+            (lin_own, hidden_bias, decoder_weight, decoder_got, jac_own, jac_got),
+            cost=1.5,
+            limit=16 << 20,
+        )
+        near_got, rest_got, far_got, tan_own = lax.optimization_barrier(
+            (near_got, rest_got, far_got, tan_own)
+        )
+        fetched = (near_got, far_got, rest_got)
+        fetched += tuple(swap(value, "c", nc, 1) for value in fetched)
+
+        def main(
+            tan1_ref, side_ref, lin_ref, near_ref, far_ref, rest_ref, near2_ref, far2_ref, rest2_ref,
+            bias_ref, wide_ref, net_own_ref,
+            half_ref, tan_ref, miss_ref, round_ref, sum_ref, out_ref,
+            lin_got_ref, back_ref,
+        ):
+            me, mx = lax.axis_index("c"), lax.axis_index("x")
+            for u, refs in enumerate(((near_ref, far_ref, rest_ref), (near2_ref, far2_ref, rest2_ref))):
+                base = (me ^ u) * hrow_c
+                for a in range(nx):
+                    start = pl.multiple_of(base + (mx ^ a) * near_rows, near_rows)
+                    half_ref[pl.ds(start, near_rows)] = refs[a][...]
+                start = pl.multiple_of(base + shared, shared)
+                half_ref[pl.ds(start, hrow_c - shared)] = refs[2][brow:]
+            lin_got_ref[...] = jnp.dot(tan1_ref[...], half_ref[...], preferred_element_type=F32)
+            bias_got = rest_ref[:brow].astype(F32)[:1]
+            own, other = hidden_slopes(lin_ref, hidden_row(bias_ref)), hidden_slopes(lin_got_ref, bias_got)
+            hidden_tangents(lin_got_ref, *other, tan_ref)
+            net = net_own_ref[...] + dot(wide_ref[:, kw:], tan_ref[...], ((1,), (1,)))
+            miss_ref[...] = net.astype(BF16)
             back_ref[...] = dot(miss_ref[...], wide_ref[...], ((0,), (0,)))
-            for b, lin in enumerate(lins):
+            pad = jnp.zeros((rank - count, kw), F32)
+            for b, (lin, (act, slope)) in enumerate(((lin_ref, own), (lin_got_ref, other))):
                 columns = slice(b * kw, (b + 1) * kw)
-                act, slope = acts[b], slopes[b]
                 sums = []
                 for s in range(count):
                     rows = slice(s * rank, (s + 1) * rank)
@@ -223,60 +263,74 @@
                     sums.append(jnp.sum(back * lin[rows], axis=0, keepdims=True))
                     round_ref[rows, columns] = (back * slope[s : s + 1]).astype(BF16)
                 act_back = back_ref[count * rank : count * rank + count, columns]
-                sums = jnp.concatenate(sums)
-                pre_back = act_back * slope - 2.0 * act * slope * sums
-                round_ref[last, columns] = jnp.concatenate([pre_back, pad]).astype(BF16)
+                pre_back = act_back * slope - 2.0 * act * slope * jnp.concatenate(sums)
+                round_ref[count * rank :, columns] = jnp.concatenate([pre_back, pad]).astype(BF16)
                 sum_ref[:, columns] = jnp.sum(pre_back, axis=0, keepdims=True)
             out_ref[...] = jnp.dot(
-                side_ref[aligned(me ^ 1, hrow_c)], round_ref[...], preferred_element_type=F32
+                side_ref[aligned(me ^ 1, hrow_c)], round_ref[:, kw:], preferred_element_type=F32
             ).astype(BF16)
 
-        half_got, hidden_tan, miss, lin_round, hidden_sum, g_away = local_call(
+        half_got, tan_got, miss, lin_round, hidden_sum, g_away = local_call(
             main,
             [
                 ((hidden, kw), BF16),
-                ((total, hidden), BF16),
+                ((total, kw), BF16),
                 ((nc * outs, total), BF16),
                 ((total, hidden), BF16),
                 ((1, hidden), F32),
-                ((hrow_c, hidden), BF16),
+                ((hrow_c, kw), BF16),
             ],
-            (
-                first_tan, first_side, lin_own, got, got_core, hidden_bias, bias_got,
-                decoder_weight, decoder_got, jac_own, jac_got,
-            ),
-            cost=6.5,
-            scratch=[
-                pltpu.VMEM((total, kw), F32),
-                pltpu.VMEM((nc * outs, hidden), BF16),
-                pltpu.VMEM((nc * outs, total), F32),
-                pltpu.VMEM((total, hidden), F32),
-            ],
-            limit=40 << 20,
-        )
-        g_got = swap(g_away, "c", nc, 1)
-
-        def own_rows(side_ref, round_ref, out_ref):
+            (first_tan, first_side, lin_own, *fetched, hidden_bias, wide, net_own),
+            cost=5,
+            scratch=[pltpu.VMEM((total, kw), F32), pltpu.VMEM((total, hidden), F32)],
+            limit=36 << 20,
+        )
+        _, g_got = swaps([g_away] * nc, "c", nc)
+
+        def between(side_ref, round_ref, own_ref, away_ref):
             me = lax.axis_index("c")
-            out_ref[...] = jnp.dot(
-                side_ref[aligned(me, hrow_c)], round_ref[...], preferred_element_type=F32
+            own_ref[...] = jnp.dot(
+                side_ref[aligned(me, hrow_c)], round_ref[:, kw:], preferred_element_type=F32
             )
-
-        (g_own,) = local_call(
-            own_rows, [((hrow_c, hidden), F32)], (first_side, lin_round), cost=1.5, limit=16 << 20
-        )
+            away_ref[...] = jnp.dot(
+                side_ref[aligned(me ^ 1, hrow_c)], round_ref[:, :kw], preferred_element_type=F32
+            ).astype(BF16)
+
+        g_own, g_away = local_call(
+            between,
+            [((hrow_c, kw), F32), ((hrow_c, kw), BF16)],
+            (first_side, lin_round),
+            cost=1.5,
+            limit=16 << 20,
+        )
+        _, g_got_last = swaps([g_away] * nc, "c", nc)
 
         def merge_core(g_ref, got_ref, *out_refs):
             mx = lax.axis_index("x")
-            for s, out_ref in enumerate(out_refs):
-                a, b = s // ny, s % ny
-                rows, columns = aligned(mx ^ a, hrow_x), slice(b * kw, (b + 1) * kw)
-                value = g_ref[rows, columns] + got_ref[rows, columns].astype(F32)
-                out_ref[...] = value.astype(BF16)
-
-        plane = local_call(merge_core, [((hrow_x, kw), BF16)] * nxy, (g_own, g_got))
-        (lin_round, miss, hidden_tan), _ = lax.optimization_barrier(
-            ((lin_round, miss, hidden_tan), plane[0])
+            for a, out_ref in enumerate(out_refs):
+                rows = aligned(mx ^ a, hrow_x)
+                out_ref[...] = (g_ref[rows] + got_ref[rows].astype(F32)).astype(BF16)
+
+        rows_shape = ((hrow_x, kw), BF16)
+        plane1, plane3 = local_call(merge_core, [rows_shape] * nx, (g_own, g_got))
+
+        def finish_core(side_ref, round_ref, got_ref, *refs):
+            me, g_ref = lax.axis_index("c"), refs[-1]
+            g_ref[...] = jnp.dot(
+                side_ref[aligned(me, hrow_c)], round_ref[:, :kw], preferred_element_type=F32
+            )
+            merge_core(g_ref, got_ref, *refs[:-1])
+
+        plane0, plane2 = local_call(
+            finish_core,
+            [rows_shape] * nx,
+            (first_side, lin_round, g_got_last),
+            scratch=[pltpu.VMEM((hrow_c, kw), F32)],
+            limit=16 << 20,
+        )
+        plane = [plane0, plane1, plane2, plane3]
+        (lin_round, miss, tan_got), _ = lax.optimization_barrier(
+            ((lin_round, miss, tan_got), plane[0])
         )
         plane = swaps(plane, ("x", "y"), nxy)
 
@@ -352,12 +406,15 @@
         )
         side = swaps(side, "z", nz)
 
-        def readout(miss_ref, tan_ref, own_ref, away_ref):
-            own_ref[...] = jnp.dot(miss_ref[:outs], tan_ref[...], preferred_element_type=F32)
-            away_ref[...] = jnp.dot(miss_ref[outs:], tan_ref[...], preferred_element_type=F32)
+        def readout(miss_ref, tan_ref, tan_got_ref, own_ref, away_ref):
+            for ref, rows in ((own_ref, slice(0, outs)), (away_ref, slice(outs, None))):
+                for b, tan in enumerate((tan_ref, tan_got_ref)):
+                    ref[:, b * kw : (b + 1) * kw] = jnp.dot(
+                        miss_ref[rows], tan[...], preferred_element_type=F32
+                    )
 
         d_own, d_away = local_call(
-            readout, [((outs, hidden), F32)] * 2, (miss, hidden_tan), cost=1, limit=16 << 20
+            readout, [((outs, hidden), F32)] * 2, (miss, tan_own, tan_got), cost=1, limit=16 << 20
         )
         *plane, d_away = lax.optimization_barrier((*plane, d_away))
         d_got = swap(d_away, "c", nc, 1)
@@ -423,29 +480,67 @@
         _, across = swaps([both] * nx, "x", nx)
         _, both_core = swaps([both] * nc, "c", nc)
         _, first_core = swaps([first] * nc, "c", nc)
-        across, both_core, first_core = lax.optimization_barrier((across, both_core, first_core))
         across_core = swap(across, "c", nc, 1)
 
-        def spread_out(*refs):
-            in_refs, side_refs = refs[: nc * nx], refs[nc * nx : nc * nx + nc]
-            hidden_ref, first_ref = refs[-2:]
+        def put(refs, base, size, out_ref, stage_ref, sem_ref, slot):
+            copies = []
+            for i in range(nz):
+                stage_ref[slot * nz + i] = refs[i].astype(F32)
+                copies.append(
+                    pltpu.make_async_copy(
+                        stage_ref.at[slot * nz + i],
+                        out_ref.at[aligned(base * nz + i, size)],
+                        sem_ref.at[slot * nz + i],
+                    )
+                )
+                copies[-1].start()
+            return copies
+
+        def spread_early(both_ref, core_ref, out_ref, stage_ref, sem_ref):
             mx, mc = lax.axis_index("x"), lax.axis_index("c")
-            for s, ref in enumerate(in_refs):
-                base = (mc ^ (s // nx)) * nx + (mx ^ (s % nx))
-                for i in range(nz):
-                    hidden_ref[aligned(base * nz + i, hrow_z)] = ref[i].astype(F32)
-            for u, ref in enumerate(side_refs):
+            copies = put(both_ref, mc * nx + mx, hrow_z, out_ref, stage_ref, sem_ref, 0)
+            copies += put(core_ref, (mc ^ 1) * nx + mx, hrow_z, out_ref, stage_ref, sem_ref, 1)
+            for copy in copies:
+                copy.wait()
+
+        stage = [pltpu.VMEM((nc * nz, hrow_z, kw), F32), pltpu.SemaphoreType.DMA((nc * nz,))]
+
+        def spread_first(own_ref, core_ref, first_ref):
+            mc = lax.axis_index("c")
+            for u, ref in enumerate((own_ref, core_ref)):
                 for i in range(nz):
                     rows = aligned((mc ^ u) * nz + i, frow_z)
                     value = ref[i].astype(F32)
                     for b in range(ny):
                         first_ref[rows, b * kw : (b + 1) * kw] = value[b * frow_z : (b + 1) * frow_z]
 
-        hidden_out, first_out = local_call(
-            spread_out,
-            [((hidden, kw), F32), ((rank, hidden), F32)],
-            (both, across, both_core, across_core, first, first_core),
-            cost=2,
+        def spread_late(held_ref, across_ref, core_ref, out_ref, stage_ref, sem_ref):
+            mx, mc = lax.axis_index("x"), lax.axis_index("c")
+            copies = put(across_ref, mc * nx + (mx ^ 1), hrow_z, out_ref, stage_ref, sem_ref, 0)
+            copies += put(core_ref, (mc ^ 1) * nx + (mx ^ 1), hrow_z, out_ref, stage_ref, sem_ref, 1)
+            for copy in copies:
+                copy.wait()
+
+        (hidden_out,) = local_call(
+            spread_early,
+            [((hidden, kw), F32)],
+            (both, both_core),
+            out_specs=[ANY],
+            scratch=stage,
+            limit=8 << 20,
+        )
+        (first_out,) = local_call(
+            spread_first, [((rank, hidden), F32)], (first, first_core), limit=4 << 20
+        )
+        (hidden_out,) = local_call(
+            spread_late,
+            [((hidden, kw), F32)],
+            (hidden_out, across, across_core),
+            specs=[ANY, VMEM, VMEM],
+            out_specs=[ANY],
+            scratch=stage,
+            aliases={0: 0},
+            limit=8 << 20,
         )
         return (first_out, first_bias_out, hidden_out, hidden_bias_out, decoder_grad)
 

time: 92 us -> 82.5 us (0.90)
  waiting for transfers between devices: 35.4 us -> 23.5 us
  starting transfers between devices: 31.1 us -> 35 us
  local copies, waits for them, and re-layouts: 3.3 us -> 1.71 us
    ppermute x30 -> x34, waiting for transfers between devices: 35.4 us -> 23.5 us  [swap(): return lax.ppermute(value, axes, [(j, j ^ step) for j in range(size)])]
    ppermute x30 -> x34, starting transfers between devices: 31.1 us -> 35 us  [swap(): return lax.ppermute(value, axes, [(j, j ^ step) for j in range(size)])]
    unnamed x18 -> x16, local copies, waits for them, and re-layouts: 2.22 us -> 0.79 us
    pallas_call x16 -> x20, Pallas kernels: 20.9 us -> 20.9 us  [kernel_call(): pl.pallas_call(body, out_shape=[jax.ShapeDtypeStruct(shape, kind) for sha...]
  transfers between devices with their start and end apart: 30 -> 34, of which waited for: 15 -> 14; matrix products, arithmetic and copies ran while one was open for 0% -> 0% of each run, Pallas kernels for 14% -> 20%
where the time goes in v1:
time: 82.5 us; the launch traced here: 82.1 us
  starting transfers between devices  35 us (42%)
  waiting for transfers between devices  23.5 us (28%)
  Pallas kernels  20.9 us (25%)
  local copies, waits for them, and re-layouts  1.71 us (2%)
  between operations  0.87 us (1%)
    ppermute x34, starting transfers between devices, swap(): return lax.ppermute(value, axes, [(j, j ^ step) for j in range(size)])  35 us
    ppermute x34, waiting for transfers between devices, swap(): return lax.ppermute(value, axes, [(j, j ^ step) for j in range(size)])  23.5 us
    pallas_call x20, Pallas kernels, kernel_call(): pl.pallas_call(body, out_shape=[jax.ShapeDtypeStruct(shape, kind) for sha...  20.9 us
  transfers between devices with their start and end apart: 34, of which 14 were waited for; matrix products, arithmetic and copies ran while one was open for 0% of the time, Pallas kernels for 20%

profile of v1, /device:TPU:0, one launch (start us, length us, event | category | flops | bytes accessed | tf_op | source)
XLA Modules:
  0.0 82.1 jit_solution(5350455617505328783)
XLA Ops:
  0.6 0.9 %constant_dynamic-slice_fusion = bf16[128,512]{1,0:T(8,128)(2,1)S(1)} fusion(bf16[1024,512]{1,0:T(8,128)(2,1)} %half_ref.3, s32[]{:T(128)S(6)} %select_n.10), kind=kLoop, calls=%fused_computation.2 | loop fusion | bytes 262148 | tf_op jit(solution)/shard_map/dynamic_slice | solution.py:107
  1.6 3.1 %collective-permute-start = (bf16[128,512]{1,0:T(8,128)(2,1)S(1)}, bf16[128,512]{1,0:T(8,128)(2,1)S(1)}, u32[]{:S(2)}, u32[]{:S(2)}) collective-permute-start(bf16[128,512]{1,0:T(8,128)(2,1)S(1)} %constant_dynamic-slice_fusion), channel_id=1, source_target_pairs={{0,1},{1,0},{2,3},{3,2},{4,5},{5,4},{6,7},{7,6},{8,9},{9,8},{10,11... | collective-permute-start | bytes 393224 | tf_op jit(solution)/shard_map/ppermute | solution.py:17
  4.7 3.2 %shard_map.128 = (bf16[9,128,128]{2,1,0:T(8,128)(2,1)}, bf16[9,128,128]{2,1,0:T(8,128)(2,1)}, f32[8,1024]{1,0:T(8,128)}, f32[128,128]{1,0:T(8,128)}) custom-call(s32[16]{0:T(128)} %window_ref.1, bf16[512,128,128]{2,1,0:T(8,128)(2,1)} %jac_ref.1, bf16[512,128]{1,0:T(8,128)(2,1)} %target_ref.1, bf16[512,128]{1,0:T(8,128)(2,1)} %input_ref.1, ...), custom_call_target="tpu_custom_call" | custom-call | flops 4294967296 | bytes 1048576 | tf_op jit(solution)/shard_map/pallas_call | solution.py:60
  7.9 0.6 collective-permute-start.4
  8.7 0.8 copy-done.6
  9.5 1.8 %shard_map.129 = (bf16[1152,1024]{1,0:T(8,128)(2,1)S(1)}, bf16[1024,1152]{1,0:T(8,128)(2,1)S(1)}, f32[1152,512]{1,0:T(8,128)S(1)}) custom-call(f32[8,1024]{1,0:T(8,128)S(1)} %copy-done.6, bf16[128,1024]{1,0:T(8,128)(2,1)S(1)} %copy-done, bf16[1024,512]{1,0:T(8,128)(2,1)S(1)} %copy-done.1), custom_call_target="tpu_custom_call" | custom-call | flops 2147483648 | bytes 1048576 | tf_op jit(solution)/shard_map/pallas_call | solution.py:60
  11.3 2.0 %collective-permute-start.2 = (bf16[128,512]{1,0:T(8,128)(2,1)S(1)}, bf16[128,512]{1,0:T(8,128)(2,1)S(1)}, u32[]{:S(2)}, u32[]{:S(2)}) collective-permute-start(bf16[128,512]{1,0:T(8,128)(2,1)S(1)} %collective-permute-done.near_ref), channel_id=1, source_target_pairs={{0,4},{4,0},{1,5},{5,1},{2,6},{6,2},{3,7},{7,3},{8,12},{12,8},{9,1... | collective-permute-start | bytes 393224 | tf_op jit(solution)/shard_map/ppermute | solution.py:17
  13.3 0.7 shard_map.130
  14.0 2.7 %collective-permute-done.2.far_ref = bf16[128,512]{1,0:T(8,128)(2,1)S(1)} collective-permute-done((bf16[128,512]{1,0:T(8,128)(2,1)S(1)}, bf16[128,512]{1,0:T(8,128)(2,1)S(1)}, u32[]{:S(2)}, u32[]{:S(2)}) %collective-permute-start.2) | collective-permute-done | bytes 131104 | tf_op jit(solution)/shard_map/ppermute | solution.py:17
  17.3 0.5 collective-permute-start.5
  17.8 1.2 %collective-permute-done.5.near2_ref = bf16[128,512]{1,0:T(8,128)(2,1)S(1)} collective-permute-done((bf16[128,512]{1,0:T(8,128)(2,1)S(1)}, bf16[128,512]{1,0:T(8,128)(2,1)S(1)}, u32[]{:S(2)}, u32[]{:S(2)}) %collective-permute-start.5) | collective-permute-done | bytes 131104 | tf_op jit(solution)/shard_map/ppermute | solution.py:17
  19.2 3.7 %shard_map.131 = (bf16[1024,512]{1,0:T(8,128)(2,1)S(1)}, bf16[1152,512]{1,0:T(8,128)(2,1)S(1)}, bf16[256,1152]{1,0:T(8,128)(2,1)S(1)}, bf16[1152,1024]{1,0:T(8,1...) custom-call(bf16[1152,1024]{1,0:T(8,128)(2,1)S(1)} %get-tuple-element.61.tan1_ref, ...), custom_call_target="tpu_custom_call" | custom-call | flops 5368709120 | bytes 1048576 | tf_op jit(solution)/shard_map/pallas_call | solution.py:60
  23.1 1.5 %shard_map.132 = (f32[512,512]{1,0:T(8,128)S(1)}, bf16[512,512]{1,0:T(8,128)(2,1)S(1)}) custom-call(bf16[1024,1152]{1,0:T(8,128)(2,1)S(1)} %get-tuple-element.62.side_ref, bf16[1152,1024]{1,0:T(8,128)(2,1)S(1)} %get-tuple-element.77.round_ref), custom_call_target="tpu_custom_call" | custom-call | flops 1610612736 | bytes 1048576 | tf_op jit(solution)/shard_map/pallas_call | solution.py:60
  25.2 1.3 %collective-permute-start.21 = (bf16[256,512]{1,0:T(8,128)(2,1)S(1)}, bf16[256,512]{1,0:T(8,128)(2,1)S(1)}, u32[]{:S(2)}, u32[]{:S(2)}) collective-permute-start(bf16[256,512]{1,0:T(8,128)(2,1)S(1)} %get-tuple-element.92), channel_id=1, source_target_pairs={{0,1},{1,0},{4,5},{5,4},{2,3},{3,2},{6,7},{7,6},{8,9},{9,8},{12,13... | collective-permute-start | bytes 786440 | tf_op jit(solution)/shard_map/ppermute | solution.py:17
  26.5 1.7 %collective-permute-start.23 = (bf16[256,512]{1,0:T(8,128)(2,1)S(1)}, bf16[256,512]{1,0:T(8,128)(2,1)S(1)}, u32[]{:S(2)}, u32[]{:S(2)}) collective-permute-start(bf16[256,512]{1,0:T(8,128)(2,1)S(1)} %get-tuple-element.94), channel_id=1, source_target_pairs={{0,5},{1,4},{4,1},{5,0},{2,7},{3,6},{6,3},{7,2},{8,13},{9,12},{12,... | collective-permute-start | bytes 786440 | tf_op jit(solution)/shard_map/ppermute | solution.py:17
  28.2 1.0 %shard_map.133 = (bf16[256,512]{1,0:T(8,128)(2,1)S(1)}, bf16[256,512]{1,0:T(8,128)(2,1)S(1)}) custom-call(bf16[1024,1152]{1,0:T(8,128)(2,1)S(1)} %get-tuple-element.62.side_ref, bf16[1152,1024]{1,0:T(8,128)(2,1)S(1)} %get-tuple-element.77.round_ref, bf16[512,512]{1,0:T(8,128)(2,1)S(1)} %collective-permute-done.8.got_ref), custom_call_target="tpu_custom_call" | custom-call | flops 1073741824 | bytes 1048576 | tf_op jit(solution)/shard_map/pallas_call | solution.py:60
  29.3 0.6 collective-permute-start.22
  29.9 0.9 %shard_map.141 = (f32[128,1024]{1,0:T(8,128)S(1)}, f32[128,1024]{1,0:T(8,128)S(1)}) custom-call(bf16[256,1152]{1,0:T(8,128)(2,1)S(1)} %get-tuple-element.95.miss_ref, bf16[1152,512]{1,0:T(8,128)(2,1)S(1)} %get-tuple-element.96.tan_ref, bf16[1152,512]{1,0:T(8,128)(2,1)S(1)} %get-tuple-element.97.tan_got_ref), custom_call_target="tpu_custom_call" | custom-call | flops 1073741824 | bytes 1048576 | tf_op jit(solution)/shard_map/pallas_call | solution.py:60
  30.7 8.5 %collective-permute-done.21.refs_1_ = bf16[256,512]{1,0:T(8,128)(2,1)S(1)} collective-permute-done((bf16[256,512]{1,0:T(8,128)(2,1)S(1)}, bf16[256,512]{1,0:T(8,128)(2,1)S(1)}, u32[]{:S(2)}, u32[]{:S(2)}) %collective-permute-start.21) | collective-permute-done | bytes 262176 | tf_op jit(solution)/shard_map/ppermute | solution.py:17
  39.2 1.2 %collective-permute-done.22.refs_2_ = bf16[256,512]{1,0:T(8,128)(2,1)S(1)} collective-permute-done((bf16[256,512]{1,0:T(8,128)(2,1)S(1)}, bf16[256,512]{1,0:T(8,128)(2,1)S(1)}, u32[]{:S(2)}, u32[]{:S(2)}) %collective-permute-start.22) | collective-permute-done | bytes 262176 | tf_op jit(solution)/shard_map/ppermute | solution.py:17
  40.5 3.2 %shard_map.134 = (f32[64,1024]{1,0:T(8,128)S(1)}, bf16[144,512]{1,0:T(8,128)(2,1)S(1)}, bf16[16,512]{1,0:T(8,128)(2,1)S(1)}) custom-call(bf16[1152,1024]{1,0:T(8,128)(2,1)S(1)} %get-tuple-element.77.round_ref, bf16[1024,512]{1,0:T(8,128)(2,1)S(1)} %copy-done.1, bf16[1024,512]{1,0:T(8,128)(2,1)S(1)} %get-tuple-element.78.got_ref, f32[8,1024]{1,0:T(8,128)S(1)} %copy-done.7, ...), custom_call_target="tpu_custom_call" | custom-call | flops 3221225472 | bytes 1048576 | tf_op jit(solution)/shard_map/pallas_call | solution.py:60
  43.7 0.6 collective-permute-start.9
  44.2 1.0 %collective-permute-done.9.got_ref = bf16[144,512]{1,0:T(8,128)(2,1)S(1)} collective-permute-done((bf16[144,512]{1,0:T(8,128)(2,1)S(1)}, bf16[144,512]{1,0:T(8,128)(2,1)S(1)}, u32[]{:S(2)}, u32[]{:S(2)}) %collective-permute-start.9) | collective-permute-done | bytes 147488 | tf_op jit(solution)/shard_map/ppermute | solution.py:17
  45.3 1.6 %collective-permute-start.10 = (bf16[48,512]{1,0:T(8,128)(2,1)S(1)}, bf16[48,512]{1,0:T(8,128)(2,1)S(1)}, u32[]{:S(2)}, u32[]{:S(2)}) collective-permute-start(bf16[48,512]{1,0:T(8,128)(2,1)S(1)} %get-tuple-element.85), channel_id=1, source_target_pairs={{0,8},{8,0},{16,24},{24,16},{1,9},{9,1},{17,25},{25,17},{2,10},{10... | collective-permute-start | bytes 147464 | tf_op jit(solution)/shard_map/ppermute | solution.py:17
  46.9 2.6 %collective-permute-start.11 = (bf16[48,512]{1,0:T(8,128)(2,1)S(1)}, bf16[48,512]{1,0:T(8,128)(2,1)S(1)}, u32[]{:S(2)}, u32[]{:S(2)}) collective-permute-start(bf16[48,512]{1,0:T(8,128)(2,1)S(1)} %get-tuple-element.86), channel_id=1, source_target_pairs={{0,16},{8,24},{16,0},{24,8},{1,17},{9,25},{17,1},{25,9},{2,18},{10... | collective-permute-start | bytes 147464 | tf_op jit(solution)/shard_map/ppermute | solution.py:17
  49.8 0.5 collective-permute-start.24
  50.7 3.6 %collective-permute-start.26 = (bf16[64,512]{1,0:T(8,128)(2,1)S(1)}, bf16[64,512]{1,0:T(8,128)(2,1)S(1)}, u32[]{:S(2)}, u32[]{:S(2)}) collective-permute-start(bf16[64,512]{1,0:T(8,128)(2,1)S(1)} %get-tuple-element.106), channel_id=1, source_target_pairs={{0,24},{8,16},{16,8},{24,0},{1,25},{9,17},{17,9},{25,1},{2,26},{10... | collective-permute-start | bytes 196616 | tf_op jit(solution)/shard_map/ppermute | solution.py:17
  54.3 0.8 %shard_map.143 = f32[128,1024]{1,0:T(8,128)} custom-call(f32[128,1024]{1,0:T(8,128)S(1)} %get-tuple-element.107.own_ref, f32[128,1024]{1,0:T(8,128)S(1)} %collective-permute-done.27.got_ref), custom_call_target="tpu_custom_call" | custom-call | flops 1073741824 | bytes 1048576 | tf_op jit(solution)/shard_map/pallas_call | solution.py:60
  55.1 0.7 collective-permute-start.12
  55.8 3.4 %collective-permute-done.25.refs_2_ = bf16[64,512]{1,0:T(8,128)(2,1)S(1)} collective-permute-done((bf16[64,512]{1,0:T(8,128)(2,1)S(1)}, bf16[64,512]{1,0:T(8,128)(2,1)S(1)}, u32[]{:S(2)}, u32[]{:S(2)}) %collective-permute-start.25) | collective-permute-done | bytes 65568 | tf_op jit(solution)/shard_map/ppermute | solution.py:17
  59.2 1.5 %collective-permute-start.30 = (bf16[64,512]{1,0:T(8,128)(2,1)S(1)}, bf16[64,512]{1,0:T(8,128)(2,1)S(1)}, u32[]{:S(2)}, u32[]{:S(2)}) collective-permute-start(bf16[64,512]{1,0:T(8,128)(2,1)S(1)} %shard_map.144.refs_0_), channel_id=1, source_target_pairs={{0,24},{8,16},{16,8},{24,0},{1,25},{9,17},{17,9},{25,1},{2,26},{10... | collective-permute-start | bytes 196616 | tf_op jit(solution)/shard_map/ppermute | solution.py:17
  60.7 1.4 %collective-permute-start.29 = (bf16[64,512]{1,0:T(8,128)(2,1)S(1)}, bf16[64,512]{1,0:T(8,128)(2,1)S(1)}, u32[]{:S(2)}, u32[]{:S(2)}) collective-permute-start(bf16[64,512]{1,0:T(8,128)(2,1)S(1)} %shard_map.144.refs_0_), channel_id=1, source_target_pairs={{0,16},{8,24},{16,0},{24,8},{1,17},{9,25},{17,1},{25,9},{2,18},{10... | collective-permute-start | bytes 196616 | tf_op jit(solution)/shard_map/ppermute | solution.py:17
  62.1 1.5 %collective-permute-start.28 = (bf16[64,512]{1,0:T(8,128)(2,1)S(1)}, bf16[64,512]{1,0:T(8,128)(2,1)S(1)}, u32[]{:S(2)}, u32[]{:S(2)}) collective-permute-start(bf16[64,512]{1,0:T(8,128)(2,1)S(1)} %shard_map.144.refs_0_), channel_id=1, source_target_pairs={{0,8},{8,0},{16,24},{24,16},{1,9},{9,1},{17,25},{25,17},{2,10},{10... | collective-permute-start | bytes 196616 | tf_op jit(solution)/shard_map/ppermute | solution.py:17
  63.7 2.2 %collective-permute-start.15 = (bf16[48,512]{1,0:T(8,128)(2,1)S(1)}, bf16[48,512]{1,0:T(8,128)(2,1)S(1)}, u32[]{:S(2)}, u32[]{:S(2)}) collective-permute-start(bf16[48,512]{1,0:T(8,128)(2,1)S(1)} %shard_map.136.refs_0_), channel_id=1, source_target_pairs={{0,5},{1,4},{4,1},{5,0},{2,7},{3,6},{6,3},{7,2},{8,13},{9,12},{12,... | collective-permute-start | bytes 147464 | tf_op jit(solution)/shard_map/ppermute | solution.py:17
  66.0 0.5 collective-permute-start.14
  66.5 0.8 collective-permute-start.13
  67.3 1.6 %collective-permute-start.32 = (bf16[4,64,512]{2,1,0:T(8,128)(2,1)S(1)}, bf16[4,64,512]{2,1,0:T(8,128)(2,1)S(1)}, u32[]{:S(2)}, u32[]{:S(2)}) collective-permute-start(bf16[4,64,512]{2,1,0:T(8,128)(2,1)S(1)} %shard_map.145.both_ref), channel_id=1, source_target_pairs={{0,4},{4,0},{1,5},{5,1},{2,6},{6,2},{3,7},{7,3},{8,12},{12,8},{9,1... | collective-permute-start | bytes 786440 | tf_op jit(solution)/shard_map/ppermute | solution.py:17
  69.3 0.9 %collective-permute-done.14.refs_2_ = bf16[48,512]{1,0:T(8,128)(2,1)S(1)} collective-permute-done((bf16[48,512]{1,0:T(8,128)(2,1)S(1)}, bf16[48,512]{1,0:T(8,128)(2,1)S(1)}, u32[]{:S(2)}, u32[]{:S(2)}) %collective-permute-start.14) | collective-permute-done | bytes 49184 | tf_op jit(solution)/shard_map/ppermute | solution.py:17
  70.6 0.6 shard_map.137
  71.2 1.4 %collective-permute-start.18 = (bf16[32,512]{1,0:T(8,128)(2,1)S(1)}, bf16[32,512]{1,0:T(8,128)(2,1)S(1)}, u32[]{:S(2)}, u32[]{:S(2)}) collective-permute-start(bf16[32,512]{1,0:T(8,128)(2,1)S(1)} %get-tuple-element.88.refs_0_), channel_id=1, source_target_pairs={{0,24},{8,16},{16,8},{24,0},{1,25},{9,17},{17,9},{25,1},{2,26},{10... | collective-permute-start | bytes 98312 | tf_op jit(solution)/shard_map/ppermute | solution.py:17
  72.6 0.5 collective-permute-start.17
  73.1 2.5 %collective-permute-start.16 = (bf16[32,512]{1,0:T(8,128)(2,1)S(1)}, bf16[32,512]{1,0:T(8,128)(2,1)S(1)}, u32[]{:S(2)}, u32[]{:S(2)}) collective-permute-start(bf16[32,512]{1,0:T(8,128)(2,1)S(1)} %get-tuple-element.88.refs_0_), channel_id=1, source_target_pairs={{0,8},{8,0},{16,24},{24,16},{1,9},{9,1},{17,25},{25,17},{2,10},{10... | collective-permute-start | bytes 98312 | tf_op jit(solution)/shard_map/ppermute | solution.py:17
  75.6 1.3 %collective-permute-done.18.refs_3_ = bf16[32,512]{1,0:T(8,128)(2,1)S(1)} collective-permute-done((bf16[32,512]{1,0:T(8,128)(2,1)S(1)}, bf16[32,512]{1,0:T(8,128)(2,1)S(1)}, u32[]{:S(2)}, u32[]{:S(2)}) %collective-permute-start.18) | collective-permute-done | bytes 32800 | tf_op jit(solution)/shard_map/ppermute | solution.py:17
  76.9 0.9 %collective-permute-done.17.refs_2_ = bf16[32,512]{1,0:T(8,128)(2,1)S(1)} collective-permute-done((bf16[32,512]{1,0:T(8,128)(2,1)S(1)}, bf16[32,512]{1,0:T(8,128)(2,1)S(1)}, u32[]{:S(2)}, u32[]{:S(2)}) %collective-permute-start.17) | collective-permute-done | bytes 32800 | tf_op jit(solution)/shard_map/ppermute | solution.py:17
  78.4 0.8 %collective-permute-done.19.core_ref = bf16[4,32,512]{2,1,0:T(8,128)(2,1)S(1)} collective-permute-done((bf16[4,32,512]{2,1,0:T(8,128)(2,1)S(1)}, bf16[4,32,512]{2,1,0:T(8,128)(2,1)S(1)}, u32[]{:S(2)}, u32[]{:S(2)}) %collective-permute-start.19) | collective-permute-done | bytes 131104 | tf_op jit(solution)/shard_map/ppermute | solution.py:17
  79.2 0.8 %shard_map.139 = f32[128,1024]{1,0:T(8,128)} custom-call(bf16[4,32,512]{2,1,0:T(8,128)(2,1)S(1)} %shard_map.138.own_ref, bf16[4,32,512]{2,1,0:T(8,128)(2,1)S(1)} %collective-permute-done.19.core_ref), custom_call_target="tpu_custom_call" | custom-call | flops 1073741824 | bytes 1048576 | tf_op jit(solution)/shard_map/pallas_call | solution.py:60
  80.0 1.0 %shard_map.146.held_ref = f32[1024,512]{1,0:T(8,128)} custom-call(bf16[4,64,512]{2,1,0:T(8,128)(2,1)S(1)} %shard_map.145.both_ref, bf16[4,64,512]{2,1,0:T(8,128)(2,1)S(1)} %collective-permute-done.31.core_ref), custom_call_target="tpu_custom_call" | custom-call | flops 1073741824 | bytes 1048576 | tf_op jit(solution)/shard_map/pallas_call | solution.py:60
  81.1 1.0 %shard_map.147 = f32[1024,512]{1,0:T(8,128)} custom-call(f32[1024,512]{1,0:T(8,128)} %shard_map.146.held_ref, bf16[4,64,512]{2,1,0:T(8,128)(2,1)S(1)} %collective-permute-done.32.across_ref, bf16[4,64,512]{2,1,0:T(8,128)(2,1)S(1)} %collective-permute-done.33.core_ref), custom_call_target="tpu_custom_call", output_to_operand_aliasing={{}: (0, {})} | custom-call | flops 1073741824 | bytes 1048576 | tf_op jit(solution)/shard_map/pallas_call | solution.py:60
  (59 shorter events, 3.9 us)
Async XLA Ops:
  1.6 6.9 %copy-start.1 = (bf16[1024,512]{1,0:T(8,128)(2,1)S(1)}, bf16[1024,512]{1,0:T(8,128)(2,1)}, u32[]{:S(2)}) copy-start(bf16[1024,512]{1,0:T(8,128)(2,1)} %half_ref.3) | copy-start | bytes 3145732
  1.6 6.9 %copy-start.2 = (bf16[512]{0:T(512)(128)(2,1)S(1)}, bf16[512]{0:T(512)(128)(2,1)}, u32[]{:S(2)}) copy-start(bf16[512]{0:T(512)(128)(2,1)} %bias_ref.5) | copy-start | bytes 3076
  1.6 7.2 %copy-start = (bf16[128,1024]{1,0:T(8,128)(2,1)S(1)}, bf16[128,1024]{1,0:T(8,128)(2,1)}, u32[]{:S(2)}) copy-start(bf16[128,1024]{1,0:T(8,128)(2,1)} %weight_ref.5) | copy-start | bytes 786436
  1.6 9.7 %collective-permute-start = (bf16[128,512]{1,0:T(8,128)(2,1)S(1)}, bf16[128,512]{1,0:T(8,128)(2,1)S(1)}, u32[]{:S(2)}, u32[]{:S(2)}) collective-permute-start(bf16[128,512]{1,0:T(8,128)(2,1)S(1)} %constant_dynamic-slice_fusion), channel_id=1, source_target_pairs={{0,1},{1,0},{2,3},{3,2},{4,5},{5,4},{6,7},{7,6},{8,9},{9,8},{10,11... | collective-permute-start | bytes 393224 | tf_op jit(solution)/shard_map/ppermute | solution.py:17
  4.7 8.7 %collective-permute-start.3 = (bf16[128,1024]{1,0:T(8,128)(2,1)}, bf16[128,1024]{1,0:T(8,128)(2,1)S(1)}, u32[]{:S(2)}, u32[]{:S(2)}) collective-permute-start(bf16[128,1024]{1,0:T(8,128)(2,1)} %dec_ref.1), channel_id=1, source_target_pairs={{0,2},{2,0},{1,3},{3,1},{4,6},{6,4},{5,7},{7,5},{8,10},{10,8},{9,1... | collective-permute-start | bytes 786440 | tf_op jit(solution)/shard_map/ppermute | solution.py:17
  7.9 5.4 %collective-permute-start.4 = (bf16[9,128,128]{2,1,0:T(8,128)(2,1)}, bf16[9,128,128]{2,1,0:T(8,128)(2,1)S(1)}, u32[]{:S(2)}, u32[]{:S(2)}) collective-permute-start(bf16[9,128,128]{2,1,0:T(8,128)(2,1)} %get-tuple-element.65), channel_id=1, source_target_pairs={{0,2},{2,0},{1,3},{3,1},{4,6},{6,4},{5,7},{7,5},{8,10},{10,8},{9,1... | collective-permute-start | bytes 884744 | tf_op jit(solution)/shard_map/ppermute | solution.py:17
  8.6 8.7 %collective-permute-start.1 = (bf16[272,512]{1,0:T(8,128)(2,1)S(1)}, bf16[272,512]{1,0:T(8,128)(2,1)S(1)}, u32[]{:S(2)}, u32[]{:S(2)}) collective-permute-start(bf16[272,512]{1,0:T(8,128)(2,1)S(1)} %dynamic-slice_select_fusion), channel_id=1, source_target_pairs={{0,1},{1,0},{2,3},{3,2},{4,5},{5,4},{6,7},{7,6},{8,9},{9,8},{10,11... | collective-permute-start | bytes 835592 | tf_op jit(solution)/shard_map/ppermute | solution.py:17
  8.7 0.8 copy-start.6
  9.5 3.8 %copy-start.3 = (bf16[9,128,128]{2,1,0:T(8,128)(2,1)S(1)}, bf16[9,128,128]{2,1,0:T(8,128)(2,1)}, u32[]{:S(2)}) copy-start(bf16[9,128,128]{2,1,0:T(8,128)(2,1)} %get-tuple-element.64.jac_ref) | copy-start | bytes 884740
  9.5 3.8 %copy-start.4 = (bf16[128,1024]{1,0:T(8,128)(2,1)S(1)}, bf16[128,1024]{1,0:T(8,128)(2,1)}, u32[]{:S(2)}) copy-start(bf16[128,1024]{1,0:T(8,128)(2,1)} %dec_ref.1) | copy-start | bytes 786436
  11.3 5.4 %collective-permute-start.2 = (bf16[128,512]{1,0:T(8,128)(2,1)S(1)}, bf16[128,512]{1,0:T(8,128)(2,1)S(1)}, u32[]{:S(2)}, u32[]{:S(2)}) collective-permute-start(bf16[128,512]{1,0:T(8,128)(2,1)S(1)} %collective-permute-done.near_ref), channel_id=1, source_target_pairs={{0,4},{4,0},{1,5},{5,1},{2,6},{6,2},{3,7},{7,3},{8,12},{12,8},{9,1... | collective-permute-start | bytes 393224 | tf_op jit(solution)/shard_map/ppermute | solution.py:17
  17.3 1.9 %collective-permute-start.7 = (bf16[272,512]{1,0:T(8,128)(2,1)S(1)}, bf16[272,512]{1,0:T(8,128)(2,1)S(1)}, u32[]{:S(2)}, u32[]{:S(2)}) collective-permute-start(bf16[272,512]{1,0:T(8,128)(2,1)S(1)} %collective-permute-done.1.rest_ref), channel_id=1, source_target_pairs={{0,2},{2,0},{1,3},{3,1},{4,6},{6,4},{5,7},{7,5},{8,10},{10,8},{9,1... | collective-permute-start | bytes 835592 | tf_op jit(solution)/shard_map/ppermute | solution.py:17
  17.3 1.7 %collective-permute-start.5 = (bf16[128,512]{1,0:T(8,128)(2,1)S(1)}, bf16[128,512]{1,0:T(8,128)(2,1)S(1)}, u32[]{:S(2)}, u32[]{:S(2)}) collective-permute-start(bf16[128,512]{1,0:T(8,128)(2,1)S(1)} %collective-permute-done.near_ref), channel_id=1, source_target_pairs={{0,2},{2,0},{1,3},{3,1},{4,6},{6,4},{5,7},{7,5},{8,10},{10,8},{9,1... | collective-permute-start | bytes 393224 | tf_op jit(solution)/shard_map/ppermute | solution.py:17
  17.8 1.4 %collective-permute-start.6 = (bf16[128,512]{1,0:T(8,128)(2,1)S(1)}, bf16[128,512]{1,0:T(8,128)(2,1)S(1)}, u32[]{:S(2)}, u32[]{:S(2)}) collective-permute-start(bf16[128,512]{1,0:T(8,128)(2,1)S(1)} %collective-permute-done.2.far_ref), channel_id=1, source_target_pairs={{0,2},{2,0},{1,3},{3,1},{4,6},{6,4},{5,7},{7,5},{8,10},{10,8},{9,1... | collective-permute-start | bytes 393224 | tf_op jit(solution)/shard_map/ppermute | solution.py:17
  22.9 2.2 %collective-permute-start.20 = (bf16[512,512]{1,0:T(8,128)(2,1)S(1)}, bf16[512,512]{1,0:T(8,128)(2,1)S(1)}, u32[]{:S(2)}, u32[]{:S(2)}) collective-permute-start(bf16[512,512]{1,0:T(8,128)(2,1)S(1)} %get-tuple-element.91), channel_id=1, source_target_pairs={{0,2},{2,0},{1,3},{3,1},{4,6},{6,4},{5,7},{7,5},{8,10},{10,8},{9,1... | collective-permute-start | bytes 1572872 | tf_op jit(solution)/shard_map/ppermute | solution.py:17
  24.7 3.6 %collective-permute-start.8 = (bf16[512,512]{1,0:T(8,128)(2,1)S(1)}, bf16[512,512]{1,0:T(8,128)(2,1)S(1)}, u32[]{:S(2)}, u32[]{:S(2)}) collective-permute-start(bf16[512,512]{1,0:T(8,128)(2,1)S(1)} %get-tuple-element.75), channel_id=1, source_target_pairs={{0,2},{2,0},{1,3},{3,1},{4,6},{6,4},{5,7},{7,5},{8,10},{10,8},{9,1... | collective-permute-start | bytes 1572872 | tf_op jit(solution)/shard_map/ppermute | solution.py:17
  25.2 14.0 %collective-permute-start.21 = (bf16[256,512]{1,0:T(8,128)(2,1)S(1)}, bf16[256,512]{1,0:T(8,128)(2,1)S(1)}, u32[]{:S(2)}, u32[]{:S(2)}) collective-permute-start(bf16[256,512]{1,0:T(8,128)(2,1)S(1)} %get-tuple-element.92), channel_id=1, source_target_pairs={{0,1},{1,0},{4,5},{5,4},{2,3},{3,2},{6,7},{7,6},{8,9},{9,8},{12,13... | collective-permute-start | bytes 786440 | tf_op jit(solution)/shard_map/ppermute | solution.py:17
  26.5 12.7 %collective-permute-start.23 = (bf16[256,512]{1,0:T(8,128)(2,1)S(1)}, bf16[256,512]{1,0:T(8,128)(2,1)S(1)}, u32[]{:S(2)}, u32[]{:S(2)}) collective-permute-start(bf16[256,512]{1,0:T(8,128)(2,1)S(1)} %get-tuple-element.94), channel_id=1, source_target_pairs={{0,5},{1,4},{4,1},{5,0},{2,7},{3,6},{6,3},{7,2},{8,13},{9,12},{12,... | collective-permute-start | bytes 786440 | tf_op jit(solution)/shard_map/ppermute | solution.py:17
  29.3 11.2 %copy-start.5 = (f32[128,128]{1,0:T(8,128)S(1)}, f32[128,128]{1,0:T(8,128)}, u32[]{:S(2)}) copy-start(f32[128,128]{1,0:T(8,128)} %get-tuple-element.79.turned_ref) | copy-start | bytes 196612
  29.3 11.2 %copy-start.7 = (f32[8,1024]{1,0:T(8,128)S(1)}, f32[8,1024]{1,0:T(8,128)}, u32[]{:S(2)}) copy-start(f32[8,1024]{1,0:T(8,128)} %get-tuple-element.60.act_ref) | copy-start | bytes 98308
  29.3 11.2 %collective-permute-start.22 = (bf16[256,512]{1,0:T(8,128)(2,1)S(1)}, bf16[256,512]{1,0:T(8,128)(2,1)S(1)}, u32[]{:S(2)}, u32[]{:S(2)}) collective-permute-start(bf16[256,512]{1,0:T(8,128)(2,1)S(1)} %get-tuple-element.93), channel_id=1, source_target_pairs={{0,4},{1,5},{4,0},{5,1},{2,6},{3,7},{6,2},{7,3},{8,12},{9,13},{12,... | collective-permute-start | bytes 786440 | tf_op jit(solution)/shard_map/ppermute | solution.py:17
  40.5 10.2 %collective-permute-start.27 = (f32[128,1024]{1,0:T(8,128)S(1)}, f32[128,1024]{1,0:T(8,128)S(1)}, u32[]{:S(2)}, u32[]{:S(2)}) collective-permute-start(f32[128,1024]{1,0:T(8,128)S(1)} %get-tuple-element.108), channel_id=1, source_target_pairs={{0,2},{2,0},{1,3},{3,1},{4,6},{6,4},{5,7},{7,5},{8,10},{10,8},{9,1... | collective-permute-start | bytes 1572872 | tf_op jit(solution)/shard_map/ppermute | solution.py:17
  43.7 1.6 %collective-permute-start.9 = (bf16[144,512]{1,0:T(8,128)(2,1)S(1)}, bf16[144,512]{1,0:T(8,128)(2,1)S(1)}, u32[]{:S(2)}, u32[]{:S(2)}) collective-permute-start(bf16[144,512]{1,0:T(8,128)(2,1)S(1)} %get-tuple-element.82), channel_id=1, source_target_pairs={{0,2},{2,0},{1,3},{3,1},{4,6},{6,4},{5,7},{7,5},{8,10},{10,8},{9,1... | collective-permute-start | bytes 442376 | tf_op jit(solution)/shard_map/ppermute | solution.py:17
  45.3 16.8 %collective-permute-start.10 = (bf16[48,512]{1,0:T(8,128)(2,1)S(1)}, bf16[48,512]{1,0:T(8,128)(2,1)S(1)}, u32[]{:S(2)}, u32[]{:S(2)}) collective-permute-start(bf16[48,512]{1,0:T(8,128)(2,1)S(1)} %get-tuple-element.85), channel_id=1, source_target_pairs={{0,8},{8,0},{16,24},{24,16},{1,9},{9,1},{17,25},{25,17},{2,10},{10... | collective-permute-start | bytes 147464 | tf_op jit(solution)/shard_map/ppermute | solution.py:17
  46.9 16.7 %collective-permute-start.11 = (bf16[48,512]{1,0:T(8,128)(2,1)S(1)}, bf16[48,512]{1,0:T(8,128)(2,1)S(1)}, u32[]{:S(2)}, u32[]{:S(2)}) collective-permute-start(bf16[48,512]{1,0:T(8,128)(2,1)S(1)} %get-tuple-element.86), channel_id=1, source_target_pairs={{0,16},{8,24},{16,0},{24,8},{1,17},{9,25},{17,1},{25,9},{2,18},{10... | collective-permute-start | bytes 147464 | tf_op jit(solution)/shard_map/ppermute | solution.py:17
  49.8 5.3 %collective-permute-start.24 = (bf16[64,512]{1,0:T(8,128)(2,1)S(1)}, bf16[64,512]{1,0:T(8,128)(2,1)S(1)}, u32[]{:S(2)}, u32[]{:S(2)}) collective-permute-start(bf16[64,512]{1,0:T(8,128)(2,1)S(1)} %get-tuple-element.104), channel_id=1, source_target_pairs={{0,8},{8,0},{16,24},{24,16},{1,9},{9,1},{17,25},{25,17},{2,10},{10... | collective-permute-start | bytes 196616 | tf_op jit(solution)/shard_map/ppermute | solution.py:17
  50.3 8.9 %collective-permute-start.25 = (bf16[64,512]{1,0:T(8,128)(2,1)S(1)}, bf16[64,512]{1,0:T(8,128)(2,1)S(1)}, u32[]{:S(2)}, u32[]{:S(2)}) collective-permute-start(bf16[64,512]{1,0:T(8,128)(2,1)S(1)} %get-tuple-element.105), channel_id=1, source_target_pairs={{0,16},{8,24},{16,0},{24,8},{1,17},{9,25},{17,1},{25,9},{2,18},{10... | collective-permute-start | bytes 196616 | tf_op jit(solution)/shard_map/ppermute | solution.py:17
  50.7 8.5 %collective-permute-start.26 = (bf16[64,512]{1,0:T(8,128)(2,1)S(1)}, bf16[64,512]{1,0:T(8,128)(2,1)S(1)}, u32[]{:S(2)}, u32[]{:S(2)}) collective-permute-start(bf16[64,512]{1,0:T(8,128)(2,1)S(1)} %get-tuple-element.106), channel_id=1, source_target_pairs={{0,24},{8,16},{16,8},{24,0},{1,25},{9,17},{17,9},{25,1},{2,26},{10... | collective-permute-start | bytes 196616 | tf_op jit(solution)/shard_map/ppermute | solution.py:17
  55.1 8.6 %collective-permute-start.12 = (bf16[48,512]{1,0:T(8,128)(2,1)S(1)}, bf16[48,512]{1,0:T(8,128)(2,1)S(1)}, u32[]{:S(2)}, u32[]{:S(2)}) collective-permute-start(bf16[48,512]{1,0:T(8,128)(2,1)S(1)} %get-tuple-element.87), channel_id=1, source_target_pairs={{0,24},{8,16},{16,8},{24,0},{1,25},{9,17},{17,9},{25,1},{2,26},{10... | collective-permute-start | bytes 147464 | tf_op jit(solution)/shard_map/ppermute | solution.py:17
  59.2 7.3 %collective-permute-start.30 = (bf16[64,512]{1,0:T(8,128)(2,1)S(1)}, bf16[64,512]{1,0:T(8,128)(2,1)S(1)}, u32[]{:S(2)}, u32[]{:S(2)}) collective-permute-start(bf16[64,512]{1,0:T(8,128)(2,1)S(1)} %shard_map.144.refs_0_), channel_id=1, source_target_pairs={{0,24},{8,16},{16,8},{24,0},{1,25},{9,17},{17,9},{25,1},{2,26},{10... | collective-permute-start | bytes 196616 | tf_op jit(solution)/shard_map/ppermute | solution.py:17
  60.7 6.6 %collective-permute-start.29 = (bf16[64,512]{1,0:T(8,128)(2,1)S(1)}, bf16[64,512]{1,0:T(8,128)(2,1)S(1)}, u32[]{:S(2)}, u32[]{:S(2)}) collective-permute-start(bf16[64,512]{1,0:T(8,128)(2,1)S(1)} %shard_map.144.refs_0_), channel_id=1, source_target_pairs={{0,16},{8,24},{16,0},{24,8},{1,17},{9,25},{17,1},{25,9},{2,18},{10... | collective-permute-start | bytes 196616 | tf_op jit(solution)/shard_map/ppermute | solution.py:17
  62.1 5.1 %collective-permute-start.28 = (bf16[64,512]{1,0:T(8,128)(2,1)S(1)}, bf16[64,512]{1,0:T(8,128)(2,1)S(1)}, u32[]{:S(2)}, u32[]{:S(2)}) collective-permute-start(bf16[64,512]{1,0:T(8,128)(2,1)S(1)} %shard_map.144.refs_0_), channel_id=1, source_target_pairs={{0,8},{8,0},{16,24},{24,16},{1,9},{9,1},{17,25},{25,17},{2,10},{10... | collective-permute-start | bytes 196616 | tf_op jit(solution)/shard_map/ppermute | solution.py:17
  63.7 5.6 %collective-permute-start.15 = (bf16[48,512]{1,0:T(8,128)(2,1)S(1)}, bf16[48,512]{1,0:T(8,128)(2,1)S(1)}, u32[]{:S(2)}, u32[]{:S(2)}) collective-permute-start(bf16[48,512]{1,0:T(8,128)(2,1)S(1)} %shard_map.136.refs_0_), channel_id=1, source_target_pairs={{0,5},{1,4},{4,1},{5,0},{2,7},{3,6},{6,3},{7,2},{8,13},{9,12},{12,... | collective-permute-start | bytes 147464 | tf_op jit(solution)/shard_map/ppermute | solution.py:17
  66.0 4.3 %collective-permute-start.14 = (bf16[48,512]{1,0:T(8,128)(2,1)S(1)}, bf16[48,512]{1,0:T(8,128)(2,1)S(1)}, u32[]{:S(2)}, u32[]{:S(2)}) collective-permute-start(bf16[48,512]{1,0:T(8,128)(2,1)S(1)} %shard_map.136.refs_0_), channel_id=1, source_target_pairs={{0,4},{1,5},{4,0},{5,1},{2,6},{3,7},{6,2},{7,3},{8,12},{9,13},{12,... | collective-permute-start | bytes 147464 | tf_op jit(solution)/shard_map/ppermute | solution.py:17
  66.5 4.1 %collective-permute-start.13 = (bf16[48,512]{1,0:T(8,128)(2,1)S(1)}, bf16[48,512]{1,0:T(8,128)(2,1)S(1)}, u32[]{:S(2)}, u32[]{:S(2)}) collective-permute-start(bf16[48,512]{1,0:T(8,128)(2,1)S(1)} %shard_map.136.refs_0_), channel_id=1, source_target_pairs={{0,1},{1,0},{4,5},{5,4},{2,3},{3,2},{6,7},{7,6},{8,9},{9,8},{12,13... | collective-permute-start | bytes 147464 | tf_op jit(solution)/shard_map/ppermute | solution.py:17
  67.3 10.6 %collective-permute-start.32 = (bf16[4,64,512]{2,1,0:T(8,128)(2,1)S(1)}, bf16[4,64,512]{2,1,0:T(8,128)(2,1)S(1)}, u32[]{:S(2)}, u32[]{:S(2)}) collective-permute-start(bf16[4,64,512]{2,1,0:T(8,128)(2,1)S(1)} %shard_map.145.both_ref), channel_id=1, source_target_pairs={{0,4},{4,0},{1,5},{5,1},{2,6},{6,2},{3,7},{7,3},{8,12},{12,8},{9,1... | collective-permute-start | bytes 786440 | tf_op jit(solution)/shard_map/ppermute | solution.py:17
  71.2 5.7 %collective-permute-start.18 = (bf16[32,512]{1,0:T(8,128)(2,1)S(1)}, bf16[32,512]{1,0:T(8,128)(2,1)S(1)}, u32[]{:S(2)}, u32[]{:S(2)}) collective-permute-start(bf16[32,512]{1,0:T(8,128)(2,1)S(1)} %get-tuple-element.88.refs_0_), channel_id=1, source_target_pairs={{0,24},{8,16},{16,8},{24,0},{1,25},{9,17},{17,9},{25,1},{2,26},{10... | collective-permute-start | bytes 98312 | tf_op jit(solution)/shard_map/ppermute | solution.py:17
  72.6 5.2 %collective-permute-start.17 = (bf16[32,512]{1,0:T(8,128)(2,1)S(1)}, bf16[32,512]{1,0:T(8,128)(2,1)S(1)}, u32[]{:S(2)}, u32[]{:S(2)}) collective-permute-start(bf16[32,512]{1,0:T(8,128)(2,1)S(1)} %get-tuple-element.88.refs_0_), channel_id=1, source_target_pairs={{0,16},{8,24},{16,0},{24,8},{1,17},{9,25},{17,1},{25,9},{2,18},{10... | collective-permute-start | bytes 98312 | tf_op jit(solution)/shard_map/ppermute | solution.py:17
  73.1 4.6 %collective-permute-start.16 = (bf16[32,512]{1,0:T(8,128)(2,1)S(1)}, bf16[32,512]{1,0:T(8,128)(2,1)S(1)}, u32[]{:S(2)}, u32[]{:S(2)}) collective-permute-start(bf16[32,512]{1,0:T(8,128)(2,1)S(1)} %get-tuple-element.88.refs_0_), channel_id=1, source_target_pairs={{0,8},{8,0},{16,24},{24,16},{1,9},{9,1},{17,25},{25,17},{2,10},{10... | collective-permute-start | bytes 98312 | tf_op jit(solution)/shard_map/ppermute | solution.py:17
  75.6 4.5 %collective-permute-start.31 = (bf16[4,64,512]{2,1,0:T(8,128)(2,1)S(1)}, bf16[4,64,512]{2,1,0:T(8,128)(2,1)S(1)}, u32[]{:S(2)}, u32[]{:S(2)}) collective-permute-start(bf16[4,64,512]{2,1,0:T(8,128)(2,1)S(1)} %shard_map.145.both_ref), channel_id=1, source_target_pairs={{0,2},{2,0},{1,3},{3,1},{4,6},{6,4},{5,7},{7,5},{8,10},{10,8},{9,1... | collective-permute-start | bytes 786440 | tf_op jit(solution)/shard_map/ppermute | solution.py:17
  77.8 1.4 %collective-permute-start.19 = (bf16[4,32,512]{2,1,0:T(8,128)(2,1)S(1)}, bf16[4,32,512]{2,1,0:T(8,128)(2,1)S(1)}, u32[]{:S(2)}, u32[]{:S(2)}) collective-permute-start(bf16[4,32,512]{2,1,0:T(8,128)(2,1)S(1)} %shard_map.138.own_ref), channel_id=1, source_target_pairs={{0,2},{2,0},{1,3},{3,1},{4,6},{6,4},{5,7},{7,5},{8,10},{10,8},{9,1... | collective-permute-start | bytes 393224 | tf_op jit(solution)/shard_map/ppermute | solution.py:17
  77.9 3.2 %collective-permute-start.33 = (bf16[4,64,512]{2,1,0:T(8,128)(2,1)S(1)}, bf16[4,64,512]{2,1,0:T(8,128)(2,1)S(1)}, u32[]{:S(2)}, u32[]{:S(2)}) collective-permute-start(bf16[4,64,512]{2,1,0:T(8,128)(2,1)S(1)} %collective-permute-done.32.across_ref), channel_id=1, source_target_pairs={{0,2},{2,0},{1,3},{3,1},{4,6},{6,4},{5,7},{7,5},{8,10},{10,8},{9,1... | collective-permute-start | bytes 786440 | tf_op jit(solution)/shard_map/ppermute | solution.py:17

commit v2 on v1

--- a/solution.py
+++ b/solution.py
@@ -93,7 +93,7 @@
         hrow_c, frow_c = hidden // nc, rank // nc
         hrow_x = hrow_c // nx
         hrow_z, frow_z = hrow_x // nz, frow_c // nz
-        brow = 16
+        brow, lead = 8, 16
 
         def swaps(values, axes, size):
             moved = [values[0]]
@@ -105,15 +105,21 @@
         near_rows = shared // nx
         c, x = lax.axis_index("c"), lax.axis_index("x")
         near = lax.dynamic_slice_in_dim(hidden_weight, c * hrow_c + x * near_rows, near_rows)
+
+        def hand_on(in_ref, out_ref):
+            out_ref[...] = in_ref[...]
+
+        (near,) = local_call(hand_on, [((near_rows, kw), BF16)], (near,), cost=20, limit=4 << 20)
         rest = lax.dynamic_slice_in_dim(
-            hidden_weight, c * hrow_c + shared - brow, hrow_c - shared + brow
+            hidden_weight, c * hrow_c + shared - lead, hrow_c - shared + lead
         )
         line = lax.broadcasted_iota(jnp.int32, rest.shape, 0)
-        rest = jnp.where(line < brow, hidden_bias[None, :], rest)
+        rest = jnp.where(line < lead, hidden_bias[None, :], rest)
         _, near_got = swaps([near] * ny, "y", ny)
         _, rest_got = swaps([rest] * ny, "y", ny)
         _, decoder_got = swaps([decoder_weight] * nc, "c", nc)
         _, far_got = swaps([near_got] * nx, "x", nx)
+        _, near_core = swaps([near_got] * nc, "c", nc)
 
         def gather(
             window_ref, jac_ref, target_ref, input_ref, weight_ref, bias_ref,
@@ -159,7 +165,7 @@
             cost=4,
             specs=[SMEM, ANY, VMEM, VMEM, VMEM, VMEM],
             scratch=[pltpu.SemaphoreType.DMA((nc, count))],
-            limit=60 << 20,
+            limit=50 << 20,
         )
         _, jac_got = swaps([jac_away] * nc, "c", nc)
 
@@ -226,11 +232,9 @@
             cost=1.5,
             limit=16 << 20,
         )
-        near_got, rest_got, far_got, tan_own = lax.optimization_barrier(
-            (near_got, rest_got, far_got, tan_own)
-        )
-        fetched = (near_got, far_got, rest_got)
-        fetched += tuple(swap(value, "c", nc, 1) for value in fetched)
+        rest_got, far_got, tan_own = lax.optimization_barrier((rest_got, far_got, tan_own))
+        fetched = (near_got, far_got, rest_got, near_core)
+        fetched += tuple(swap(value, "c", nc, 1) for value in (far_got, rest_got))
 
         def main(
             tan1_ref, side_ref, lin_ref, near_ref, far_ref, rest_ref, near2_ref, far2_ref, rest2_ref,
@@ -245,9 +249,9 @@
                     start = pl.multiple_of(base + (mx ^ a) * near_rows, near_rows)
                     half_ref[pl.ds(start, near_rows)] = refs[a][...]
                 start = pl.multiple_of(base + shared, shared)
-                half_ref[pl.ds(start, hrow_c - shared)] = refs[2][brow:]
+                half_ref[pl.ds(start, hrow_c - shared)] = refs[2][lead:]
             lin_got_ref[...] = jnp.dot(tan1_ref[...], half_ref[...], preferred_element_type=F32)
-            bias_got = rest_ref[:brow].astype(F32)[:1]
+            bias_got = rest_ref[:lead].astype(F32)[:1]
             own, other = hidden_slopes(lin_ref, hidden_row(bias_ref)), hidden_slopes(lin_got_ref, bias_got)
             hidden_tangents(lin_got_ref, *other, tan_ref)
             net = net_own_ref[...] + dot(wide_ref[:, kw:], tan_ref[...], ((1,), (1,)))
@@ -480,7 +484,7 @@
         _, across = swaps([both] * nx, "x", nx)
         _, both_core = swaps([both] * nc, "c", nc)
         _, first_core = swaps([first] * nc, "c", nc)
-        across_core = swap(across, "c", nc, 1)
+        _, across_core = swaps([across] * nc, "c", nc)
 
         def put(refs, base, size, out_ref, stage_ref, sem_ref, slot):
             copies = []

time: 82.5 us -> 80.6 us (0.977)
  Pallas kernels: 20.9 us -> 19.6 us
    pallas_call x20 -> x21, Pallas kernels: 20.9 us -> 19.6 us  [kernel_call(): pl.pallas_call(body, out_shape=[jax.ShapeDtypeStruct(shape, kind) for sha...]
  transfers between devices with their start and end apart: 34 -> 34, of which waited for: 14 -> 15; matrix products, arithmetic and copies ran while one was open for 0% -> 0% of each run, Pallas kernels for 20% -> 18%
where the time goes in v2:
time: 80.6 us; the launch traced here: 80.4 us
  starting transfers between devices  35.1 us (44%)
  waiting for transfers between devices  23.7 us (29%)
  Pallas kernels  19.6 us (24%)
  local copies, waits for them, and re-layouts  0.97 us (1%)
  between operations  0.92 us (1%)
    ppermute x34, starting transfers between devices, swap(): return lax.ppermute(value, axes, [(j, j ^ step) for j in range(size)])  35.1 us
    ppermute x34, waiting for transfers between devices, swap(): return lax.ppermute(value, axes, [(j, j ^ step) for j in range(size)])  23.7 us
    pallas_call x21, Pallas kernels, kernel_call(): pl.pallas_call(body, out_shape=[jax.ShapeDtypeStruct(shape, kind) for sha...  19.6 us
  transfers between devices with their start and end apart: 34, of which 15 were waited for; matrix products, arithmetic and copies ran while one was open for 0% of the time, Pallas kernels for 18%

profile of v2, /device:TPU:0, one launch (start us, length us, event | category | flops | bytes accessed | tf_op | source)
XLA Modules:
  0.0 80.4 jit_solution(15017237541326570920)
XLA Ops:
  0.6 0.9 %constant_dynamic-slice_fusion.in_ref = bf16[128,512]{1,0:T(8,128)(2,1)S(1)} fusion(bf16[1024,512]{1,0:T(8,128)(2,1)} %half_ref.3, s32[]{:T(128)S(6)} %select_n.10), kind=kLoop, calls=%fused_computation.2 | loop fusion | bytes 262148 | tf_op jit(solution)/shard_map/dynamic_slice | solution.py:107
  1.7 3.1 %collective-permute-start = (bf16[128,512]{1,0:T(8,128)(2,1)S(1)}, bf16[128,512]{1,0:T(8,128)(2,1)S(1)}, u32[]{:S(2)}, u32[]{:S(2)}) collective-permute-start(bf16[128,512]{1,0:T(8,128)(2,1)S(1)} %shard_map.130), channel_id=1, source_target_pairs={{0,1},{1,0},{2,3},{3,2},{4,5},{5,4},{6,7},{7,6},{8,9},{9,8},{10,11... | collective-permute-start | bytes 393224 | tf_op jit(solution)/shard_map/ppermute | solution.py:17
  4.8 1.9 %shard_map.128 = (bf16[9,128,128]{2,1,0:T(8,128)(2,1)S(1)}, bf16[9,128,128]{2,1,0:T(8,128)(2,1)S(1)}, f32[8,1024]{1,0:T(8,128)S(1)}, f32[128,128]{1,0:T(8,128)S(1)}) custom-call(s32[16]{0:T(128)S(1)} %copy-done.6, bf16[512,128,128]{2,1,0:T(8,128)(2,1)} %jac_ref.1, bf16[512,128]{1,0:T(8,128)(2,1)S(1)} %copy-done.2, bf16[512,128]{1,0:T(8,128)(2,1)S(1)} %copy-done.3, ...), custom_call_target="tpu_custom_call" | custom-call | flops 4294967296 | bytes 1048576 | tf_op jit(solution)/shard_map/pallas_call | solution.py:60
  6.7 0.6 collective-permute-start.4
  7.4 0.8 %collective-permute-start.1 = (bf16[272,512]{1,0:T(8,128)(2,1)S(1)}, bf16[272,512]{1,0:T(8,128)(2,1)S(1)}, u32[]{:S(2)}, u32[]{:S(2)}) collective-permute-start(bf16[272,512]{1,0:T(8,128)(2,1)S(1)} %dynamic-slice_select_fusion), channel_id=1, source_target_pairs={{0,1},{1,0},{2,3},{3,2},{4,5},{5,4},{6,7},{7,6},{8,9},{9,8},{10,11... | collective-permute-start | bytes 835592 | tf_op jit(solution)/shard_map/ppermute | solution.py:17
  8.2 1.8 %shard_map.129 = (bf16[1152,1024]{1,0:T(8,128)(2,1)S(1)}, bf16[1024,1152]{1,0:T(8,128)(2,1)S(1)}, f32[1152,512]{1,0:T(8,128)S(1)}) custom-call(f32[8,1024]{1,0:T(8,128)S(1)} %get-tuple-element.59.act_ref, bf16[128,1024]{1,0:T(8,128)(2,1)S(1)} %copy-done, bf16[1024,512]{1,0:T(8,128)(2,1)S(1)} %copy-done.1), custom_call_target="tpu_custom_call" | custom-call | flops 2147483648 | bytes 1048576 | tf_op jit(solution)/shard_map/pallas_call | solution.py:60
  10.0 1.6 %collective-permute-start.2 = (bf16[128,512]{1,0:T(8,128)(2,1)S(1)}, bf16[128,512]{1,0:T(8,128)(2,1)S(1)}, u32[]{:S(2)}, u32[]{:S(2)}) collective-permute-start(bf16[128,512]{1,0:T(8,128)(2,1)S(1)} %collective-permute-done.near_ref), channel_id=1, source_target_pairs={{0,4},{4,0},{1,5},{5,1},{2,6},{6,2},{3,7},{7,3},{8,12},{12,8},{9,1... | collective-permute-start | bytes 393224 | tf_op jit(solution)/shard_map/ppermute | solution.py:17
  11.6 0.7 shard_map.131
  12.3 3.1 %collective-permute-done.2.far_ref = bf16[128,512]{1,0:T(8,128)(2,1)S(1)} collective-permute-done((bf16[128,512]{1,0:T(8,128)(2,1)S(1)}, bf16[128,512]{1,0:T(8,128)(2,1)S(1)}, u32[]{:S(2)}, u32[]{:S(2)}) %collective-permute-start.2) | collective-permute-done | bytes 131104 | tf_op jit(solution)/shard_map/ppermute | solution.py:17
  15.4 0.7 collective-permute-done.1.rest_ref
  16.0 0.5 collective-permute-start.5
  16.5 1.2 %collective-permute-done.5.near2_ref = bf16[128,512]{1,0:T(8,128)(2,1)S(1)} collective-permute-done((bf16[128,512]{1,0:T(8,128)(2,1)S(1)}, bf16[128,512]{1,0:T(8,128)(2,1)S(1)}, u32[]{:S(2)}, u32[]{:S(2)}) %collective-permute-start.5) | collective-permute-done | bytes 131104 | tf_op jit(solution)/shard_map/ppermute | solution.py:17
  18.0 3.7 %shard_map.132 = (bf16[1024,512]{1,0:T(8,128)(2,1)S(1)}, bf16[1152,512]{1,0:T(8,128)(2,1)S(1)}, bf16[256,1152]{1,0:T(8,128)(2,1)S(1)}, bf16[1152,1024]{1,0:T(8,1...) custom-call(bf16[1152,1024]{1,0:T(8,128)(2,1)S(1)} %get-tuple-element.60.tan1_ref, ...), custom_call_target="tpu_custom_call" | custom-call | flops 5368709120 | bytes 1048576 | tf_op jit(solution)/shard_map/pallas_call | solution.py:60
  21.9 1.5 %shard_map.133 = (f32[512,512]{1,0:T(8,128)S(1)}, bf16[512,512]{1,0:T(8,128)(2,1)S(1)}) custom-call(bf16[1024,1152]{1,0:T(8,128)(2,1)S(1)} %get-tuple-element.61.side_ref, bf16[1152,1024]{1,0:T(8,128)(2,1)S(1)} %get-tuple-element.75.round_ref), custom_call_target="tpu_custom_call" | custom-call | flops 1610612736 | bytes 1048576 | tf_op jit(solution)/shard_map/pallas_call | solution.py:60
  24.0 0.9 %collective-permute-start.21 = (bf16[256,512]{1,0:T(8,128)(2,1)S(1)}, bf16[256,512]{1,0:T(8,128)(2,1)S(1)}, u32[]{:S(2)}, u32[]{:S(2)}) collective-permute-start(bf16[256,512]{1,0:T(8,128)(2,1)S(1)} %get-tuple-element.90), channel_id=1, source_target_pairs={{0,1},{1,0},{4,5},{5,4},{2,3},{3,2},{6,7},{7,6},{8,9},{9,8},{12,13... | collective-permute-start | bytes 786440 | tf_op jit(solution)/shard_map/ppermute | solution.py:17
  24.9 2.1 %collective-permute-start.23 = (bf16[256,512]{1,0:T(8,128)(2,1)S(1)}, bf16[256,512]{1,0:T(8,128)(2,1)S(1)}, u32[]{:S(2)}, u32[]{:S(2)}) collective-permute-start(bf16[256,512]{1,0:T(8,128)(2,1)S(1)} %get-tuple-element.92), channel_id=1, source_target_pairs={{0,5},{1,4},{4,1},{5,0},{2,7},{3,6},{6,3},{7,2},{8,13},{9,12},{12,... | collective-permute-start | bytes 786440 | tf_op jit(solution)/shard_map/ppermute | solution.py:17
  27.0 1.0 %shard_map.134 = (bf16[256,512]{1,0:T(8,128)(2,1)S(1)}, bf16[256,512]{1,0:T(8,128)(2,1)S(1)}) custom-call(bf16[1024,1152]{1,0:T(8,128)(2,1)S(1)} %get-tuple-element.61.side_ref, bf16[1152,1024]{1,0:T(8,128)(2,1)S(1)} %get-tuple-element.75.round_ref, bf16[512,512]{1,0:T(8,128)(2,1)S(1)} %collective-permute-done.8.got_ref), custom_call_target="tpu_custom_call" | custom-call | flops 1073741824 | bytes 1048576 | tf_op jit(solution)/shard_map/pallas_call | solution.py:60
  28.0 0.6 collective-permute-start.22
  28.6 0.9 %shard_map.142 = (f32[128,1024]{1,0:T(8,128)S(1)}, f32[128,1024]{1,0:T(8,128)S(1)}) custom-call(bf16[256,1152]{1,0:T(8,128)(2,1)S(1)} %get-tuple-element.93.miss_ref, bf16[1152,512]{1,0:T(8,128)(2,1)S(1)} %get-tuple-element.94.tan_ref, bf16[1152,512]{1,0:T(8,128)(2,1)S(1)} %get-tuple-element.95.tan_got_ref), custom_call_target="tpu_custom_call" | custom-call | flops 1073741824 | bytes 1048576 | tf_op jit(solution)/shard_map/pallas_call | solution.py:60
  29.5 8.5 %collective-permute-done.21.refs_1_ = bf16[256,512]{1,0:T(8,128)(2,1)S(1)} collective-permute-done((bf16[256,512]{1,0:T(8,128)(2,1)S(1)}, bf16[256,512]{1,0:T(8,128)(2,1)S(1)}, u32[]{:S(2)}, u32[]{:S(2)}) %collective-permute-start.21) | collective-permute-done | bytes 262176 | tf_op jit(solution)/shard_map/ppermute | solution.py:17
  38.0 1.2 %collective-permute-done.22.refs_2_ = bf16[256,512]{1,0:T(8,128)(2,1)S(1)} collective-permute-done((bf16[256,512]{1,0:T(8,128)(2,1)S(1)}, bf16[256,512]{1,0:T(8,128)(2,1)S(1)}, u32[]{:S(2)}, u32[]{:S(2)}) %collective-permute-start.22) | collective-permute-done | bytes 262176 | tf_op jit(solution)/shard_map/ppermute | solution.py:17
  39.2 3.2 %shard_map.135 = (f32[64,1024]{1,0:T(8,128)S(1)}, bf16[136,512]{1,0:T(8,128)(2,1)S(1)}, bf16[8,512]{1,0:T(8,128)(2,1)S(1)}) custom-call(bf16[1152,1024]{1,0:T(8,128)(2,1)S(1)} %get-tuple-element.75.round_ref, bf16[1024,512]{1,0:T(8,128)(2,1)S(1)} %copy-done.1, bf16[1024,512]{1,0:T(8,128)(2,1)S(1)} %get-tuple-element.76.got_ref, ...), custom_call_target="tpu_custom_call" | custom-call | flops 3221225472 | bytes 1048576 | tf_op jit(solution)/shard_map/pallas_call | solution.py:60
  42.4 0.6 collective-permute-start.9
  43.0 1.0 %collective-permute-done.9.got_ref = bf16[136,512]{1,0:T(8,128)(2,1)S(1)} collective-permute-done((bf16[136,512]{1,0:T(8,128)(2,1)S(1)}, bf16[136,512]{1,0:T(8,128)(2,1)S(1)}, u32[]{:S(2)}, u32[]{:S(2)}) %collective-permute-start.9) | collective-permute-done | bytes 139296 | tf_op jit(solution)/shard_map/ppermute | solution.py:17
  44.0 1.6 %collective-permute-start.10 = (bf16[40,512]{1,0:T(8,128)(2,1)S(1)}, bf16[40,512]{1,0:T(8,128)(2,1)S(1)}, u32[]{:S(2)}, u32[]{:S(2)}) collective-permute-start(bf16[40,512]{1,0:T(8,128)(2,1)S(1)} %get-tuple-element.83), channel_id=1, source_target_pairs={{0,8},{8,0},{16,24},{24,16},{1,9},{9,1},{17,25},{25,17},{2,10},{10... | collective-permute-start | bytes 122888 | tf_op jit(solution)/shard_map/ppermute | solution.py:17
  45.7 2.6 %collective-permute-start.11 = (bf16[40,512]{1,0:T(8,128)(2,1)S(1)}, bf16[40,512]{1,0:T(8,128)(2,1)S(1)}, u32[]{:S(2)}, u32[]{:S(2)}) collective-permute-start(bf16[40,512]{1,0:T(8,128)(2,1)S(1)} %get-tuple-element.84), channel_id=1, source_target_pairs={{0,16},{8,24},{16,0},{24,8},{1,17},{9,25},{17,1},{25,9},{2,18},{10... | collective-permute-start | bytes 122888 | tf_op jit(solution)/shard_map/ppermute | solution.py:17
  48.5 0.5 collective-permute-start.24
  49.4 3.6 %collective-permute-start.26 = (bf16[64,512]{1,0:T(8,128)(2,1)S(1)}, bf16[64,512]{1,0:T(8,128)(2,1)S(1)}, u32[]{:S(2)}, u32[]{:S(2)}) collective-permute-start(bf16[64,512]{1,0:T(8,128)(2,1)S(1)} %get-tuple-element.104), channel_id=1, source_target_pairs={{0,24},{8,16},{16,8},{24,0},{1,25},{9,17},{17,9},{25,1},{2,26},{10... | collective-permute-start | bytes 196616 | tf_op jit(solution)/shard_map/ppermute | solution.py:17
  53.0 0.8 %shard_map.144 = f32[128,1024]{1,0:T(8,128)} custom-call(f32[128,1024]{1,0:T(8,128)S(1)} %get-tuple-element.105.own_ref, f32[128,1024]{1,0:T(8,128)S(1)} %collective-permute-done.27.got_ref), custom_call_target="tpu_custom_call" | custom-call | flops 1073741824 | bytes 1048576 | tf_op jit(solution)/shard_map/pallas_call | solution.py:60
  53.8 0.6 collective-permute-start.12
  54.4 3.4 %collective-permute-done.25.refs_2_ = bf16[64,512]{1,0:T(8,128)(2,1)S(1)} collective-permute-done((bf16[64,512]{1,0:T(8,128)(2,1)S(1)}, bf16[64,512]{1,0:T(8,128)(2,1)S(1)}, u32[]{:S(2)}, u32[]{:S(2)}) %collective-permute-start.25) | collective-permute-done | bytes 65568 | tf_op jit(solution)/shard_map/ppermute | solution.py:17
  57.9 1.5 %collective-permute-start.30 = (bf16[64,512]{1,0:T(8,128)(2,1)S(1)}, bf16[64,512]{1,0:T(8,128)(2,1)S(1)}, u32[]{:S(2)}, u32[]{:S(2)}) collective-permute-start(bf16[64,512]{1,0:T(8,128)(2,1)S(1)} %shard_map.145.refs_0_), channel_id=1, source_target_pairs={{0,24},{8,16},{16,8},{24,0},{1,25},{9,17},{17,9},{25,1},{2,26},{10... | collective-permute-start | bytes 196616 | tf_op jit(solution)/shard_map/ppermute | solution.py:17
  59.3 1.4 %collective-permute-start.29 = (bf16[64,512]{1,0:T(8,128)(2,1)S(1)}, bf16[64,512]{1,0:T(8,128)(2,1)S(1)}, u32[]{:S(2)}, u32[]{:S(2)}) collective-permute-start(bf16[64,512]{1,0:T(8,128)(2,1)S(1)} %shard_map.145.refs_0_), channel_id=1, source_target_pairs={{0,16},{8,24},{16,0},{24,8},{1,17},{9,25},{17,1},{25,9},{2,18},{10... | collective-permute-start | bytes 196616 | tf_op jit(solution)/shard_map/ppermute | solution.py:17
  60.7 1.6 %collective-permute-start.28 = (bf16[64,512]{1,0:T(8,128)(2,1)S(1)}, bf16[64,512]{1,0:T(8,128)(2,1)S(1)}, u32[]{:S(2)}, u32[]{:S(2)}) collective-permute-start(bf16[64,512]{1,0:T(8,128)(2,1)S(1)} %shard_map.145.refs_0_), channel_id=1, source_target_pairs={{0,8},{8,0},{16,24},{24,16},{1,9},{9,1},{17,25},{25,17},{2,10},{10... | collective-permute-start | bytes 196616 | tf_op jit(solution)/shard_map/ppermute | solution.py:17
  62.4 1.9 %collective-permute-start.15 = (bf16[40,512]{1,0:T(8,128)(2,1)S(1)}, bf16[40,512]{1,0:T(8,128)(2,1)S(1)}, u32[]{:S(2)}, u32[]{:S(2)}) collective-permute-start(bf16[40,512]{1,0:T(8,128)(2,1)S(1)} %shard_map.137.refs_0_), channel_id=1, source_target_pairs={{0,5},{1,4},{4,1},{5,0},{2,7},{3,6},{6,3},{7,2},{8,13},{9,12},{12,... | collective-permute-start | bytes 122888 | tf_op jit(solution)/shard_map/ppermute | solution.py:17
  64.2 0.5 collective-permute-start.14
  64.8 1.1 %collective-permute-start.13 = (bf16[40,512]{1,0:T(8,128)(2,1)S(1)}, bf16[40,512]{1,0:T(8,128)(2,1)S(1)}, u32[]{:S(2)}, u32[]{:S(2)}) collective-permute-start(bf16[40,512]{1,0:T(8,128)(2,1)S(1)} %shard_map.137.refs_0_), channel_id=1, source_target_pairs={{0,1},{1,0},{4,5},{5,4},{2,3},{3,2},{6,7},{7,6},{8,9},{9,8},{12,13... | collective-permute-start | bytes 122888 | tf_op jit(solution)/shard_map/ppermute | solution.py:17
  66.0 1.6 %collective-permute-start.32 = (bf16[4,64,512]{2,1,0:T(8,128)(2,1)S(1)}, bf16[4,64,512]{2,1,0:T(8,128)(2,1)S(1)}, u32[]{:S(2)}, u32[]{:S(2)}) collective-permute-start(bf16[4,64,512]{2,1,0:T(8,128)(2,1)S(1)} %shard_map.146.both_ref), channel_id=1, source_target_pairs={{0,4},{4,0},{1,5},{5,1},{2,6},{6,2},{3,7},{7,3},{8,12},{12,8},{9,1... | collective-permute-start | bytes 786440 | tf_op jit(solution)/shard_map/ppermute | solution.py:17
  67.8 0.7 collective-permute-done.14.refs_2_
  68.8 0.6 shard_map.138
  69.4 1.4 %collective-permute-start.18 = (bf16[32,512]{1,0:T(8,128)(2,1)S(1)}, bf16[32,512]{1,0:T(8,128)(2,1)S(1)}, u32[]{:S(2)}, u32[]{:S(2)}) collective-permute-start(bf16[32,512]{1,0:T(8,128)(2,1)S(1)} %get-tuple-element.86.refs_0_), channel_id=1, source_target_pairs={{0,24},{8,16},{16,8},{24,0},{1,25},{9,17},{17,9},{25,1},{2,26},{10... | collective-permute-start | bytes 98312 | tf_op jit(solution)/shard_map/ppermute | solution.py:17
  71.2 2.5 %collective-permute-start.16 = (bf16[32,512]{1,0:T(8,128)(2,1)S(1)}, bf16[32,512]{1,0:T(8,128)(2,1)S(1)}, u32[]{:S(2)}, u32[]{:S(2)}) collective-permute-start(bf16[32,512]{1,0:T(8,128)(2,1)S(1)} %get-tuple-element.86.refs_0_), channel_id=1, source_target_pairs={{0,8},{8,0},{16,24},{24,16},{1,9},{9,1},{17,25},{25,17},{2,10},{10... | collective-permute-start | bytes 98312 | tf_op jit(solution)/shard_map/ppermute | solution.py:17
  73.8 1.3 %collective-permute-done.18.refs_3_ = bf16[32,512]{1,0:T(8,128)(2,1)S(1)} collective-permute-done((bf16[32,512]{1,0:T(8,128)(2,1)S(1)}, bf16[32,512]{1,0:T(8,128)(2,1)S(1)}, u32[]{:S(2)}, u32[]{:S(2)}) %collective-permute-start.18) | collective-permute-done | bytes 32800 | tf_op jit(solution)/shard_map/ppermute | solution.py:17
  75.1 0.8 collective-permute-done.17.refs_2_
  76.6 0.8 %collective-permute-done.19.core_ref = bf16[4,32,512]{2,1,0:T(8,128)(2,1)S(1)} collective-permute-done((bf16[4,32,512]{2,1,0:T(8,128)(2,1)S(1)}, bf16[4,32,512]{2,1,0:T(8,128)(2,1)S(1)}, u32[]{:S(2)}, u32[]{:S(2)}) %collective-permute-start.19) | collective-permute-done | bytes 131104 | tf_op jit(solution)/shard_map/ppermute | solution.py:17
  77.4 0.8 %shard_map.140 = f32[128,1024]{1,0:T(8,128)} custom-call(bf16[4,32,512]{2,1,0:T(8,128)(2,1)S(1)} %shard_map.139.own_ref, bf16[4,32,512]{2,1,0:T(8,128)(2,1)S(1)} %collective-permute-done.19.core_ref), custom_call_target="tpu_custom_call" | custom-call | flops 1073741824 | bytes 1048576 | tf_op jit(solution)/shard_map/pallas_call | solution.py:60
  78.3 1.0 %shard_map.147.held_ref = f32[1024,512]{1,0:T(8,128)} custom-call(bf16[4,64,512]{2,1,0:T(8,128)(2,1)S(1)} %shard_map.146.both_ref, bf16[4,64,512]{2,1,0:T(8,128)(2,1)S(1)} %collective-permute-done.31.core_ref), custom_call_target="tpu_custom_call" | custom-call | flops 1073741824 | bytes 1048576 | tf_op jit(solution)/shard_map/pallas_call | solution.py:60
  79.3 1.0 %shard_map.148 = f32[1024,512]{1,0:T(8,128)} custom-call(f32[1024,512]{1,0:T(8,128)} %shard_map.147.held_ref, bf16[4,64,512]{2,1,0:T(8,128)(2,1)S(1)} %collective-permute-done.32.across_ref, bf16[4,64,512]{2,1,0:T(8,128)(2,1)S(1)} %collective-permute-done.33.core_ref), custom_call_target="tpu_custom_call", output_to_operand_aliasing={{}: (0, {})} | custom-call | flops 1073741824 | bytes 1048576 | tf_op jit(solution)/shard_map/pallas_call | solution.py:60
  (60 shorter events, 3.6 us)
Async XLA Ops:
  1.6 3.2 %copy-start.7 = (bf16[128,1024]{1,0:T(8,128)(2,1)S(1)}, bf16[128,1024]{1,0:T(8,128)(2,1)}, u32[]{:S(2)}) copy-start(bf16[128,1024]{1,0:T(8,128)(2,1)} %dec_ref.1) | copy-start | bytes 786436
  1.6 3.2 %copy-start = (bf16[128,1024]{1,0:T(8,128)(2,1)S(1)}, bf16[128,1024]{1,0:T(8,128)(2,1)}, u32[]{:S(2)}) copy-start(bf16[128,1024]{1,0:T(8,128)(2,1)} %weight_ref.5) | copy-start | bytes 786436
  1.6 3.2 %copy-start.2 = (bf16[512,128]{1,0:T(8,128)(2,1)S(1)}, bf16[512,128]{1,0:T(8,128)(2,1)}, u32[]{:S(2)}) copy-start(bf16[512,128]{1,0:T(8,128)(2,1)} %target_ref.1) | copy-start | bytes 393220
  1.6 3.2 %copy-start.3 = (bf16[512,128]{1,0:T(8,128)(2,1)S(1)}, bf16[512,128]{1,0:T(8,128)(2,1)}, u32[]{:S(2)}) copy-start(bf16[512,128]{1,0:T(8,128)(2,1)} %input_ref.1) | copy-start | bytes 393220
  1.6 3.2 %copy-start.4 = (bf16[1024]{0:T(1024)(128)(2,1)S(1)}, bf16[1024]{0:T(1024)(128)(2,1)}, u32[]{:S(2)}) copy-start(bf16[1024]{0:T(1024)(128)(2,1)} %bias_ref.3) | copy-start | bytes 6148
  1.6 3.2 %copy-start.6 = (s32[16]{0:T(128)S(1)}, s32[16]{0:T(128)}, u32[]{:S(2)}) copy-start(s32[16]{0:T(128)} %window_ref.1) | copy-start | bytes 196
  1.7 5.6 %copy-start.1 = (bf16[1024,512]{1,0:T(8,128)(2,1)S(1)}, bf16[1024,512]{1,0:T(8,128)(2,1)}, u32[]{:S(2)}) copy-start(bf16[1024,512]{1,0:T(8,128)(2,1)} %half_ref.3) | copy-start | bytes 3145732
  1.7 5.6 %copy-start.5 = (bf16[512]{0:T(512)(128)(2,1)S(1)}, bf16[512]{0:T(512)(128)(2,1)}, u32[]{:S(2)}) copy-start(bf16[512]{0:T(512)(128)(2,1)} %bias_ref.5) | copy-start | bytes 3076
  1.7 8.3 %collective-permute-start = (bf16[128,512]{1,0:T(8,128)(2,1)S(1)}, bf16[128,512]{1,0:T(8,128)(2,1)S(1)}, u32[]{:S(2)}, u32[]{:S(2)}) collective-permute-start(bf16[128,512]{1,0:T(8,128)(2,1)S(1)} %shard_map.130), channel_id=1, source_target_pairs={{0,1},{1,0},{2,3},{3,2},{4,5},{5,4},{6,7},{7,6},{8,9},{9,8},{10,11... | collective-permute-start | bytes 393224 | tf_op jit(solution)/shard_map/ppermute | solution.py:17
  4.7 6.8 %collective-permute-start.3 = (bf16[128,1024]{1,0:T(8,128)(2,1)S(1)}, bf16[128,1024]{1,0:T(8,128)(2,1)S(1)}, u32[]{:S(2)}, u32[]{:S(2)}) collective-permute-start(bf16[128,1024]{1,0:T(8,128)(2,1)S(1)} %copy-done.7), channel_id=1, source_target_pairs={{0,2},{2,0},{1,3},{3,1},{4,6},{6,4},{5,7},{7,5},{8,10},{10,8},{9,1... | collective-permute-start | bytes 786440 | tf_op jit(solution)/shard_map/ppermute | solution.py:17
  6.7 4.9 %collective-permute-start.4 = (bf16[9,128,128]{2,1,0:T(8,128)(2,1)S(1)}, bf16[9,128,128]{2,1,0:T(8,128)(2,1)S(1)}, u32[]{:S(2)}, u32[]{:S(2)}) collective-permute-start(bf16[9,128,128]{2,1,0:T(8,128)(2,1)S(1)} %get-tuple-element.64), channel_id=1, source_target_pairs={{0,2},{2,0},{1,3},{3,1},{4,6},{6,4},{5,7},{7,5},{8,10},{10,8},{9,1... | collective-permute-start | bytes 884744 | tf_op jit(solution)/shard_map/ppermute | solution.py:17
  7.4 8.7 %collective-permute-start.1 = (bf16[272,512]{1,0:T(8,128)(2,1)S(1)}, bf16[272,512]{1,0:T(8,128)(2,1)S(1)}, u32[]{:S(2)}, u32[]{:S(2)}) collective-permute-start(bf16[272,512]{1,0:T(8,128)(2,1)S(1)} %dynamic-slice_select_fusion), channel_id=1, source_target_pairs={{0,1},{1,0},{2,3},{3,2},{4,5},{5,4},{6,7},{7,6},{8,9},{9,8},{10,11... | collective-permute-start | bytes 835592 | tf_op jit(solution)/shard_map/ppermute | solution.py:17
  10.0 5.3 %collective-permute-start.2 = (bf16[128,512]{1,0:T(8,128)(2,1)S(1)}, bf16[128,512]{1,0:T(8,128)(2,1)S(1)}, u32[]{:S(2)}, u32[]{:S(2)}) collective-permute-start(bf16[128,512]{1,0:T(8,128)(2,1)S(1)} %collective-permute-done.near_ref), channel_id=1, source_target_pairs={{0,4},{4,0},{1,5},{5,1},{2,6},{6,2},{3,7},{7,3},{8,12},{12,8},{9,1... | collective-permute-start | bytes 393224 | tf_op jit(solution)/shard_map/ppermute | solution.py:17
  16.0 1.9 %collective-permute-start.7 = (bf16[272,512]{1,0:T(8,128)(2,1)S(1)}, bf16[272,512]{1,0:T(8,128)(2,1)S(1)}, u32[]{:S(2)}, u32[]{:S(2)}) collective-permute-start(bf16[272,512]{1,0:T(8,128)(2,1)S(1)} %collective-permute-done.1.rest_ref), channel_id=1, source_target_pairs={{0,2},{2,0},{1,3},{3,1},{4,6},{6,4},{5,7},{7,5},{8,10},{10,8},{9,1... | collective-permute-start | bytes 835592 | tf_op jit(solution)/shard_map/ppermute | solution.py:17
  16.0 1.7 %collective-permute-start.5 = (bf16[128,512]{1,0:T(8,128)(2,1)S(1)}, bf16[128,512]{1,0:T(8,128)(2,1)S(1)}, u32[]{:S(2)}, u32[]{:S(2)}) collective-permute-start(bf16[128,512]{1,0:T(8,128)(2,1)S(1)} %collective-permute-done.near_ref), channel_id=1, source_target_pairs={{0,2},{2,0},{1,3},{3,1},{4,6},{6,4},{5,7},{7,5},{8,10},{10,8},{9,1... | collective-permute-start | bytes 393224 | tf_op jit(solution)/shard_map/ppermute | solution.py:17
  16.5 1.4 %collective-permute-start.6 = (bf16[128,512]{1,0:T(8,128)(2,1)S(1)}, bf16[128,512]{1,0:T(8,128)(2,1)S(1)}, u32[]{:S(2)}, u32[]{:S(2)}) collective-permute-start(bf16[128,512]{1,0:T(8,128)(2,1)S(1)} %collective-permute-done.2.far_ref), channel_id=1, source_target_pairs={{0,2},{2,0},{1,3},{3,1},{4,6},{6,4},{5,7},{7,5},{8,10},{10,8},{9,1... | collective-permute-start | bytes 393224 | tf_op jit(solution)/shard_map/ppermute | solution.py:17
  21.7 2.2 %collective-permute-start.20 = (bf16[512,512]{1,0:T(8,128)(2,1)S(1)}, bf16[512,512]{1,0:T(8,128)(2,1)S(1)}, u32[]{:S(2)}, u32[]{:S(2)}) collective-permute-start(bf16[512,512]{1,0:T(8,128)(2,1)S(1)} %get-tuple-element.89), channel_id=1, source_target_pairs={{0,2},{2,0},{1,3},{3,1},{4,6},{6,4},{5,7},{7,5},{8,10},{10,8},{9,1... | collective-permute-start | bytes 1572872 | tf_op jit(solution)/shard_map/ppermute | solution.py:17
  23.4 3.5 %collective-permute-start.8 = (bf16[512,512]{1,0:T(8,128)(2,1)S(1)}, bf16[512,512]{1,0:T(8,128)(2,1)S(1)}, u32[]{:S(2)}, u32[]{:S(2)}) collective-permute-start(bf16[512,512]{1,0:T(8,128)(2,1)S(1)} %get-tuple-element.73), channel_id=1, source_target_pairs={{0,2},{2,0},{1,3},{3,1},{4,6},{6,4},{5,7},{7,5},{8,10},{10,8},{9,1... | collective-permute-start | bytes 1572872 | tf_op jit(solution)/shard_map/ppermute | solution.py:17
  24.0 14.0 %collective-permute-start.21 = (bf16[256,512]{1,0:T(8,128)(2,1)S(1)}, bf16[256,512]{1,0:T(8,128)(2,1)S(1)}, u32[]{:S(2)}, u32[]{:S(2)}) collective-permute-start(bf16[256,512]{1,0:T(8,128)(2,1)S(1)} %get-tuple-element.90), channel_id=1, source_target_pairs={{0,1},{1,0},{4,5},{5,4},{2,3},{3,2},{6,7},{7,6},{8,9},{9,8},{12,13... | collective-permute-start | bytes 786440 | tf_op jit(solution)/shard_map/ppermute | solution.py:17
  24.9 13.1 %collective-permute-start.23 = (bf16[256,512]{1,0:T(8,128)(2,1)S(1)}, bf16[256,512]{1,0:T(8,128)(2,1)S(1)}, u32[]{:S(2)}, u32[]{:S(2)}) collective-permute-start(bf16[256,512]{1,0:T(8,128)(2,1)S(1)} %get-tuple-element.92), channel_id=1, source_target_pairs={{0,5},{1,4},{4,1},{5,0},{2,7},{3,6},{6,3},{7,2},{8,13},{9,12},{12,... | collective-permute-start | bytes 786440 | tf_op jit(solution)/shard_map/ppermute | solution.py:17
  28.0 11.2 %collective-permute-start.22 = (bf16[256,512]{1,0:T(8,128)(2,1)S(1)}, bf16[256,512]{1,0:T(8,128)(2,1)S(1)}, u32[]{:S(2)}, u32[]{:S(2)}) collective-permute-start(bf16[256,512]{1,0:T(8,128)(2,1)S(1)} %get-tuple-element.91), channel_id=1, source_target_pairs={{0,4},{1,5},{4,0},{5,1},{2,6},{3,7},{6,2},{7,3},{8,12},{9,13},{12,... | collective-permute-start | bytes 786440 | tf_op jit(solution)/shard_map/ppermute | solution.py:17
  39.2 10.2 %collective-permute-start.27 = (f32[128,1024]{1,0:T(8,128)S(1)}, f32[128,1024]{1,0:T(8,128)S(1)}, u32[]{:S(2)}, u32[]{:S(2)}) collective-permute-start(f32[128,1024]{1,0:T(8,128)S(1)} %get-tuple-element.106), channel_id=1, source_target_pairs={{0,2},{2,0},{1,3},{3,1},{4,6},{6,4},{5,7},{7,5},{8,10},{10,8},{9,1... | collective-permute-start | bytes 1572872 | tf_op jit(solution)/shard_map/ppermute | solution.py:17
  42.4 1.6 %collective-permute-start.9 = (bf16[136,512]{1,0:T(8,128)(2,1)S(1)}, bf16[136,512]{1,0:T(8,128)(2,1)S(1)}, u32[]{:S(2)}, u32[]{:S(2)}) collective-permute-start(bf16[136,512]{1,0:T(8,128)(2,1)S(1)} %get-tuple-element.80), channel_id=1, source_target_pairs={{0,2},{2,0},{1,3},{3,1},{4,6},{6,4},{5,7},{7,5},{8,10},{10,8},{9,1... | collective-permute-start | bytes 417800 | tf_op jit(solution)/shard_map/ppermute | solution.py:17
  44.0 16.7 %collective-permute-start.10 = (bf16[40,512]{1,0:T(8,128)(2,1)S(1)}, bf16[40,512]{1,0:T(8,128)(2,1)S(1)}, u32[]{:S(2)}, u32[]{:S(2)}) collective-permute-start(bf16[40,512]{1,0:T(8,128)(2,1)S(1)} %get-tuple-element.83), channel_id=1, source_target_pairs={{0,8},{8,0},{16,24},{24,16},{1,9},{9,1},{17,25},{25,17},{2,10},{10... | collective-permute-start | bytes 122888 | tf_op jit(solution)/shard_map/ppermute | solution.py:17
  45.7 16.7 %collective-permute-start.11 = (bf16[40,512]{1,0:T(8,128)(2,1)S(1)}, bf16[40,512]{1,0:T(8,128)(2,1)S(1)}, u32[]{:S(2)}, u32[]{:S(2)}) collective-permute-start(bf16[40,512]{1,0:T(8,128)(2,1)S(1)} %get-tuple-element.84), channel_id=1, source_target_pairs={{0,16},{8,24},{16,0},{24,8},{1,17},{9,25},{17,1},{25,9},{2,18},{10... | collective-permute-start | bytes 122888 | tf_op jit(solution)/shard_map/ppermute | solution.py:17
  48.5 5.3 %collective-permute-start.24 = (bf16[64,512]{1,0:T(8,128)(2,1)S(1)}, bf16[64,512]{1,0:T(8,128)(2,1)S(1)}, u32[]{:S(2)}, u32[]{:S(2)}) collective-permute-start(bf16[64,512]{1,0:T(8,128)(2,1)S(1)} %get-tuple-element.102), channel_id=1, source_target_pairs={{0,8},{8,0},{16,24},{24,16},{1,9},{9,1},{17,25},{25,17},{2,10},{10... | collective-permute-start | bytes 196616 | tf_op jit(solution)/shard_map/ppermute | solution.py:17
  49.1 8.8 %collective-permute-start.25 = (bf16[64,512]{1,0:T(8,128)(2,1)S(1)}, bf16[64,512]{1,0:T(8,128)(2,1)S(1)}, u32[]{:S(2)}, u32[]{:S(2)}) collective-permute-start(bf16[64,512]{1,0:T(8,128)(2,1)S(1)} %get-tuple-element.103), channel_id=1, source_target_pairs={{0,16},{8,24},{16,0},{24,8},{1,17},{9,25},{17,1},{25,9},{2,18},{10... | collective-permute-start | bytes 196616 | tf_op jit(solution)/shard_map/ppermute | solution.py:17
  49.4 8.4 %collective-permute-start.26 = (bf16[64,512]{1,0:T(8,128)(2,1)S(1)}, bf16[64,512]{1,0:T(8,128)(2,1)S(1)}, u32[]{:S(2)}, u32[]{:S(2)}) collective-permute-start(bf16[64,512]{1,0:T(8,128)(2,1)S(1)} %get-tuple-element.104), channel_id=1, source_target_pairs={{0,24},{8,16},{16,8},{24,0},{1,25},{9,17},{17,9},{25,1},{2,26},{10... | collective-permute-start | bytes 196616 | tf_op jit(solution)/shard_map/ppermute | solution.py:17
  53.8 8.5 %collective-permute-start.12 = (bf16[40,512]{1,0:T(8,128)(2,1)S(1)}, bf16[40,512]{1,0:T(8,128)(2,1)S(1)}, u32[]{:S(2)}, u32[]{:S(2)}) collective-permute-start(bf16[40,512]{1,0:T(8,128)(2,1)S(1)} %get-tuple-element.85), channel_id=1, source_target_pairs={{0,24},{8,16},{16,8},{24,0},{1,25},{9,17},{17,9},{25,1},{2,26},{10... | collective-permute-start | bytes 122888 | tf_op jit(solution)/shard_map/ppermute | solution.py:17
  57.9 6.9 %collective-permute-start.30 = (bf16[64,512]{1,0:T(8,128)(2,1)S(1)}, bf16[64,512]{1,0:T(8,128)(2,1)S(1)}, u32[]{:S(2)}, u32[]{:S(2)}) collective-permute-start(bf16[64,512]{1,0:T(8,128)(2,1)S(1)} %shard_map.145.refs_0_), channel_id=1, source_target_pairs={{0,24},{8,16},{16,8},{24,0},{1,25},{9,17},{17,9},{25,1},{2,26},{10... | collective-permute-start | bytes 196616 | tf_op jit(solution)/shard_map/ppermute | solution.py:17
  59.3 6.6 %collective-permute-start.29 = (bf16[64,512]{1,0:T(8,128)(2,1)S(1)}, bf16[64,512]{1,0:T(8,128)(2,1)S(1)}, u32[]{:S(2)}, u32[]{:S(2)}) collective-permute-start(bf16[64,512]{1,0:T(8,128)(2,1)S(1)} %shard_map.145.refs_0_), channel_id=1, source_target_pairs={{0,16},{8,24},{16,0},{24,8},{1,17},{9,25},{17,1},{25,9},{2,18},{10... | collective-permute-start | bytes 196616 | tf_op jit(solution)/shard_map/ppermute | solution.py:17
  60.7 5.2 %collective-permute-start.28 = (bf16[64,512]{1,0:T(8,128)(2,1)S(1)}, bf16[64,512]{1,0:T(8,128)(2,1)S(1)}, u32[]{:S(2)}, u32[]{:S(2)}) collective-permute-start(bf16[64,512]{1,0:T(8,128)(2,1)S(1)} %shard_map.145.refs_0_), channel_id=1, source_target_pairs={{0,8},{8,0},{16,24},{24,16},{1,9},{9,1},{17,25},{25,17},{2,10},{10... | collective-permute-start | bytes 196616 | tf_op jit(solution)/shard_map/ppermute | solution.py:17
  62.4 5.4 %collective-permute-start.15 = (bf16[40,512]{1,0:T(8,128)(2,1)S(1)}, bf16[40,512]{1,0:T(8,128)(2,1)S(1)}, u32[]{:S(2)}, u32[]{:S(2)}) collective-permute-start(bf16[40,512]{1,0:T(8,128)(2,1)S(1)} %shard_map.137.refs_0_), channel_id=1, source_target_pairs={{0,5},{1,4},{4,1},{5,0},{2,7},{3,6},{6,3},{7,2},{8,13},{9,12},{12,... | collective-permute-start | bytes 122888 | tf_op jit(solution)/shard_map/ppermute | solution.py:17
  64.2 4.2 %collective-permute-start.14 = (bf16[40,512]{1,0:T(8,128)(2,1)S(1)}, bf16[40,512]{1,0:T(8,128)(2,1)S(1)}, u32[]{:S(2)}, u32[]{:S(2)}) collective-permute-start(bf16[40,512]{1,0:T(8,128)(2,1)S(1)} %shard_map.137.refs_0_), channel_id=1, source_target_pairs={{0,4},{1,5},{4,0},{5,1},{2,6},{3,7},{6,2},{7,3},{8,12},{9,13},{12,... | collective-permute-start | bytes 122888 | tf_op jit(solution)/shard_map/ppermute | solution.py:17
  64.8 4.0 %collective-permute-start.13 = (bf16[40,512]{1,0:T(8,128)(2,1)S(1)}, bf16[40,512]{1,0:T(8,128)(2,1)S(1)}, u32[]{:S(2)}, u32[]{:S(2)}) collective-permute-start(bf16[40,512]{1,0:T(8,128)(2,1)S(1)} %shard_map.137.refs_0_), channel_id=1, source_target_pairs={{0,1},{1,0},{4,5},{5,4},{2,3},{3,2},{6,7},{7,6},{8,9},{9,8},{12,13... | collective-permute-start | bytes 122888 | tf_op jit(solution)/shard_map/ppermute | solution.py:17
  66.0 10.2 %collective-permute-start.32 = (bf16[4,64,512]{2,1,0:T(8,128)(2,1)S(1)}, bf16[4,64,512]{2,1,0:T(8,128)(2,1)S(1)}, u32[]{:S(2)}, u32[]{:S(2)}) collective-permute-start(bf16[4,64,512]{2,1,0:T(8,128)(2,1)S(1)} %shard_map.146.both_ref), channel_id=1, source_target_pairs={{0,4},{4,0},{1,5},{5,1},{2,6},{6,2},{3,7},{7,3},{8,12},{12,8},{9,1... | collective-permute-start | bytes 786440 | tf_op jit(solution)/shard_map/ppermute | solution.py:17
  69.4 5.7 %collective-permute-start.18 = (bf16[32,512]{1,0:T(8,128)(2,1)S(1)}, bf16[32,512]{1,0:T(8,128)(2,1)S(1)}, u32[]{:S(2)}, u32[]{:S(2)}) collective-permute-start(bf16[32,512]{1,0:T(8,128)(2,1)S(1)} %get-tuple-element.86.refs_0_), channel_id=1, source_target_pairs={{0,24},{8,16},{16,8},{24,0},{1,25},{9,17},{17,9},{25,1},{2,26},{10... | collective-permute-start | bytes 98312 | tf_op jit(solution)/shard_map/ppermute | solution.py:17
  70.8 5.1 %collective-permute-start.17 = (bf16[32,512]{1,0:T(8,128)(2,1)S(1)}, bf16[32,512]{1,0:T(8,128)(2,1)S(1)}, u32[]{:S(2)}, u32[]{:S(2)}) collective-permute-start(bf16[32,512]{1,0:T(8,128)(2,1)S(1)} %get-tuple-element.86.refs_0_), channel_id=1, source_target_pairs={{0,16},{8,24},{16,0},{24,8},{1,17},{9,25},{17,1},{25,9},{2,18},{10... | collective-permute-start | bytes 98312 | tf_op jit(solution)/shard_map/ppermute | solution.py:17
  71.2 4.8 %collective-permute-start.16 = (bf16[32,512]{1,0:T(8,128)(2,1)S(1)}, bf16[32,512]{1,0:T(8,128)(2,1)S(1)}, u32[]{:S(2)}, u32[]{:S(2)}) collective-permute-start(bf16[32,512]{1,0:T(8,128)(2,1)S(1)} %get-tuple-element.86.refs_0_), channel_id=1, source_target_pairs={{0,8},{8,0},{16,24},{24,16},{1,9},{9,1},{17,25},{25,17},{2,10},{10... | collective-permute-start | bytes 98312 | tf_op jit(solution)/shard_map/ppermute | solution.py:17
  73.8 4.5 %collective-permute-start.31 = (bf16[4,64,512]{2,1,0:T(8,128)(2,1)S(1)}, bf16[4,64,512]{2,1,0:T(8,128)(2,1)S(1)}, u32[]{:S(2)}, u32[]{:S(2)}) collective-permute-start(bf16[4,64,512]{2,1,0:T(8,128)(2,1)S(1)} %shard_map.146.both_ref), channel_id=1, source_target_pairs={{0,2},{2,0},{1,3},{3,1},{4,6},{6,4},{5,7},{7,5},{8,10},{10,8},{9,1... | collective-permute-start | bytes 786440 | tf_op jit(solution)/shard_map/ppermute | solution.py:17
  76.0 1.4 %collective-permute-start.19 = (bf16[4,32,512]{2,1,0:T(8,128)(2,1)S(1)}, bf16[4,32,512]{2,1,0:T(8,128)(2,1)S(1)}, u32[]{:S(2)}, u32[]{:S(2)}) collective-permute-start(bf16[4,32,512]{2,1,0:T(8,128)(2,1)S(1)} %shard_map.139.own_ref), channel_id=1, source_target_pairs={{0,2},{2,0},{1,3},{3,1},{4,6},{6,4},{5,7},{7,5},{8,10},{10,8},{9,1... | collective-permute-start | bytes 393224 | tf_op jit(solution)/shard_map/ppermute | solution.py:17
  76.1 3.2 %collective-permute-start.33 = (bf16[4,64,512]{2,1,0:T(8,128)(2,1)S(1)}, bf16[4,64,512]{2,1,0:T(8,128)(2,1)S(1)}, u32[]{:S(2)}, u32[]{:S(2)}) collective-permute-start(bf16[4,64,512]{2,1,0:T(8,128)(2,1)S(1)} %collective-permute-done.32.across_ref), channel_id=1, source_target_pairs={{0,2},{2,0},{1,3},{3,1},{4,6},{6,4},{5,7},{7,5},{8,10},{10,8},{9,1... | collective-permute-start | bytes 786440 | tf_op jit(solution)/shard_map/ppermute | solution.py:17

commit v3 on v2

--- a/solution.py
+++ b/solution.py
@@ -1,3 +1,5 @@
+import functools
+
 import jax
 import jax.numpy as jnp
 from jax import lax
@@ -500,7 +502,7 @@
                 copies[-1].start()
             return copies
 
-        def spread_early(both_ref, core_ref, out_ref, stage_ref, sem_ref):
+        def early(both_ref, core_ref, out_ref, stage_ref, sem_ref):
             mx, mc = lax.axis_index("x"), lax.axis_index("c")
             copies = put(both_ref, mc * nx + mx, hrow_z, out_ref, stage_ref, sem_ref, 0)
             copies += put(core_ref, (mc ^ 1) * nx + mx, hrow_z, out_ref, stage_ref, sem_ref, 1)
@@ -509,7 +511,7 @@
 
         stage = [pltpu.VMEM((nc * nz, hrow_z, kw), F32), pltpu.SemaphoreType.DMA((nc * nz,))]
 
-        def spread_first(own_ref, core_ref, first_ref):
+        def top(own_ref, core_ref, first_ref):
             mc = lax.axis_index("c")
             for u, ref in enumerate((own_ref, core_ref)):
                 for i in range(nz):
@@ -518,34 +520,32 @@
                     for b in range(ny):
                         first_ref[rows, b * kw : (b + 1) * kw] = value[b * frow_z : (b + 1) * frow_z]
 
-        def spread_late(held_ref, across_ref, core_ref, out_ref, stage_ref, sem_ref):
+        def late(core, held_ref, across_ref, out_ref, stage_ref, sem_ref):
             mx, mc = lax.axis_index("x"), lax.axis_index("c")
-            copies = put(across_ref, mc * nx + (mx ^ 1), hrow_z, out_ref, stage_ref, sem_ref, 0)
-            copies += put(core_ref, (mc ^ 1) * nx + (mx ^ 1), hrow_z, out_ref, stage_ref, sem_ref, 1)
-            for copy in copies:
+            base = (mc ^ core) * nx + (mx ^ 1)
+            for copy in put(across_ref, base, hrow_z, out_ref, stage_ref, sem_ref, 0):
                 copy.wait()
 
         (hidden_out,) = local_call(
-            spread_early,
+            early,
             [((hidden, kw), F32)],
             (both, both_core),
             out_specs=[ANY],
             scratch=stage,
             limit=8 << 20,
         )
-        (first_out,) = local_call(
-            spread_first, [((rank, hidden), F32)], (first, first_core), limit=4 << 20
-        )
-        (hidden_out,) = local_call(
-            spread_late,
-            [((hidden, kw), F32)],
-            (hidden_out, across, across_core),
-            specs=[ANY, VMEM, VMEM],
-            out_specs=[ANY],
-            scratch=stage,
-            aliases={0: 0},
-            limit=8 << 20,
-        )
+        (first_out,) = local_call(top, [((rank, hidden), F32)], (first, first_core), limit=4 << 20)
+        for core, value in ((0, across), (1, across_core)):
+            (hidden_out,) = local_call(
+                functools.partial(late, core),
+                [((hidden, kw), F32)],
+                (hidden_out, value),
+                specs=[ANY, VMEM],
+                out_specs=[ANY],
+                scratch=stage,
+                aliases={0: 0},
+                limit=8 << 20,
+            )
         return (first_out, first_bias_out, hidden_out, hidden_bias_out, decoder_grad)
 
     return on_device

time: 80.6 us -> 84.1 us (1.043)
  waiting for transfers between devices: 23.7 us -> 27.3 us
    ppermute x34, waiting for transfers between devices: 23.7 us -> 27.3 us  [swap(): return lax.ppermute(value, axes, [(j, j ^ step) for j in range(size)])]
    ppermute x34, starting transfers between devices: 35.1 us -> 34.3 us  [swap(): return lax.ppermute(value, axes, [(j, j ^ step) for j in range(size)])]
    pallas_call x21 -> x22, Pallas kernels: 19.6 us -> 20.3 us  [kernel_call(): pl.pallas_call(body, out_shape=[jax.ShapeDtypeStruct(shape, kind) for sha...]
  transfers between devices with their start and end apart: 34 -> 34, of which waited for: 15 -> 13; matrix products, arithmetic and copies ran while one was open for 0% -> 0% of each run, Pallas kernels for 18% -> 19%
where the time goes in v3:
time: 84.1 us; the launch traced here: 83.9 us
  starting transfers between devices  34.3 us (41%)
  waiting for transfers between devices  27.3 us (32%)
  Pallas kernels  20.3 us (24%)
  local copies, waits for them, and re-layouts  0.97 us (1%)
  between operations  0.93 us (1%)
    ppermute x34, starting transfers between devices, swap(): return lax.ppermute(value, axes, [(j, j ^ step) for j in range(size)])  34.3 us
    ppermute x34, waiting for transfers between devices, swap(): return lax.ppermute(value, axes, [(j, j ^ step) for j in range(size)])  27.3 us
    pallas_call x22, Pallas kernels, kernel_call(): pl.pallas_call(body, out_shape=[jax.ShapeDtypeStruct(shape, kind) for sha...  20.3 us
  transfers between devices with their start and end apart: 34, of which 13 were waited for; matrix products, arithmetic and copies ran while one was open for 0% of the time, Pallas kernels for 19%

profile of v3, /device:TPU:0, one launch (start us, length us, event | category | flops | bytes accessed | tf_op | source)
XLA Modules:
  0.0 83.9 jit_solution(3732410044405146988)
XLA Ops:
  0.6 0.9 %constant_dynamic-slice_fusion.in_ref = bf16[128,512]{1,0:T(8,128)(2,1)S(1)} fusion(bf16[1024,512]{1,0:T(8,128)(2,1)} %half_ref.3, s32[]{:T(128)S(6)} %select_n.10), kind=kLoop, calls=%fused_computation.2 | loop fusion | bytes 262148 | tf_op jit(solution)/shard_map/dynamic_slice | solution.py:109
  1.7 3.1 %collective-permute-start = (bf16[128,512]{1,0:T(8,128)(2,1)S(1)}, bf16[128,512]{1,0:T(8,128)(2,1)S(1)}, u32[]{:S(2)}, u32[]{:S(2)}) collective-permute-start(bf16[128,512]{1,0:T(8,128)(2,1)S(1)} %shard_map.130), channel_id=1, source_target_pairs={{0,1},{1,0},{2,3},{3,2},{4,5},{5,4},{6,7},{7,6},{8,9},{9,8},{10,11... | collective-permute-start | bytes 393224 | tf_op jit(solution)/shard_map/ppermute | solution.py:19
  4.8 1.9 %shard_map.128 = (bf16[9,128,128]{2,1,0:T(8,128)(2,1)S(1)}, bf16[9,128,128]{2,1,0:T(8,128)(2,1)S(1)}, f32[8,1024]{1,0:T(8,128)S(1)}, f32[128,128]{1,0:T(8,128)S(1)}) custom-call(s32[16]{0:T(128)S(1)} %copy-done.6, bf16[512,128,128]{2,1,0:T(8,128)(2,1)} %jac_ref.1, bf16[512,128]{1,0:T(8,128)(2,1)S(1)} %copy-done.2, bf16[512,128]{1,0:T(8,128)(2,1)S(1)} %copy-done.3, ...), custom_call_target="tpu_custom_call" | custom-call | flops 4294967296 | bytes 1048576 | tf_op jit(solution)/shard_map/pallas_call | solution.py:62
  6.7 0.6 collective-permute-start.4
  7.4 0.8 collective-permute-start.1
  8.2 1.8 %shard_map.129 = (bf16[1152,1024]{1,0:T(8,128)(2,1)S(1)}, bf16[1024,1152]{1,0:T(8,128)(2,1)S(1)}, f32[1152,512]{1,0:T(8,128)S(1)}) custom-call(f32[8,1024]{1,0:T(8,128)S(1)} %get-tuple-element.59.act_ref, bf16[128,1024]{1,0:T(8,128)(2,1)S(1)} %copy-done, bf16[1024,512]{1,0:T(8,128)(2,1)S(1)} %copy-done.1), custom_call_target="tpu_custom_call" | custom-call | flops 2147483648 | bytes 1048576 | tf_op jit(solution)/shard_map/pallas_call | solution.py:62
  10.0 1.6 %collective-permute-start.2 = (bf16[128,512]{1,0:T(8,128)(2,1)S(1)}, bf16[128,512]{1,0:T(8,128)(2,1)S(1)}, u32[]{:S(2)}, u32[]{:S(2)}) collective-permute-start(bf16[128,512]{1,0:T(8,128)(2,1)S(1)} %collective-permute-done.near_ref), channel_id=1, source_target_pairs={{0,4},{4,0},{1,5},{5,1},{2,6},{6,2},{3,7},{7,3},{8,12},{12,8},{9,1... | collective-permute-start | bytes 393224 | tf_op jit(solution)/shard_map/ppermute | solution.py:19
  11.6 0.7 shard_map.131
  12.3 3.1 %collective-permute-done.2.far_ref = bf16[128,512]{1,0:T(8,128)(2,1)S(1)} collective-permute-done((bf16[128,512]{1,0:T(8,128)(2,1)S(1)}, bf16[128,512]{1,0:T(8,128)(2,1)S(1)}, u32[]{:S(2)}, u32[]{:S(2)}) %collective-permute-start.2) | collective-permute-done | bytes 131104 | tf_op jit(solution)/shard_map/ppermute | solution.py:19
  15.4 0.7 collective-permute-done.1.rest_ref
  16.0 0.5 collective-permute-start.5
  16.5 1.2 %collective-permute-done.5.near2_ref = bf16[128,512]{1,0:T(8,128)(2,1)S(1)} collective-permute-done((bf16[128,512]{1,0:T(8,128)(2,1)S(1)}, bf16[128,512]{1,0:T(8,128)(2,1)S(1)}, u32[]{:S(2)}, u32[]{:S(2)}) %collective-permute-start.5) | collective-permute-done | bytes 131104 | tf_op jit(solution)/shard_map/ppermute | solution.py:19
  18.0 3.7 %shard_map.132 = (bf16[1024,512]{1,0:T(8,128)(2,1)S(1)}, bf16[1152,512]{1,0:T(8,128)(2,1)S(1)}, bf16[256,1152]{1,0:T(8,128)(2,1)S(1)}, bf16[1152,1024]{1,0:T(8,1...) custom-call(bf16[1152,1024]{1,0:T(8,128)(2,1)S(1)} %get-tuple-element.60.tan1_ref, ...), custom_call_target="tpu_custom_call" | custom-call | flops 5368709120 | bytes 1048576 | tf_op jit(solution)/shard_map/pallas_call | solution.py:62
  21.9 1.5 %shard_map.133 = (f32[512,512]{1,0:T(8,128)S(1)}, bf16[512,512]{1,0:T(8,128)(2,1)S(1)}) custom-call(bf16[1024,1152]{1,0:T(8,128)(2,1)S(1)} %get-tuple-element.61.side_ref, bf16[1152,1024]{1,0:T(8,128)(2,1)S(1)} %get-tuple-element.75.round_ref), custom_call_target="tpu_custom_call" | custom-call | flops 1610612736 | bytes 1048576 | tf_op jit(solution)/shard_map/pallas_call | solution.py:62
  23.4 0.4 collective-permute-start.8
  24.0 0.9 %collective-permute-start.21 = (bf16[256,512]{1,0:T(8,128)(2,1)S(1)}, bf16[256,512]{1,0:T(8,128)(2,1)S(1)}, u32[]{:S(2)}, u32[]{:S(2)}) collective-permute-start(bf16[256,512]{1,0:T(8,128)(2,1)S(1)} %get-tuple-element.90), channel_id=1, source_target_pairs={{0,1},{1,0},{4,5},{5,4},{2,3},{3,2},{6,7},{7,6},{8,9},{9,8},{12,13... | collective-permute-start | bytes 786440 | tf_op jit(solution)/shard_map/ppermute | solution.py:19
  24.9 2.1 %collective-permute-start.23 = (bf16[256,512]{1,0:T(8,128)(2,1)S(1)}, bf16[256,512]{1,0:T(8,128)(2,1)S(1)}, u32[]{:S(2)}, u32[]{:S(2)}) collective-permute-start(bf16[256,512]{1,0:T(8,128)(2,1)S(1)} %get-tuple-element.92), channel_id=1, source_target_pairs={{0,5},{1,4},{4,1},{5,0},{2,7},{3,6},{6,3},{7,2},{8,13},{9,12},{12,... | collective-permute-start | bytes 786440 | tf_op jit(solution)/shard_map/ppermute | solution.py:19
  27.0 1.0 %shard_map.134 = (bf16[256,512]{1,0:T(8,128)(2,1)S(1)}, bf16[256,512]{1,0:T(8,128)(2,1)S(1)}) custom-call(bf16[1024,1152]{1,0:T(8,128)(2,1)S(1)} %get-tuple-element.61.side_ref, bf16[1152,1024]{1,0:T(8,128)(2,1)S(1)} %get-tuple-element.75.round_ref, bf16[512,512]{1,0:T(8,128)(2,1)S(1)} %collective-permute-done.8.got_ref), custom_call_target="tpu_custom_call" | custom-call | flops 1073741824 | bytes 1048576 | tf_op jit(solution)/shard_map/pallas_call | solution.py:62
  28.0 0.6 collective-permute-start.22
  28.6 0.9 %shard_map.142 = (f32[128,1024]{1,0:T(8,128)S(1)}, f32[128,1024]{1,0:T(8,128)S(1)}) custom-call(bf16[256,1152]{1,0:T(8,128)(2,1)S(1)} %get-tuple-element.93.miss_ref, bf16[1152,512]{1,0:T(8,128)(2,1)S(1)} %get-tuple-element.94.tan_ref, bf16[1152,512]{1,0:T(8,128)(2,1)S(1)} %get-tuple-element.95.tan_got_ref), custom_call_target="tpu_custom_call" | custom-call | flops 1073741824 | bytes 1048576 | tf_op jit(solution)/shard_map/pallas_call | solution.py:62
  29.5 8.5 %collective-permute-done.21.refs_1_ = bf16[256,512]{1,0:T(8,128)(2,1)S(1)} collective-permute-done((bf16[256,512]{1,0:T(8,128)(2,1)S(1)}, bf16[256,512]{1,0:T(8,128)(2,1)S(1)}, u32[]{:S(2)}, u32[]{:S(2)}) %collective-permute-start.21) | collective-permute-done | bytes 262176 | tf_op jit(solution)/shard_map/ppermute | solution.py:19
  38.0 1.2 %collective-permute-done.22.refs_2_ = bf16[256,512]{1,0:T(8,128)(2,1)S(1)} collective-permute-done((bf16[256,512]{1,0:T(8,128)(2,1)S(1)}, bf16[256,512]{1,0:T(8,128)(2,1)S(1)}, u32[]{:S(2)}, u32[]{:S(2)}) %collective-permute-start.22) | collective-permute-done | bytes 262176 | tf_op jit(solution)/shard_map/ppermute | solution.py:19
  39.2 3.2 %shard_map.135 = (f32[64,1024]{1,0:T(8,128)S(1)}, bf16[136,512]{1,0:T(8,128)(2,1)S(1)}, bf16[8,512]{1,0:T(8,128)(2,1)S(1)}) custom-call(bf16[1152,1024]{1,0:T(8,128)(2,1)S(1)} %get-tuple-element.75.round_ref, bf16[1024,512]{1,0:T(8,128)(2,1)S(1)} %copy-done.1, bf16[1024,512]{1,0:T(8,128)(2,1)S(1)} %get-tuple-element.76.got_ref, ...), custom_call_target="tpu_custom_call" | custom-call | flops 3221225472 | bytes 1048576 | tf_op jit(solution)/shard_map/pallas_call | solution.py:62
  42.4 0.6 collective-permute-start.9
  43.0 1.0 %collective-permute-done.9.got_ref = bf16[136,512]{1,0:T(8,128)(2,1)S(1)} collective-permute-done((bf16[136,512]{1,0:T(8,128)(2,1)S(1)}, bf16[136,512]{1,0:T(8,128)(2,1)S(1)}, u32[]{:S(2)}, u32[]{:S(2)}) %collective-permute-start.9) | collective-permute-done | bytes 139296 | tf_op jit(solution)/shard_map/ppermute | solution.py:19
  44.0 1.6 %collective-permute-start.10 = (bf16[40,512]{1,0:T(8,128)(2,1)S(1)}, bf16[40,512]{1,0:T(8,128)(2,1)S(1)}, u32[]{:S(2)}, u32[]{:S(2)}) collective-permute-start(bf16[40,512]{1,0:T(8,128)(2,1)S(1)} %get-tuple-element.83), channel_id=1, source_target_pairs={{0,8},{8,0},{16,24},{24,16},{1,9},{9,1},{17,25},{25,17},{2,10},{10... | collective-permute-start | bytes 122888 | tf_op jit(solution)/shard_map/ppermute | solution.py:19
  45.7 2.6 %collective-permute-start.11 = (bf16[40,512]{1,0:T(8,128)(2,1)S(1)}, bf16[40,512]{1,0:T(8,128)(2,1)S(1)}, u32[]{:S(2)}, u32[]{:S(2)}) collective-permute-start(bf16[40,512]{1,0:T(8,128)(2,1)S(1)} %get-tuple-element.84), channel_id=1, source_target_pairs={{0,16},{8,24},{16,0},{24,8},{1,17},{9,25},{17,1},{25,9},{2,18},{10... | collective-permute-start | bytes 122888 | tf_op jit(solution)/shard_map/ppermute | solution.py:19
  48.5 2.8 %collective-permute-done.11.refs_2_ = bf16[40,512]{1,0:T(8,128)(2,1)S(1)} collective-permute-done((bf16[40,512]{1,0:T(8,128)(2,1)S(1)}, bf16[40,512]{1,0:T(8,128)(2,1)S(1)}, u32[]{:S(2)}, u32[]{:S(2)}) %collective-permute-start.11) | collective-permute-done | bytes 40992 | tf_op jit(solution)/shard_map/ppermute | solution.py:19
  51.3 2.8 %collective-permute-done.12.refs_3_ = bf16[40,512]{1,0:T(8,128)(2,1)S(1)} collective-permute-done((bf16[40,512]{1,0:T(8,128)(2,1)S(1)}, bf16[40,512]{1,0:T(8,128)(2,1)S(1)}, u32[]{:S(2)}, u32[]{:S(2)}) %collective-permute-start.12) | collective-permute-done | bytes 40992 | tf_op jit(solution)/shard_map/ppermute | solution.py:19
  54.1 1.9 %collective-permute-start.15 = (bf16[40,512]{1,0:T(8,128)(2,1)S(1)}, bf16[40,512]{1,0:T(8,128)(2,1)S(1)}, u32[]{:S(2)}, u32[]{:S(2)}) collective-permute-start(bf16[40,512]{1,0:T(8,128)(2,1)S(1)} %shard_map.137.refs_0_), channel_id=1, source_target_pairs={{0,5},{1,4},{4,1},{5,0},{2,7},{3,6},{6,3},{7,2},{8,13},{9,12},{12,... | collective-permute-start | bytes 122888 | tf_op jit(solution)/shard_map/ppermute | solution.py:19
  56.0 0.5 collective-permute-start.14
  56.9 1.3 %collective-permute-start.25 = (bf16[64,512]{1,0:T(8,128)(2,1)S(1)}, bf16[64,512]{1,0:T(8,128)(2,1)S(1)}, u32[]{:S(2)}, u32[]{:S(2)}) collective-permute-start(bf16[64,512]{1,0:T(8,128)(2,1)S(1)} %get-tuple-element.103), channel_id=1, source_target_pairs={{0,16},{8,24},{16,0},{24,8},{1,17},{9,25},{17,1},{25,9},{2,18},{10... | collective-permute-start | bytes 196616 | tf_op jit(solution)/shard_map/ppermute | solution.py:19
  58.1 3.1 %collective-permute-start.26 = (bf16[64,512]{1,0:T(8,128)(2,1)S(1)}, bf16[64,512]{1,0:T(8,128)(2,1)S(1)}, u32[]{:S(2)}, u32[]{:S(2)}) collective-permute-start(bf16[64,512]{1,0:T(8,128)(2,1)S(1)} %get-tuple-element.104), channel_id=1, source_target_pairs={{0,24},{8,16},{16,8},{24,0},{1,25},{9,17},{17,9},{25,1},{2,26},{10... | collective-permute-start | bytes 196616 | tf_op jit(solution)/shard_map/ppermute | solution.py:19
  61.2 0.8 %shard_map.144 = f32[128,1024]{1,0:T(8,128)} custom-call(f32[128,1024]{1,0:T(8,128)S(1)} %get-tuple-element.105.own_ref, f32[128,1024]{1,0:T(8,128)S(1)} %collective-permute-done.27.got_ref), custom_call_target="tpu_custom_call" | custom-call | flops 1073741824 | bytes 1048576 | tf_op jit(solution)/shard_map/pallas_call | solution.py:62
  62.5 1.1 %collective-permute-start.13 = (bf16[40,512]{1,0:T(8,128)(2,1)S(1)}, bf16[40,512]{1,0:T(8,128)(2,1)S(1)}, u32[]{:S(2)}, u32[]{:S(2)}) collective-permute-start(bf16[40,512]{1,0:T(8,128)(2,1)S(1)} %shard_map.137.refs_0_), channel_id=1, source_target_pairs={{0,1},{1,0},{4,5},{5,4},{2,3},{3,2},{6,7},{7,6},{8,9},{9,8},{12,13... | collective-permute-start | bytes 122888 | tf_op jit(solution)/shard_map/ppermute | solution.py:19
  63.7 0.6 collective-permute-done.26.refs_3_
  64.3 3.1 %collective-permute-start.30 = (bf16[64,512]{1,0:T(8,128)(2,1)S(1)}, bf16[64,512]{1,0:T(8,128)(2,1)S(1)}, u32[]{:S(2)}, u32[]{:S(2)}) collective-permute-start(bf16[64,512]{1,0:T(8,128)(2,1)S(1)} %shard_map.145.refs_0_), channel_id=1, source_target_pairs={{0,24},{8,16},{16,8},{24,0},{1,25},{9,17},{17,9},{25,1},{2,26},{10... | collective-permute-start | bytes 196616 | tf_op jit(solution)/shard_map/ppermute | solution.py:19
  67.4 1.4 %collective-permute-start.28 = (bf16[64,512]{1,0:T(8,128)(2,1)S(1)}, bf16[64,512]{1,0:T(8,128)(2,1)S(1)}, u32[]{:S(2)}, u32[]{:S(2)}) collective-permute-start(bf16[64,512]{1,0:T(8,128)(2,1)S(1)} %shard_map.145.refs_0_), channel_id=1, source_target_pairs={{0,8},{8,0},{16,24},{24,16},{1,9},{9,1},{17,25},{25,17},{2,10},{10... | collective-permute-start | bytes 196616 | tf_op jit(solution)/shard_map/ppermute | solution.py:19
  68.8 0.6 shard_map.138
  69.4 3.0 %collective-permute-start.18 = (bf16[32,512]{1,0:T(8,128)(2,1)S(1)}, bf16[32,512]{1,0:T(8,128)(2,1)S(1)}, u32[]{:S(2)}, u32[]{:S(2)}) collective-permute-start(bf16[32,512]{1,0:T(8,128)(2,1)S(1)} %get-tuple-element.86.refs_0_), channel_id=1, source_target_pairs={{0,24},{8,16},{16,8},{24,0},{1,25},{9,17},{17,9},{25,1},{2,26},{10... | collective-permute-start | bytes 98312 | tf_op jit(solution)/shard_map/ppermute | solution.py:19
  72.4 1.4 %collective-permute-start.16 = (bf16[32,512]{1,0:T(8,128)(2,1)S(1)}, bf16[32,512]{1,0:T(8,128)(2,1)S(1)}, u32[]{:S(2)}, u32[]{:S(2)}) collective-permute-start(bf16[32,512]{1,0:T(8,128)(2,1)S(1)} %get-tuple-element.86.refs_0_), channel_id=1, source_target_pairs={{0,8},{8,0},{16,24},{24,16},{1,9},{9,1},{17,25},{25,17},{2,10},{10... | collective-permute-start | bytes 98312 | tf_op jit(solution)/shard_map/ppermute | solution.py:19
  73.8 1.5 %collective-permute-start.32 = (bf16[4,64,512]{2,1,0:T(8,128)(2,1)S(1)}, bf16[4,64,512]{2,1,0:T(8,128)(2,1)S(1)}, u32[]{:S(2)}, u32[]{:S(2)}) collective-permute-start(bf16[4,64,512]{2,1,0:T(8,128)(2,1)S(1)} %shard_map.146.both_ref), channel_id=1, source_target_pairs={{0,4},{4,0},{1,5},{5,1},{2,6},{6,2},{3,7},{7,3},{8,12},{12,8},{9,1... | collective-permute-start | bytes 786440 | tf_op jit(solution)/shard_map/ppermute | solution.py:19
  75.4 1.9 %collective-permute-done.17.refs_2_ = bf16[32,512]{1,0:T(8,128)(2,1)S(1)} collective-permute-done((bf16[32,512]{1,0:T(8,128)(2,1)S(1)}, bf16[32,512]{1,0:T(8,128)(2,1)S(1)}, u32[]{:S(2)}, u32[]{:S(2)}) %collective-permute-start.17) | collective-permute-done | bytes 32800 | tf_op jit(solution)/shard_map/ppermute | solution.py:19
  77.3 2.9 %collective-permute-done.32.across_ref = bf16[4,64,512]{2,1,0:T(8,128)(2,1)S(1)} collective-permute-done((bf16[4,64,512]{2,1,0:T(8,128)(2,1)S(1)}, bf16[4,64,512]{2,1,0:T(8,128)(2,1)S(1)}, u32[]{:S(2)}, u32[]{:S(2)}) %collective-permute-start.32) | collective-permute-done | bytes 262176 | tf_op jit(solution)/shard_map/ppermute | solution.py:19
  80.3 0.8 shard_map.140
  81.1 1.0 %shard_map.147.held_ref = f32[1024,512]{1,0:T(8,128)} custom-call(bf16[4,64,512]{2,1,0:T(8,128)(2,1)S(1)} %shard_map.146.both_ref, bf16[4,64,512]{2,1,0:T(8,128)(2,1)S(1)} %collective-permute-done.31.core_ref), custom_call_target="tpu_custom_call" | custom-call | flops 1073741824 | bytes 1048576 | tf_op jit(solution)/shard_map/pallas_call | solution.py:62
  82.1 0.9 %shard_map.148.held_ref = f32[1024,512]{1,0:T(8,128)} custom-call(f32[1024,512]{1,0:T(8,128)} %shard_map.147.held_ref, bf16[4,64,512]{2,1,0:T(8,128)(2,1)S(1)} %collective-permute-done.32.across_ref), custom_call_target="tpu_custom_call", output_to_operand_aliasing={{}: (0, {})} | custom-call | flops 1073741824 | bytes 1048576 | tf_op jit(solution)/shard_map/pallas_call | solution.py:62
  83.0 0.9 %shard_map.149 = f32[1024,512]{1,0:T(8,128)} custom-call(f32[1024,512]{1,0:T(8,128)} %shard_map.148.held_ref, bf16[4,64,512]{2,1,0:T(8,128)(2,1)S(1)} %collective-permute-done.33.across_ref), custom_call_target="tpu_custom_call", output_to_operand_aliasing={{}: (0, {})} | custom-call | flops 1073741824 | bytes 1048576 | tf_op jit(solution)/shard_map/pallas_call | solution.py:62
  (61 shorter events, 2.0 us)
Async XLA Ops:
  1.6 3.2 %copy-start.7 = (bf16[128,1024]{1,0:T(8,128)(2,1)S(1)}, bf16[128,1024]{1,0:T(8,128)(2,1)}, u32[]{:S(2)}) copy-start(bf16[128,1024]{1,0:T(8,128)(2,1)} %dec_ref.1) | copy-start | bytes 786436
  1.6 3.2 %copy-start = (bf16[128,1024]{1,0:T(8,128)(2,1)S(1)}, bf16[128,1024]{1,0:T(8,128)(2,1)}, u32[]{:S(2)}) copy-start(bf16[128,1024]{1,0:T(8,128)(2,1)} %weight_ref.5) | copy-start | bytes 786436
  1.6 3.2 %copy-start.2 = (bf16[512,128]{1,0:T(8,128)(2,1)S(1)}, bf16[512,128]{1,0:T(8,128)(2,1)}, u32[]{:S(2)}) copy-start(bf16[512,128]{1,0:T(8,128)(2,1)} %target_ref.1) | copy-start | bytes 393220
  1.6 3.2 %copy-start.3 = (bf16[512,128]{1,0:T(8,128)(2,1)S(1)}, bf16[512,128]{1,0:T(8,128)(2,1)}, u32[]{:S(2)}) copy-start(bf16[512,128]{1,0:T(8,128)(2,1)} %input_ref.1) | copy-start | bytes 393220
  1.6 3.2 %copy-start.4 = (bf16[1024]{0:T(1024)(128)(2,1)S(1)}, bf16[1024]{0:T(1024)(128)(2,1)}, u32[]{:S(2)}) copy-start(bf16[1024]{0:T(1024)(128)(2,1)} %bias_ref.3) | copy-start | bytes 6148
  1.6 3.2 %copy-start.6 = (s32[16]{0:T(128)S(1)}, s32[16]{0:T(128)}, u32[]{:S(2)}) copy-start(s32[16]{0:T(128)} %window_ref.1) | copy-start | bytes 196
  1.7 5.6 %copy-start.1 = (bf16[1024,512]{1,0:T(8,128)(2,1)S(1)}, bf16[1024,512]{1,0:T(8,128)(2,1)}, u32[]{:S(2)}) copy-start(bf16[1024,512]{1,0:T(8,128)(2,1)} %half_ref.3) | copy-start | bytes 3145732
  1.7 5.6 %copy-start.5 = (bf16[512]{0:T(512)(128)(2,1)S(1)}, bf16[512]{0:T(512)(128)(2,1)}, u32[]{:S(2)}) copy-start(bf16[512]{0:T(512)(128)(2,1)} %bias_ref.5) | copy-start | bytes 3076
  1.7 8.3 %collective-permute-start = (bf16[128,512]{1,0:T(8,128)(2,1)S(1)}, bf16[128,512]{1,0:T(8,128)(2,1)S(1)}, u32[]{:S(2)}, u32[]{:S(2)}) collective-permute-start(bf16[128,512]{1,0:T(8,128)(2,1)S(1)} %shard_map.130), channel_id=1, source_target_pairs={{0,1},{1,0},{2,3},{3,2},{4,5},{5,4},{6,7},{7,6},{8,9},{9,8},{10,11... | collective-permute-start | bytes 393224 | tf_op jit(solution)/shard_map/ppermute | solution.py:19
  4.7 6.8 %collective-permute-start.3 = (bf16[128,1024]{1,0:T(8,128)(2,1)S(1)}, bf16[128,1024]{1,0:T(8,128)(2,1)S(1)}, u32[]{:S(2)}, u32[]{:S(2)}) collective-permute-start(bf16[128,1024]{1,0:T(8,128)(2,1)S(1)} %copy-done.7), channel_id=1, source_target_pairs={{0,2},{2,0},{1,3},{3,1},{4,6},{6,4},{5,7},{7,5},{8,10},{10,8},{9,1... | collective-permute-start | bytes 786440 | tf_op jit(solution)/shard_map/ppermute | solution.py:19
  6.7 4.9 %collective-permute-start.4 = (bf16[9,128,128]{2,1,0:T(8,128)(2,1)S(1)}, bf16[9,128,128]{2,1,0:T(8,128)(2,1)S(1)}, u32[]{:S(2)}, u32[]{:S(2)}) collective-permute-start(bf16[9,128,128]{2,1,0:T(8,128)(2,1)S(1)} %get-tuple-element.64), channel_id=1, source_target_pairs={{0,2},{2,0},{1,3},{3,1},{4,6},{6,4},{5,7},{7,5},{8,10},{10,8},{9,1... | collective-permute-start | bytes 884744 | tf_op jit(solution)/shard_map/ppermute | solution.py:19
  7.4 8.7 %collective-permute-start.1 = (bf16[272,512]{1,0:T(8,128)(2,1)S(1)}, bf16[272,512]{1,0:T(8,128)(2,1)S(1)}, u32[]{:S(2)}, u32[]{:S(2)}) collective-permute-start(bf16[272,512]{1,0:T(8,128)(2,1)S(1)} %dynamic-slice_select_fusion), channel_id=1, source_target_pairs={{0,1},{1,0},{2,3},{3,2},{4,5},{5,4},{6,7},{7,6},{8,9},{9,8},{10,11... | collective-permute-start | bytes 835592 | tf_op jit(solution)/shard_map/ppermute | solution.py:19
  10.0 5.3 %collective-permute-start.2 = (bf16[128,512]{1,0:T(8,128)(2,1)S(1)}, bf16[128,512]{1,0:T(8,128)(2,1)S(1)}, u32[]{:S(2)}, u32[]{:S(2)}) collective-permute-start(bf16[128,512]{1,0:T(8,128)(2,1)S(1)} %collective-permute-done.near_ref), channel_id=1, source_target_pairs={{0,4},{4,0},{1,5},{5,1},{2,6},{6,2},{3,7},{7,3},{8,12},{12,8},{9,1... | collective-permute-start | bytes 393224 | tf_op jit(solution)/shard_map/ppermute | solution.py:19
  16.0 1.9 %collective-permute-start.7 = (bf16[272,512]{1,0:T(8,128)(2,1)S(1)}, bf16[272,512]{1,0:T(8,128)(2,1)S(1)}, u32[]{:S(2)}, u32[]{:S(2)}) collective-permute-start(bf16[272,512]{1,0:T(8,128)(2,1)S(1)} %collective-permute-done.1.rest_ref), channel_id=1, source_target_pairs={{0,2},{2,0},{1,3},{3,1},{4,6},{6,4},{5,7},{7,5},{8,10},{10,8},{9,1... | collective-permute-start | bytes 835592 | tf_op jit(solution)/shard_map/ppermute | solution.py:19
  16.0 1.7 %collective-permute-start.5 = (bf16[128,512]{1,0:T(8,128)(2,1)S(1)}, bf16[128,512]{1,0:T(8,128)(2,1)S(1)}, u32[]{:S(2)}, u32[]{:S(2)}) collective-permute-start(bf16[128,512]{1,0:T(8,128)(2,1)S(1)} %collective-permute-done.near_ref), channel_id=1, source_target_pairs={{0,2},{2,0},{1,3},{3,1},{4,6},{6,4},{5,7},{7,5},{8,10},{10,8},{9,1... | collective-permute-start | bytes 393224 | tf_op jit(solution)/shard_map/ppermute | solution.py:19
  16.5 1.4 %collective-permute-start.6 = (bf16[128,512]{1,0:T(8,128)(2,1)S(1)}, bf16[128,512]{1,0:T(8,128)(2,1)S(1)}, u32[]{:S(2)}, u32[]{:S(2)}) collective-permute-start(bf16[128,512]{1,0:T(8,128)(2,1)S(1)} %collective-permute-done.2.far_ref), channel_id=1, source_target_pairs={{0,2},{2,0},{1,3},{3,1},{4,6},{6,4},{5,7},{7,5},{8,10},{10,8},{9,1... | collective-permute-start | bytes 393224 | tf_op jit(solution)/shard_map/ppermute | solution.py:19
  21.7 2.2 %collective-permute-start.20 = (bf16[512,512]{1,0:T(8,128)(2,1)S(1)}, bf16[512,512]{1,0:T(8,128)(2,1)S(1)}, u32[]{:S(2)}, u32[]{:S(2)}) collective-permute-start(bf16[512,512]{1,0:T(8,128)(2,1)S(1)} %get-tuple-element.89), channel_id=1, source_target_pairs={{0,2},{2,0},{1,3},{3,1},{4,6},{6,4},{5,7},{7,5},{8,10},{10,8},{9,1... | collective-permute-start | bytes 1572872 | tf_op jit(solution)/shard_map/ppermute | solution.py:19
  23.4 3.5 %collective-permute-start.8 = (bf16[512,512]{1,0:T(8,128)(2,1)S(1)}, bf16[512,512]{1,0:T(8,128)(2,1)S(1)}, u32[]{:S(2)}, u32[]{:S(2)}) collective-permute-start(bf16[512,512]{1,0:T(8,128)(2,1)S(1)} %get-tuple-element.73), channel_id=1, source_target_pairs={{0,2},{2,0},{1,3},{3,1},{4,6},{6,4},{5,7},{7,5},{8,10},{10,8},{9,1... | collective-permute-start | bytes 1572872 | tf_op jit(solution)/shard_map/ppermute | solution.py:19
  24.0 14.0 %collective-permute-start.21 = (bf16[256,512]{1,0:T(8,128)(2,1)S(1)}, bf16[256,512]{1,0:T(8,128)(2,1)S(1)}, u32[]{:S(2)}, u32[]{:S(2)}) collective-permute-start(bf16[256,512]{1,0:T(8,128)(2,1)S(1)} %get-tuple-element.90), channel_id=1, source_target_pairs={{0,1},{1,0},{4,5},{5,4},{2,3},{3,2},{6,7},{7,6},{8,9},{9,8},{12,13... | collective-permute-start | bytes 786440 | tf_op jit(solution)/shard_map/ppermute | solution.py:19
  24.9 13.1 %collective-permute-start.23 = (bf16[256,512]{1,0:T(8,128)(2,1)S(1)}, bf16[256,512]{1,0:T(8,128)(2,1)S(1)}, u32[]{:S(2)}, u32[]{:S(2)}) collective-permute-start(bf16[256,512]{1,0:T(8,128)(2,1)S(1)} %get-tuple-element.92), channel_id=1, source_target_pairs={{0,5},{1,4},{4,1},{5,0},{2,7},{3,6},{6,3},{7,2},{8,13},{9,12},{12,... | collective-permute-start | bytes 786440 | tf_op jit(solution)/shard_map/ppermute | solution.py:19
  28.0 11.2 %collective-permute-start.22 = (bf16[256,512]{1,0:T(8,128)(2,1)S(1)}, bf16[256,512]{1,0:T(8,128)(2,1)S(1)}, u32[]{:S(2)}, u32[]{:S(2)}) collective-permute-start(bf16[256,512]{1,0:T(8,128)(2,1)S(1)} %get-tuple-element.91), channel_id=1, source_target_pairs={{0,4},{1,5},{4,0},{5,1},{2,6},{3,7},{6,2},{7,3},{8,12},{9,13},{12,... | collective-permute-start | bytes 786440 | tf_op jit(solution)/shard_map/ppermute | solution.py:19
  39.2 18.9 %collective-permute-start.27 = (f32[128,1024]{1,0:T(8,128)S(1)}, f32[128,1024]{1,0:T(8,128)S(1)}, u32[]{:S(2)}, u32[]{:S(2)}) collective-permute-start(f32[128,1024]{1,0:T(8,128)S(1)} %get-tuple-element.106), channel_id=1, source_target_pairs={{0,2},{2,0},{1,3},{3,1},{4,6},{6,4},{5,7},{7,5},{8,10},{10,8},{9,1... | collective-permute-start | bytes 1572872 | tf_op jit(solution)/shard_map/ppermute | solution.py:19
  42.4 1.6 %collective-permute-start.9 = (bf16[136,512]{1,0:T(8,128)(2,1)S(1)}, bf16[136,512]{1,0:T(8,128)(2,1)S(1)}, u32[]{:S(2)}, u32[]{:S(2)}) collective-permute-start(bf16[136,512]{1,0:T(8,128)(2,1)S(1)} %get-tuple-element.80), channel_id=1, source_target_pairs={{0,2},{2,0},{1,3},{3,1},{4,6},{6,4},{5,7},{7,5},{8,10},{10,8},{9,1... | collective-permute-start | bytes 417800 | tf_op jit(solution)/shard_map/ppermute | solution.py:19
  44.0 4.5 %collective-permute-start.10 = (bf16[40,512]{1,0:T(8,128)(2,1)S(1)}, bf16[40,512]{1,0:T(8,128)(2,1)S(1)}, u32[]{:S(2)}, u32[]{:S(2)}) collective-permute-start(bf16[40,512]{1,0:T(8,128)(2,1)S(1)} %get-tuple-element.83), channel_id=1, source_target_pairs={{0,8},{8,0},{16,24},{24,16},{1,9},{9,1},{17,25},{25,17},{2,10},{10... | collective-permute-start | bytes 122888 | tf_op jit(solution)/shard_map/ppermute | solution.py:19
  45.7 5.6 %collective-permute-start.11 = (bf16[40,512]{1,0:T(8,128)(2,1)S(1)}, bf16[40,512]{1,0:T(8,128)(2,1)S(1)}, u32[]{:S(2)}, u32[]{:S(2)}) collective-permute-start(bf16[40,512]{1,0:T(8,128)(2,1)S(1)} %get-tuple-element.84), channel_id=1, source_target_pairs={{0,16},{8,24},{16,0},{24,8},{1,17},{9,25},{17,1},{25,9},{2,18},{10... | collective-permute-start | bytes 122888 | tf_op jit(solution)/shard_map/ppermute | solution.py:19
  48.3 5.8 %collective-permute-start.12 = (bf16[40,512]{1,0:T(8,128)(2,1)S(1)}, bf16[40,512]{1,0:T(8,128)(2,1)S(1)}, u32[]{:S(2)}, u32[]{:S(2)}) collective-permute-start(bf16[40,512]{1,0:T(8,128)(2,1)S(1)} %get-tuple-element.85), channel_id=1, source_target_pairs={{0,24},{8,16},{16,8},{24,0},{1,25},{9,17},{17,9},{25,1},{2,26},{10... | collective-permute-start | bytes 122888 | tf_op jit(solution)/shard_map/ppermute | solution.py:19
  54.1 13.3 %collective-permute-start.15 = (bf16[40,512]{1,0:T(8,128)(2,1)S(1)}, bf16[40,512]{1,0:T(8,128)(2,1)S(1)}, u32[]{:S(2)}, u32[]{:S(2)}) collective-permute-start(bf16[40,512]{1,0:T(8,128)(2,1)S(1)} %shard_map.137.refs_0_), channel_id=1, source_target_pairs={{0,5},{1,4},{4,1},{5,0},{2,7},{3,6},{6,3},{7,2},{8,13},{9,12},{12,... | collective-permute-start | bytes 122888 | tf_op jit(solution)/shard_map/ppermute | solution.py:19
  56.0 12.8 %collective-permute-start.14 = (bf16[40,512]{1,0:T(8,128)(2,1)S(1)}, bf16[40,512]{1,0:T(8,128)(2,1)S(1)}, u32[]{:S(2)}, u32[]{:S(2)}) collective-permute-start(bf16[40,512]{1,0:T(8,128)(2,1)S(1)} %shard_map.137.refs_0_), channel_id=1, source_target_pairs={{0,4},{1,5},{4,0},{5,1},{2,6},{3,7},{6,2},{7,3},{8,12},{9,13},{12,... | collective-permute-start | bytes 122888 | tf_op jit(solution)/shard_map/ppermute | solution.py:19
  56.8 5.7 %collective-permute-start.24 = (bf16[64,512]{1,0:T(8,128)(2,1)S(1)}, bf16[64,512]{1,0:T(8,128)(2,1)S(1)}, u32[]{:S(2)}, u32[]{:S(2)}) collective-permute-start(bf16[64,512]{1,0:T(8,128)(2,1)S(1)} %get-tuple-element.102), channel_id=1, source_target_pairs={{0,8},{8,0},{16,24},{24,16},{1,9},{9,1},{17,25},{25,17},{2,10},{10... | collective-permute-start | bytes 196616 | tf_op jit(solution)/shard_map/ppermute | solution.py:19
  56.9 6.8 %collective-permute-start.25 = (bf16[64,512]{1,0:T(8,128)(2,1)S(1)}, bf16[64,512]{1,0:T(8,128)(2,1)S(1)}, u32[]{:S(2)}, u32[]{:S(2)}) collective-permute-start(bf16[64,512]{1,0:T(8,128)(2,1)S(1)} %get-tuple-element.103), channel_id=1, source_target_pairs={{0,16},{8,24},{16,0},{24,8},{1,17},{9,25},{17,1},{25,9},{2,18},{10... | collective-permute-start | bytes 196616 | tf_op jit(solution)/shard_map/ppermute | solution.py:19
  58.1 6.1 %collective-permute-start.26 = (bf16[64,512]{1,0:T(8,128)(2,1)S(1)}, bf16[64,512]{1,0:T(8,128)(2,1)S(1)}, u32[]{:S(2)}, u32[]{:S(2)}) collective-permute-start(bf16[64,512]{1,0:T(8,128)(2,1)S(1)} %get-tuple-element.104), channel_id=1, source_target_pairs={{0,24},{8,16},{16,8},{24,0},{1,25},{9,17},{17,9},{25,1},{2,26},{10... | collective-permute-start | bytes 196616 | tf_op jit(solution)/shard_map/ppermute | solution.py:19
  62.5 6.3 %collective-permute-start.13 = (bf16[40,512]{1,0:T(8,128)(2,1)S(1)}, bf16[40,512]{1,0:T(8,128)(2,1)S(1)}, u32[]{:S(2)}, u32[]{:S(2)}) collective-permute-start(bf16[40,512]{1,0:T(8,128)(2,1)S(1)} %shard_map.137.refs_0_), channel_id=1, source_target_pairs={{0,1},{1,0},{4,5},{5,4},{2,3},{3,2},{6,7},{7,6},{8,9},{9,8},{12,13... | collective-permute-start | bytes 122888 | tf_op jit(solution)/shard_map/ppermute | solution.py:19
  64.3 8.1 %collective-permute-start.30 = (bf16[64,512]{1,0:T(8,128)(2,1)S(1)}, bf16[64,512]{1,0:T(8,128)(2,1)S(1)}, u32[]{:S(2)}, u32[]{:S(2)}) collective-permute-start(bf16[64,512]{1,0:T(8,128)(2,1)S(1)} %shard_map.145.refs_0_), channel_id=1, source_target_pairs={{0,24},{8,16},{16,8},{24,0},{1,25},{9,17},{17,9},{25,1},{2,26},{10... | collective-permute-start | bytes 196616 | tf_op jit(solution)/shard_map/ppermute | solution.py:19
  67.4 6.4 %collective-permute-start.29 = (bf16[64,512]{1,0:T(8,128)(2,1)S(1)}, bf16[64,512]{1,0:T(8,128)(2,1)S(1)}, u32[]{:S(2)}, u32[]{:S(2)}) collective-permute-start(bf16[64,512]{1,0:T(8,128)(2,1)S(1)} %shard_map.145.refs_0_), channel_id=1, source_target_pairs={{0,16},{8,24},{16,0},{24,8},{1,17},{9,25},{17,1},{25,9},{2,18},{10... | collective-permute-start | bytes 196616 | tf_op jit(solution)/shard_map/ppermute | solution.py:19
  67.4 6.4 %collective-permute-start.28 = (bf16[64,512]{1,0:T(8,128)(2,1)S(1)}, bf16[64,512]{1,0:T(8,128)(2,1)S(1)}, u32[]{:S(2)}, u32[]{:S(2)}) collective-permute-start(bf16[64,512]{1,0:T(8,128)(2,1)S(1)} %shard_map.145.refs_0_), channel_id=1, source_target_pairs={{0,8},{8,0},{16,24},{24,16},{1,9},{9,1},{17,25},{25,17},{2,10},{10... | collective-permute-start | bytes 196616 | tf_op jit(solution)/shard_map/ppermute | solution.py:19
  69.4 6.0 %collective-permute-start.18 = (bf16[32,512]{1,0:T(8,128)(2,1)S(1)}, bf16[32,512]{1,0:T(8,128)(2,1)S(1)}, u32[]{:S(2)}, u32[]{:S(2)}) collective-permute-start(bf16[32,512]{1,0:T(8,128)(2,1)S(1)} %get-tuple-element.86.refs_0_), channel_id=1, source_target_pairs={{0,24},{8,16},{16,8},{24,0},{1,25},{9,17},{17,9},{25,1},{2,26},{10... | collective-permute-start | bytes 98312 | tf_op jit(solution)/shard_map/ppermute | solution.py:19
  72.4 4.8 %collective-permute-start.17 = (bf16[32,512]{1,0:T(8,128)(2,1)S(1)}, bf16[32,512]{1,0:T(8,128)(2,1)S(1)}, u32[]{:S(2)}, u32[]{:S(2)}) collective-permute-start(bf16[32,512]{1,0:T(8,128)(2,1)S(1)} %get-tuple-element.86.refs_0_), channel_id=1, source_target_pairs={{0,16},{8,24},{16,0},{24,8},{1,17},{9,25},{17,1},{25,9},{2,18},{10... | collective-permute-start | bytes 98312 | tf_op jit(solution)/shard_map/ppermute | solution.py:19
  72.4 4.8 %collective-permute-start.16 = (bf16[32,512]{1,0:T(8,128)(2,1)S(1)}, bf16[32,512]{1,0:T(8,128)(2,1)S(1)}, u32[]{:S(2)}, u32[]{:S(2)}) collective-permute-start(bf16[32,512]{1,0:T(8,128)(2,1)S(1)} %get-tuple-element.86.refs_0_), channel_id=1, source_target_pairs={{0,8},{8,0},{16,24},{24,16},{1,9},{9,1},{17,25},{25,17},{2,10},{10... | collective-permute-start | bytes 98312 | tf_op jit(solution)/shard_map/ppermute | solution.py:19
  73.8 6.4 %collective-permute-start.32 = (bf16[4,64,512]{2,1,0:T(8,128)(2,1)S(1)}, bf16[4,64,512]{2,1,0:T(8,128)(2,1)S(1)}, u32[]{:S(2)}, u32[]{:S(2)}) collective-permute-start(bf16[4,64,512]{2,1,0:T(8,128)(2,1)S(1)} %shard_map.146.both_ref), channel_id=1, source_target_pairs={{0,4},{4,0},{1,5},{5,1},{2,6},{6,2},{3,7},{7,3},{8,12},{12,8},{9,1... | collective-permute-start | bytes 786440 | tf_op jit(solution)/shard_map/ppermute | solution.py:19
  75.4 5.7 %collective-permute-start.31 = (bf16[4,64,512]{2,1,0:T(8,128)(2,1)S(1)}, bf16[4,64,512]{2,1,0:T(8,128)(2,1)S(1)}, u32[]{:S(2)}, u32[]{:S(2)}) collective-permute-start(bf16[4,64,512]{2,1,0:T(8,128)(2,1)S(1)} %shard_map.146.both_ref), channel_id=1, source_target_pairs={{0,2},{2,0},{1,3},{3,1},{4,6},{6,4},{5,7},{7,5},{8,10},{10,8},{9,1... | collective-permute-start | bytes 786440 | tf_op jit(solution)/shard_map/ppermute | solution.py:19
  77.2 3.0 %collective-permute-start.19 = (bf16[4,32,512]{2,1,0:T(8,128)(2,1)S(1)}, bf16[4,32,512]{2,1,0:T(8,128)(2,1)S(1)}, u32[]{:S(2)}, u32[]{:S(2)}) collective-permute-start(bf16[4,32,512]{2,1,0:T(8,128)(2,1)S(1)} %shard_map.139.own_ref), channel_id=1, source_target_pairs={{0,2},{2,0},{1,3},{3,1},{4,6},{6,4},{5,7},{7,5},{8,10},{10,8},{9,1... | collective-permute-start | bytes 393224 | tf_op jit(solution)/shard_map/ppermute | solution.py:19
  80.2 2.8 %collective-permute-start.33 = (bf16[4,64,512]{2,1,0:T(8,128)(2,1)S(1)}, bf16[4,64,512]{2,1,0:T(8,128)(2,1)S(1)}, u32[]{:S(2)}, u32[]{:S(2)}) collective-permute-start(bf16[4,64,512]{2,1,0:T(8,128)(2,1)S(1)} %collective-permute-done.32.across_ref), channel_id=1, source_target_pairs={{0,2},{2,0},{1,3},{3,1},{4,6},{6,4},{5,7},{7,5},{8,10},{10,8},{9,1... | collective-permute-start | bytes 786440 | tf_op jit(solution)/shard_map/ppermute | solution.py:19
